TPU v7x, 8 devices: a whole 2x2x1 slice. The times are simulated.
8 devices in a mesh: fsdp: 8 (over z, y, x, core).
Axes of the slice: x: 2, y: 2, z: 1, core: 2. Of those that a mesh axis runs over, the one named last changes fastest.
Arguments:
- x_in: bfloat16 [32, 512, 2048], P('fsdp')
- grad_out: bfloat16 [32, 512, 2048], P('fsdp')
- norm_attn: bfloat16 [2048], P('fsdp')
- w_query: bfloat16 [2048, 16, 128], P('fsdp')
- w_key: bfloat16 [2048, 16, 128], P('fsdp')
- w_value: bfloat16 [2048, 16, 128], P('fsdp')
- w_rel: bfloat16 [2048, 16, 128], P('fsdp')
- bias_u: bfloat16 [2048], P('fsdp')
- bias_w: bfloat16 [2048], P('fsdp')
- w_attn_out: bfloat16 [2048, 2048], P('fsdp')
- norm_mlp: bfloat16 [2048], P('fsdp')
- w_up: bfloat16 [2048, 8192], P('fsdp')
- w_down: bfloat16 [8192, 2048], P('fsdp')
Outputs:
- output 1: bfloat16 [32, 512, 2048], P('fsdp')
- output 2: bfloat16 [32, 512, 2048], P('fsdp')
- output 3: float32 [2048], P('fsdp')
- output 4: float32 [2048, 16, 128], P('fsdp')
- output 5: float32 [2048, 16, 128], P('fsdp')
- output 6: float32 [2048, 16, 128], P('fsdp')
- output 7: float32 [2048, 16, 128], P('fsdp')
- output 8: float32 [2048], P('fsdp')
- output 9: float32 [2048], P('fsdp')
- output 10: float32 [2048, 2048], P('fsdp')
- output 11: float32 [2048], P('fsdp')
- output 12: float32 [2048, 8192], P('fsdp')
- output 13: float32 [8192, 2048], P('fsdp')
All inputs are finite; a program needn't handle non-finite values.
Results may differ from a plain program's by a relative error of at most 0.02.
Values are sent between devices in bfloat16 or wider.
A program may use at most 1 GiB of HBM per device.

v0:
```python
import jax
import jax.numpy as jnp
from jax import lax
from jax.sharding import PartitionSpec as P

EPS = 1e-6
MASK_VALUE = -1e30


def sin_table(seq_len, model_width):
    distance = (seq_len - 1 - jnp.arange(seq_len)).astype(jnp.float32)
    inv_freq = 10000.0 ** (-jnp.arange(0, model_width, 2).astype(jnp.float32) / model_width)
    angles = distance[:, None] * inv_freq[None, :]
    return jnp.concatenate([jnp.sin(angles), jnp.cos(angles)], axis=-1).astype(jnp.bfloat16)


def rms_norm(x_f32, gain_vec):
    mean_sq = jnp.mean(x_f32 * x_f32, axis=-1, keepdims=True)
    return (x_f32 * lax.rsqrt(mean_sq + EPS) * gain_vec).astype(jnp.bfloat16)


def rel_shift(scores):
    lead_dims = scores.shape[:-2]
    num_keys = scores.shape[-1]
    padded = jnp.pad(scores, [(0, 0)] * len(lead_dims) + [(0, 0), (1, 0)])
    padded = padded.reshape(lead_dims + (num_keys + 1, num_keys))
    return padded[..., 1:, :].reshape(lead_dims + (num_keys, num_keys))


def gelu_tanh(pre_f32):
    return jax.nn.gelu(pre_f32, approximate=True)


def attention(q_heads, k_heads, v_heads, r_heads, bias_u, bias_w):
    seq_len = q_heads.shape[1]
    head_dim = q_heads.shape[3]
    q_f32 = q_heads.astype(jnp.float32)
    q_u = (q_f32 + bias_u).astype(jnp.bfloat16)
    q_w = (q_f32 + bias_w).astype(jnp.bfloat16)
    content = jnp.einsum('bshd,bthd->bhst', q_u, k_heads, preferred_element_type=jnp.float32)
    position = rel_shift(jnp.einsum('bshd,khd->bhsk', q_w, r_heads, preferred_element_type=jnp.float32))
    logits = (content + position) * (head_dim ** -0.5)
    causal = jnp.arange(seq_len)[:, None] >= jnp.arange(seq_len)[None, :]
    attn_probs = jax.nn.softmax(jnp.where(causal, logits, MASK_VALUE), axis=-1).astype(jnp.bfloat16)
    return jnp.einsum('bhst,bthd->bshd', attn_probs, v_heads, preferred_element_type=jnp.float32).astype(jnp.bfloat16)


def solution(mesh):
    axis_name = mesh.axis_names[0]
    group_size = mesh.shape[axis_name]

    def gather(local_shard):
        return lax.all_gather(local_shard, axis_name, axis=0, tiled=True)

    def scatter_mean(grad_full, batch_scale):
        return lax.psum_scatter(grad_full * batch_scale, axis_name, scatter_dimension=0, tiled=True)

    def local_step(x_in, grad_out, norm_attn, w_query, w_key, w_value, w_rel, bias_u, bias_w, w_attn_out, norm_mlp, w_up, w_down):
        batch_local, seq_len, model_width = x_in.shape
        num_heads, head_dim = w_query.shape[1], w_query.shape[2]
        hidden = num_heads * head_dim
        batch_scale = 1.0 / (batch_local * group_size)
        pos_table = sin_table(seq_len, model_width)
        x_f32 = x_in.astype(jnp.float32)

        gain_attn = gather(norm_attn).astype(jnp.float32)
        h_attn = rms_norm(x_f32, gain_attn)
        query_full = gather(w_query)
        key_full = gather(w_key)
        value_full = gather(w_value)
        rel_full = gather(w_rel)
        u_full = gather(bias_u).astype(jnp.float32).reshape(num_heads, head_dim)
        w_full = gather(bias_w).astype(jnp.float32).reshape(num_heads, head_dim)
        q_heads = jnp.einsum('duo,ojf->dujf', h_attn, query_full, preferred_element_type=jnp.float32).astype(jnp.bfloat16)
        k_heads = jnp.einsum('duo,ojf->dujf', h_attn, key_full, preferred_element_type=jnp.float32).astype(jnp.bfloat16)
        v_heads = jnp.einsum('duo,ojf->dujf', h_attn, value_full, preferred_element_type=jnp.float32).astype(jnp.bfloat16)
        r_heads = jnp.einsum('mo,ojf->mjf', pos_table, rel_full, preferred_element_type=jnp.float32).astype(jnp.bfloat16)
        context, attn_pull = jax.vjp(attention, q_heads, k_heads, v_heads, r_heads, u_full, w_full)
        out_full = gather(w_attn_out).reshape(num_heads, head_dim, model_width)
        x1_f32 = (x_f32 + jnp.einsum('bshd,hdm->bsm', context, out_full, preferred_element_type=jnp.float32)).astype(jnp.bfloat16).astype(jnp.float32)
        gain_mlp = gather(norm_mlp).astype(jnp.float32)
        h_mlp = rms_norm(x1_f32, gain_mlp)
        up_full = gather(w_up)
        pre_act = jnp.einsum('bsm,mf->bsf', h_mlp, up_full, preferred_element_type=jnp.float32).astype(jnp.bfloat16)
        gelu_out, gelu_pull = jax.vjp(gelu_tanh, pre_act.astype(jnp.float32))
        activated = gelu_out.astype(jnp.bfloat16)
        down_full = gather(w_down)
        y_out = (x1_f32 + jnp.einsum('bsf,fm->bsm', activated, down_full, preferred_element_type=jnp.float32)).astype(jnp.bfloat16)

        y_out, norm_attn, w_query, w_key, w_value, w_attn_out, norm_mlp, w_up, w_down = lax.optimization_barrier(
            (y_out, norm_attn, w_query, w_key, w_value, w_attn_out, norm_mlp, w_up, w_down))

        dy_f32 = grad_out.astype(jnp.float32)
        down_full = gather(w_down)
        grad_down = jnp.einsum('bsf,bsm->fm', activated, grad_out, preferred_element_type=jnp.float32)
        d_act = jnp.einsum('bsm,fm->bsf', grad_out, down_full, preferred_element_type=jnp.float32).astype(jnp.bfloat16)
        d_pre = gelu_pull(d_act.astype(jnp.float32))[0].astype(jnp.bfloat16)
        up_full = gather(w_up)
        grad_up = jnp.einsum('bsm,bsf->mf', h_mlp, d_pre, preferred_element_type=jnp.float32)
        d_h_mlp = jnp.einsum('bsf,mf->bsm', d_pre, up_full, preferred_element_type=jnp.float32).astype(jnp.bfloat16)
        gain_mlp = gather(norm_mlp).astype(jnp.float32)
        mlp_norm_pull = jax.vjp(rms_norm, x1_f32, gain_mlp)[1]
        d_x1_norm, grad_norm_mlp = mlp_norm_pull(d_h_mlp)
        d_x1 = (dy_f32 + d_x1_norm).astype(jnp.bfloat16)
        out_full = gather(w_attn_out).reshape(num_heads, head_dim, model_width)
        grad_attn_out = jnp.einsum('bshd,bsm->hdm', context, d_x1, preferred_element_type=jnp.float32).reshape(hidden, model_width)
        d_context = jnp.einsum('bsm,hdm->bshd', d_x1, out_full, preferred_element_type=jnp.float32).astype(jnp.bfloat16)
        d_q, d_k, d_v, d_r, grad_u, grad_w = attn_pull(d_context)
        query_full = gather(w_query)
        key_full = gather(w_key)
        value_full = gather(w_value)
        grad_query = jnp.einsum('duo,dujf->ojf', h_attn, d_q, preferred_element_type=jnp.float32)
        grad_key = jnp.einsum('duo,dujf->ojf', h_attn, d_k, preferred_element_type=jnp.float32)
        grad_value = jnp.einsum('duo,dujf->ojf', h_attn, d_v, preferred_element_type=jnp.float32)
        grad_rel = jnp.einsum('mo,mjf->ojf', pos_table, d_r, preferred_element_type=jnp.float32)
        d_h_attn = (jnp.einsum('dujf,ojf->duo', d_q, query_full, preferred_element_type=jnp.float32)
                    + jnp.einsum('dujf,ojf->duo', d_k, key_full, preferred_element_type=jnp.float32)
                    + jnp.einsum('dujf,ojf->duo', d_v, value_full, preferred_element_type=jnp.float32)).astype(jnp.bfloat16)
        gain_attn = gather(norm_attn).astype(jnp.float32)
        attn_norm_pull = jax.vjp(rms_norm, x_f32, gain_attn)[1]
        d_x_norm, grad_norm_attn = attn_norm_pull(d_h_attn)
        grad_x = (d_x1.astype(jnp.float32) + d_x_norm).astype(jnp.bfloat16)
        grad_list = (grad_norm_attn, grad_query, grad_key, grad_value, grad_rel, grad_u.reshape(hidden), grad_w.reshape(hidden), grad_attn_out, grad_norm_mlp, grad_up, grad_down)
        return (y_out, grad_x) + tuple(scatter_mean(grad_full, batch_scale) for grad_full in grad_list)

    sharded = P(axis_name)
    return jax.shard_map(local_step, mesh=mesh, in_specs=(sharded,) * 13, out_specs=(sharded,) * 13, check_vma=False)
```

profile of v0, /device:TPU:0, one launch (start us, length us, event | category | flops | bytes accessed | tf_op | source)
XLA Modules:
  0.0 2682.5 jit_solution(3991278230408660568)
XLA Ops:
  86.7 26.5 all-gather.22.cloned.1.call-done
  113.2 25.2 fusion.44
  141.8 25.3 convolution_bitcast_fusion
  167.1 67.2 %copy.153 = f32[4,16,512,512]{3,2,1,0:T(8,128)} copy(f32[4,16,512,512]{2,3,0,1:T(8,128)} %convolution_bitcast_fusion) | data formatting | bytes 134217728
  234.3 52.7 %pad.12.clone = f32[4,16,512,513]{3,2,1,0:T(8,128)} pad(f32[4,16,512,512]{3,2,1,0:T(8,128)} %copy.153, f32[]{:T(128)} %constant.17.clone.1), padding=0_0x0_0x0_0x1_0 | pad | bytes 134348800 | tf_op jit(solution)/shard_map/jvp(jit(_pad))/pad | solution.py:25
  287.0 101.8 %reshape.124 = f32[4,16,513,512]{3,2,1,0:T(8,128)} reshape(f32[4,16,512,513]{3,2,1,0:T(8,128)} %pad.12.clone) | data formatting | bytes 134479872 | tf_op jit(solution)/shard_map/jvp()/reshape | solution.py:26
  413.5 24.7 fusion.112
  438.2 60.8 %fusion.182 = (f32[4,16,512]{2,1,0:T(8,128)S(1)}, f32[4,16,512,512]{3,2,1,0:T(8,128)}) fusion(f32[4,16,513,512]{3,2,1,0:T(8,128)} %reshape.124, bf16[4,512,16,128]{3,1,2,0:T(8,128)(2,1)} %fusion.122, pred[512,512]{1,0:T(8,128)(4,1)S(1)} %copy-done.7, bf16[4,512,16,128]{3,1,2,0:T(8,128)(2,1)} %get-tuple-element.81, f32[16,128]{1,0:T(8,128)S(1)} %bitcast.284), kind=kOutput, calls=%fused_computation.174 | convolution fusion | flops 4391436800 | bytes 151396352 | tf_op jit(solution)/shard_map/jvp()/sub | solution.py:44
  499.0 33.2 %divide_convert_fusion = bf16[4,16,512,512]{3,2,1,0:T(8,128)(2,1)} fusion(f32[4,16,512,512]{3,2,1,0:T(8,128)} %get-tuple-element.83, f32[4,16,512]{2,1,0:T(8,128)S(1)} %get-tuple-element.82), kind=kLoop, calls=%fused_computation.34 | loop fusion | flops 33554432 | bytes 100794368 | tf_op jit(solution)/shard_map/jvp()/convert_element_type | solution.py:44
  553.2 26.5 fusion.54
  580.4 81.0 %fusion.32 = bf16[4,512,8192]{2,1,0:T(8,128)(2,1)} fusion(bf16[2048,8192]{1,0:T(8,128)(2,1)} %all-gather.30.cloned.1.call-done, bf16[4,512,2048]{2,1,0:T(8,128)(2,1)} %get-tuple-element.85, f32[2048]{0:T(1024)S(1)} %bitcast.276, f32[4,512]{1,0:T(4,128)S(1)} %fusion.171), kind=kOutput, calls=%fused_computation.60 | convolution fusion | flops 68753031168 | bytes 75513856 | tf_op jit(solution)/shard_map/bsm,mf->bsf/dot_general | solution.py:84
  661.4 92.2 %fusion.55 = bf16[4,512,2048]{2,1,0:T(8,128)(2,1)} fusion(bf16[4,512,2048]{2,1,0:T(8,128)(2,1)} %get-tuple-element.85, bf16[8192,2048]{1,0:T(8,128)(2,1)} %all-gather.32.cloned.1.call-done, bf16[4,512,8192]{2,1,0:T(8,128)(2,1)} %fusion.32), kind=kOutput, calls=%fused_computation.85 | convolution fusion | flops 68899831808 | bytes 83886080 | tf_op jit(solution)/shard_map/bsf,fm->bsm/dot_general | solution.py:88
  769.1 139.7 %all-gather.34.cloned.1.call-done = bf16[8192,2048]{1,0:T(8,128)(2,1)} async-done(((bf16[1024,2048]{1,0:T(8,128)(2,1)}), bf16[8192,2048]{1,0:T(8,128)(2,1)}) %all-gather.34.cloned.1.call-update) | async-done | bytes 33554448 | tf_op jit(solution)/shard_map/all_gather | solution.py:53
  908.9 121.5 %fusion.10 = bf16[4,512,8192]{2,1,0:T(8,128)(2,1)} fusion(bf16[4,512,8192]{2,1,0:T(8,128)(2,1)} %fusion.32, bf16[4,512,2048]{2,1,0:T(8,128)(2,1)} %param.14, bf16[8192,2048]{1,0:T(8,128)(2,1)} %all-gather.34.cloned.1.call-done), kind=kOutput, calls=%fused_computation.17 | convolution fusion | flops 69105352704 | bytes 109051904 | tf_op jit(solution)/shard_map/bsm,fm->bsf/dot_general | solution.py:96
  1030.4 35.4 %all-gather.36.cloned.1.call-done = bf16[2048,8192]{1,0:T(8,128)(2,1)} async-done(((bf16[256,8192]{1,0:T(8,128)(2,1)}), bf16[2048,8192]{1,0:T(8,128)(2,1)}) %all-gather.36.cloned.1.call-update) | async-done | bytes 33554448 | tf_op jit(solution)/shard_map/all_gather | solution.py:53
  1065.8 86.4 %fusion.45 = (f32[2048]{0:T(1024)}, f32[4,512]{1,0:T(4,128)S(1)}, bf16[4,512,2048]{2,1,0:T(8,128)(2,1)}) fusion(bf16[4,512,2048]{2,1,0:T(8,128)(2,1)} %get-tuple-element.85, f32[4,512]{1,0:T(4,128)S(1)} %copy-done.20, f32[2048]{0:T(1024)S(1)} %bitcast.274, bf16[4,512,8192]{2,1,0:T(8,128)(2,1)} %fusion.10, bf16[2048,8192]{1,0:T(8,128)(2,1)} %all-gather.36.cloned.1.call-done), kind=kOutput, calls=%fused_computation.75 | convolution fusion | flops 68757225472 | bytes 83918848 | tf_op jit(solution)/shard_map/bsf,mf->bsm/dot_general | solution.py:100
  1210.6 25.3 bitcast_multiply_fusion.3
  1236.9 39.1 %fusion.7 = (f32[4,16,512]{2,1,0:T(8,128)S(1)}, bf16[4,16,512,512]{3,2,1,0:T(8,128)(2,1)}) fusion(f32[4,16,512,512]{3,2,1,0:T(8,128)} %get-tuple-element.83, f32[4,16,512]{2,1,0:T(8,128)S(1)} %multiply_divide_fusion, bf16[4,512,16,128]{3,1,2,0:T(8,128)(2,1)} %fusion.112, bf16[4,512,16,128]{3,1,2,0:T(8,128)(2,1)} %fusion.127), kind=kOutput, calls=%fused_computation.14 | convolution fusion | flops 4378820608 | bytes 117702656 | tf_op jit(solution)/shard_map/transpose(jvp(bhst,bthd->bshd))/dot_general | solution.py:45
  1276.1 51.1 %fusion.5 = bf16[4,16,512,512]{3,2,1,0:T(8,128)(2,1)} fusion(f32[4,16,512,512]{3,2,1,0:T(8,128)} %get-tuple-element.83, bf16[4,16,512,512]{3,2,1,0:T(8,128)(2,1)} %get-tuple-element.88, f32[4,16,512]{2,1,0:T(8,128)S(1)} %neg.16, f32[4,16,512]{2,1,0:T(8,128)S(1)} %copy-done.6, pred[512,512]{1,0:T(8,128)(4,1)S(1)} %copy-done.8), kind=kLoop, calls=%fused_computation.12 | loop fusion | flops 117440512 | bytes 134742016 | tf_op jit(solution)/shard_map/transpose(jvp())/mul | solution.py:42
  1350.9 83.6 %reshape.127 = bf16[4,16,512,513]{3,2,1,0:T(8,128)(2,1)} reshape(bf16[4,16,513,512]{3,2,1,0:T(8,128)(2,1)} %pad.13) | data formatting | bytes 67239936 | tf_op jit(solution)/shard_map/transpose(jvp())/reshape | solution.py:26
  1434.5 38.1 %broadcast_multiply_fusion = f32[2048,16,128]{2,0,1:T(8,128)} fusion(bf16[4,512,16,128]{3,1,2,0:T(8,128)(2,1)} %copy-done, bf16[512,1024]{1,0:T(8,128)(2,1)S(1)} %copy-done.12, bf16[512,1024]{1,0:T(8,128)(2,1)S(1)} %copy-done.10, bf16[4,16,512,513]{3,2,1,0:T(8,128)(2,1)} %reshape.127), kind=kOutput, calls=%fused_computation.134 | convolution fusion | flops 8598323200 | bytes 60817408 | tf_op jit(solution)/shard_map/mo,mjf->ojf/dot_general | solution.py:115
  1472.7 25.9 bitcast_reduce_fusion
  1543.5 27.2 %bitcast_multiply_fusion.6 = f32[2048,16,128]{2,0,1:T(8,128)} fusion(bf16[4,16,512,128]{3,2,0,1:T(8,128)(2,1)} %get-tuple-element.91, bf16[16,4,512,128]{3,2,1,0:T(8,128)(2,1)} %get-tuple-element.93, bf16[4,512,2048]{2,1,0:T(8,128)(2,1)} %param.13, f32[2048]{0:T(1024)S(1)} %bitcast.282, f32[4,512]{1,0:T(4,128)S(1)} %copy-done.17), kind=kOutput, calls=%fused_computation.90 | convolution fusion | flops 17217617920 | bytes 41959424 | tf_op jit(solution)/shard_map/duo,dujf->ojf/dot_general | solution.py:112
  1570.7 26.1 bitcast_multiply_fusion.4
  1596.9 26.3 bitcast_multiply_fusion.5
  1623.3 94.8 %bitcast_multiply_fusion = f32[8192,2048]{1,0:T(8,128)} fusion(bf16[4,512,2048]{2,1,0:T(8,128)(2,1)} %param.14, bf16[4,512,8192]{2,1,0:T(8,128)(2,1)} %fusion.32), kind=kOutput, calls=%fused_computation.28 | convolution fusion | flops 68904026112 | bytes 109051904 | tf_op jit(solution)/shard_map/bsf,bsm->fm/dot_general | solution.py:95
  1718.9 84.6 %bitcast_multiply_fusion.1 = f32[2048,8192]{1,0:T(8,128)} fusion(bf16[4,512,8192]{2,1,0:T(8,128)(2,1)} %fusion.10, bf16[4,512,2048]{2,1,0:T(8,128)(2,1)} %get-tuple-element.85, f32[2048]{0:T(1024)S(1)} %bitcast.277, f32[4,512]{1,0:T(4,128)S(1)} %copy-done.21), kind=kOutput, calls=%fused_computation.29 | convolution fusion | flops 68753031168 | bytes 109068288 | tf_op jit(solution)/shard_map/bsm,bsf->mf/dot_general | solution.py:99
  1813.9 26.6 fusion.67
  1840.5 24.9 fusion.59
  1865.4 33.1 %fusion.46 = (f32[2048]{0:T(1024)S(1)}, f32[4,512]{1,0:T(4,128)S(1)}, bf16[4,512,2048]{2,1,0:T(8,128)(2,1)}) fusion(bf16[4,512,2048]{2,1,0:T(8,128)(2,1)} %param.13, f32[4,512]{1,0:T(4,128)S(1)} %copy-done.18, f32[2048]{0:T(1024)S(1)} %bitcast.272, f32[4,512,2048,1]{2,1,3,0:T(8,128)} %fusion.67, bf16[2048,16,128]{2,0,1:T(8,128)(2,1)} %all-gather.42.cloned.1.call-done, ...), kind=kOutput, calls=%fused_computation.76 | convolution fusion | flops 17226002432 | bytes 67141632 | tf_op jit(solution)/shard_map/dujf,ojf->duo/dot_general | solution.py:117
  1960.8 335.2 %reduce-scatter.20.cloned.1.call-done = f32[1024,2048]{1,0:T(8,128)} async-done(((f32[8192,2048]{1,0:T(8,128)}), f32[1024,2048]{1,0:T(8,128)}) %reduce-scatter.20.cloned.1.call-update) | async-done | bytes 8388624 | tf_op jit(solution)/shard_map/reduce_scatter | solution.py:56
  2295.9 379.6 %reduce-scatter.18.cloned.1.call-done = f32[256,8192]{1,0:T(8,128)} async-done(((f32[2048,8192]{1,0:T(8,128)}), f32[256,8192]{1,0:T(8,128)}) %reduce-scatter.18.cloned.1.call-update) | async-done | bytes 8388624 | tf_op jit(solution)/shard_map/reduce_scatter | solution.py:56
  (194 shorter events, 345.9 us)
Async XLA Ops:
  7.2 69.8 %all-gather.26.cloned.1.call-start = ((), (), s32[]{:S(2)}) async-start(), calls=%async_computation.10 | async-start | bytes 9437184 | tf_op jit(solution)/shard_map/all_gather | solution.py:53
  9.8 103.5 %all-gather.22.cloned.1.call-start = ((), (), s32[]{:S(2)}) async-start(), calls=%async_computation.8 | async-start | bytes 9437184 | tf_op jit(solution)/shard_map/all_gather | solution.py:53
  12.3 376.5 %all-gather.24.cloned.1.call-start = ((), (), s32[]{:S(2)}) async-start(), calls=%async_computation.9 | async-start | bytes 9437184 | tf_op jit(solution)/shard_map/all_gather | solution.py:53
  14.8 398.7 %all-gather.20.cloned.1.call-start = ((), (), s32[]{:S(2)}) async-start(), calls=%async_computation.7 | async-start | bytes 9437184 | tf_op jit(solution)/shard_map/all_gather | solution.py:53
  17.4 535.8 %all-gather.28.cloned.1.call-start = ((), (), s32[]{:S(2)}) async-start(), calls=%async_computation.11 | async-start | bytes 9437184 | tf_op jit(solution)/shard_map/all_gather | solution.py:53
  18.0 562.4 %all-gather.30.cloned.1.call-start = ((), (), s32[]{:S(2)}) async-start(), calls=%async_computation.12 | async-start | bytes 37748736 | tf_op jit(solution)/shard_map/all_gather | solution.py:53
  18.6 642.8 %all-gather.32.cloned.1.call-start = ((), (), s32[]{:S(2)}) async-start(), calls=%async_computation.13 | async-start | bytes 37748736 | tf_op jit(solution)/shard_map/all_gather | solution.py:53
  19.3 889.6 %all-gather.34.cloned.1.call-start = ((), (), s32[]{:S(2)}) async-start(), calls=%async_computation.14 | async-start | bytes 37748736 | tf_op jit(solution)/shard_map/all_gather | solution.py:53
  42.2 371.3 %copy-start.27 = (f32[8,1,256]{2,1,0:T(1,128)}, f32[8,1,256]{2,1,0:T(1,128)S(1)}, u32[]{:S(2)}) copy-start(f32[8,1,256]{2,1,0:T(1,128)S(1)} %convert_element_type.241) | copy-start | bytes 24580
  68.6 344.9 %copy-start.15 = (f32[4,512]{1,0:T(4,128)}, f32[4,512]{1,0:T(4,128)S(1)}, u32[]{:S(2)}) copy-start(f32[4,512]{1,0:T(4,128)S(1)} %fusion.170) | copy-start | bytes 24580
  580.3 81.0 %copy-start.19 = (f32[4,512]{1,0:T(4,128)}, f32[4,512]{1,0:T(4,128)S(1)}, u32[]{:S(2)}) copy-start(f32[4,512]{1,0:T(4,128)S(1)} %fusion.171) | copy-start | bytes 24580
  661.4 93.7 %copy-start.1 = (bf16[256,16,128]{2,1,0:T(8,128)(2,1)S(1)}, bf16[256,16,128]{2,1,0:T(8,128)(2,1)}, u32[]{:S(2)}) copy-start(bf16[256,16,128]{2,1,0:T(8,128)(2,1)} %param.18) | copy-start | bytes 3145732
  661.4 95.0 %copy-start.2 = (bf16[256,16,128]{2,1,0:T(8,128)(2,1)S(1)}, bf16[256,16,128]{2,1,0:T(8,128)(2,1)}, u32[]{:S(2)}) copy-start(bf16[256,16,128]{2,1,0:T(8,128)(2,1)} %param.16) | copy-start | bytes 3145732
  661.4 96.3 %copy-start.38 = (bf16[256]{0:T(256)(128)(2,1)S(1)}, bf16[256]{0:T(256)(128)(2,1)}, u32[]{:S(2)}) copy-start(bf16[256]{0:T(256)(128)(2,1)} %param.23) | copy-start | bytes 1540
  661.4 106.4 %copy-start.3 = (bf16[256,16,128]{2,1,0:T(8,128)(2,1)S(1)}, bf16[256,16,128]{2,1,0:T(8,128)(2,1)}, u32[]{:S(2)}) copy-start(bf16[256,16,128]{2,1,0:T(8,128)(2,1)} %param.17) | copy-start | bytes 3145732
  753.7 312.2 %all-gather.36.cloned.1.call-start = ((), (), s32[]{:S(2)}) async-start(), calls=%async_computation.15 | async-start | bytes 37748736 | tf_op jit(solution)/shard_map/all_gather | solution.py:53
  754.4 411.4 %all-gather.38.cloned.1.call-start = ((), (), s32[]{:S(2)}) async-start(), calls=%async_computation.16 | async-start | bytes 9437184 | tf_op jit(solution)/shard_map/all_gather | solution.py:53
  755.0 1058.9 %all-gather.44.cloned.1.call-start = ((), (), s32[]{:S(2)}) async-start(), calls=%async_computation.19 | async-start | bytes 9437184 | tf_op jit(solution)/shard_map/all_gather | solution.py:53
  756.3 1084.2 %all-gather.40.cloned.1.call-start = ((), (), s32[]{:S(2)}) async-start(), calls=%async_computation.17 | async-start | bytes 9437184 | tf_op jit(solution)/shard_map/all_gather | solution.py:53
  757.6 1107.8 %all-gather.42.cloned.1.call-start = ((), (), s32[]{:S(2)}) async-start(), calls=%async_computation.18 | async-start | bytes 9437184 | tf_op jit(solution)/shard_map/all_gather | solution.py:53
  769.1 1173.6 %reduce-scatter.12.cloned.1.call-start = ((), (), s32[]{:S(2)}) async-start(), calls=%async_computation.22 | async-start | bytes 18874368 | tf_op jit(solution)/shard_map/reduce_scatter | solution.py:56
  908.9 157.0 %copy-start.20 = (f32[4,512]{1,0:T(4,128)S(1)}, f32[4,512]{1,0:T(4,128)}, u32[]{:S(2)}) copy-start(f32[4,512]{1,0:T(4,128)} %copy-done.19) | copy-start | bytes 24580
  908.9 157.0 %copy-start.22 = (f32[8,1,256]{2,1,0:T(1,128)S(1)}, f32[8,1,256]{2,1,0:T(1,128)}, u32[]{:S(2)}) copy-start(f32[8,1,256]{2,1,0:T(1,128)} %convert_element_type.243) | copy-start | bytes 24580
  1065.8 86.4 %copy-start.24 = (f32[4,512]{1,0:T(4,128)S(1)}, f32[4,512]{1,0:T(4,128)}, u32[]{:S(2)}) copy-start(f32[4,512]{1,0:T(4,128)} %copy-done.23) | copy-start | bytes 24580
  1236.0 711.2 %reduce-scatter.14.cloned.1.call-start = ((), (), s32[]{:S(2)}) async-start(), calls=%async_computation.23 | async-start | bytes 18874368 | tf_op jit(solution)/shard_map/reduce_scatter | solution.py:56
  1350.9 83.6 %copy-start.10 = (bf16[512,1024]{1,0:T(8,128)(2,1)S(1)}, bf16[512,1024]{1,0:T(8,128)(2,1)}, u32[]{:S(2)}) copy-start(bf16[512,1024]{1,0:T(8,128)(2,1)} %copy-done.9) | copy-start | bytes 3145732
  1350.9 83.6 %copy-start.12 = (bf16[512,1024]{1,0:T(8,128)(2,1)S(1)}, bf16[512,1024]{1,0:T(8,128)(2,1)}, u32[]{:S(2)}) copy-start(bf16[512,1024]{1,0:T(8,128)(2,1)} %copy-done.11) | copy-start | bytes 3145732
  1472.7 479.0 %reduce-scatter.8.cloned.1.call-start = ((), (), s32[]{:S(2)}) async-start(), calls=%async_computation.20 | async-start | bytes 18874368 | tf_op jit(solution)/shard_map/reduce_scatter | solution.py:56
  1570.7 385.5 %reduce-scatter.10.cloned.1.call-start = ((), (), s32[]{:S(2)}) async-start(), calls=%async_computation.21 | async-start | bytes 18874368 | tf_op jit(solution)/shard_map/reduce_scatter | solution.py:56
  1596.9 363.9 %reduce-scatter.16.cloned.1.call-start = ((), (), s32[]{:S(2)}) async-start(), calls=%async_computation.24 | async-start | bytes 18874368 | tf_op jit(solution)/shard_map/reduce_scatter | solution.py:56
  1623.3 672.7 %reduce-scatter.20.cloned.1.call-start = ((), (), s32[]{:S(2)}) async-start(), calls=%async_computation.26 | async-start | bytes 75497472 | tf_op jit(solution)/shard_map/reduce_scatter | solution.py:56
  1718.2 957.3 %reduce-scatter.18.cloned.1.call-start = ((), (), s32[]{:S(2)}) async-start(), calls=%async_computation.25 | async-start | bytes 75497472 | tf_op jit(solution)/shard_map/reduce_scatter | solution.py:56
  (29 other events, 553.2 us)
Sparse Core Ops, SparseCore 0:
  10.4 51.5 all-gather.25
  64.5 48.7 all-gather.21
  115.6 48.6 all-gather.23
  166.6 48.6 all-gather.19
  217.0 48.6 all-gather.27
  267.4 155.0 all-gather.29
  424.4 155.0 all-gather.31
  753.8 155.0 all-gather.33
  910.7 155.0 all-gather.35
  1067.5 48.6 all-gather.37
  1118.6 48.6 all-gather.43
  1169.6 48.6 all-gather.39
  1220.8 48.6 all-gather.41
  1272.9 107.7 reduce-scatter.11
  1472.8 108.5 reduce-scatter.13
  1584.7 107.7 reduce-scatter.7
  1695.8 107.7 reduce-scatter.9
  1807.5 108.6 reduce-scatter.15
  1920.3 375.6 reduce-scatter.19
  2299.8 375.6 reduce-scatter.17
where the time goes:
time: 2690 us; the launch traced here: 2680 us
  matrix products  1160 us (43%)
  waiting for transfers between devices  920 us (34%)
  local copies, waits for them, and re-layouts  370 us (14%)
  other arithmetic  132 us (5%)
  blocking collectives  84.2 us (3%)
    reduce_scatter x7, waiting for transfers between devices, scatter_mean(): lax.psum_scatter(grad_full * batch_scale, axis_name, scatter_dimension=0,...  715 us
    all_gather x13, waiting for transfers between devices, gather(): return lax.all_gather(local_shard, axis_name, axis=0, tiled=True)  202 us
    reshape x2, local copies, waits for them, and re-layouts, rel_shift(): padded = padded.reshape(lead_dims + (num_keys + 1, num_keys))  185 us
    dot_general x1, matrix products, local_step(): jnp.einsum('bsm,fm->bsf', grad_out, down_full, preferred_element_type=jnp...  122 us
    unnamed x101, local copies, waits for them, and re-layouts  105 us
    dot_general x1, matrix products, local_step(): jnp.einsum('bsf,bsm->fm', activated, grad_out, preferred_element_type=jnp...  94.8 us
    dot_general x1, matrix products, local_step(): jnp.einsum('bsf,fm->bsm', activated, down_full, preferred_element_type=jn...  92.2 us
    dot_general x1, matrix products, local_step(): jnp.einsum('bsf,mf->bsm', d_pre, up_full, preferred_element_type=jnp.floa...  86.4 us
  transfers between devices with their start and end apart: 20, of which 5 were waited for; matrix products, arithmetic and copies ran while one was open for 58% of the time, Pallas kernels for 0%

commit v1 on v0

v1 whole, which is shorter than its diff:
```python
import functools

import jax
import jax.numpy as jnp
from jax import lax
from jax.experimental import pallas as pl
from jax.experimental.pallas import tpu as pltpu
from jax.sharding import PartitionSpec as P


EPS = 1e-6
MASK_VALUE = -1e30
BLK = 128
F32 = jnp.float32
BF16 = jnp.bfloat16


def sin_table(seq_len, model_width):
    distance = (seq_len - 1 - jnp.arange(seq_len)).astype(F32)
    inv_freq = 10000.0 ** (-jnp.arange(0, model_width, 2).astype(F32) / model_width)
    angles = distance[:, None] * inv_freq[None, :]
    return jnp.concatenate([jnp.sin(angles), jnp.cos(angles)], axis=-1).astype(BF16)


def rms_norm(x_f32, gain_vec):
    mean_sq = jnp.mean(x_f32 * x_f32, axis=-1, keepdims=True)
    return (x_f32 * lax.rsqrt(mean_sq + EPS) * gain_vec).astype(BF16)


def gelu_tanh(pre_f32):
    return jax.nn.gelu(pre_f32, approximate=True)


def dot_nn(a, b):
    return lax.dot_general(a, b, (((1,), (0,)), ((), ())), preferred_element_type=F32)


def dot_nt(a, b):
    return lax.dot_general(a, b, (((1,), (1,)), ((), ())), preferred_element_type=F32)


def dot_tn(a, b):
    return lax.dot_general(a, b, (((0,), (0,)), ((), ())), preferred_element_type=F32)


def after(value, *earlier):
    return lax.optimization_barrier((value, *earlier))[0]


def tril_mask():
    return lax.broadcasted_iota(jnp.int32, (BLK, BLK), 0) >= lax.broadcasted_iota(jnp.int32, (BLK, BLK), 1)


def shear(x):
    return pltpu.roll(x, 1, axis=1, stride=1, stride_axis=0)


def block_probs(q_u, q_w, keys, rel, block, seq_len, head_dim, tril):
    top = (block + 1) * BLK
    content = dot_nt(q_u, keys[:top])
    table = dot_nt(q_w, rel[seq_len - top:])
    turned = [shear(table[:, c * BLK:(c + 1) * BLK]) for c in range(block + 1)]
    scale = head_dim ** -0.5
    parts = []
    for c in range(block + 1):
        part = content[:, c * BLK:(c + 1) * BLK]
        if c < block:
            part = (part + jnp.where(tril, turned[c], turned[c + 1])) * scale
        else:
            part = jnp.where(tril, (part + turned[c]) * scale, MASK_VALUE)
        parts.append(part)
    logits = jnp.concatenate(parts, axis=1) if block else parts[0]
    grown = jnp.exp(logits - jnp.max(logits, axis=1, keepdims=True))
    return grown * (1.0 / jnp.sum(grown, axis=1, keepdims=True))


def attn_fwd_kernel(q_ref, k_ref, v_ref, r_ref, u_ref, w_ref, c_ref, *, heads, head_dim):
    seq_len = q_ref.shape[1]
    tril = tril_mask()
    for n in range(heads):
        cols = slice(n * head_dim, (n + 1) * head_dim)
        q_f32 = q_ref[0, :, cols].astype(F32)
        q_u = (q_f32 + u_ref[0, :, cols]).astype(BF16)
        q_w = (q_f32 + w_ref[0, :, cols]).astype(BF16)
        keys, vals, rel = k_ref[0, :, cols], v_ref[0, :, cols], r_ref[0, :, cols]
        for block in range(seq_len // BLK):
            rows = slice(block * BLK, (block + 1) * BLK)
            probs = block_probs(q_u[rows], q_w[rows], keys, rel, block, seq_len, head_dim, tril)
            c_ref[0, rows, cols] = dot_nn(probs.astype(BF16), vals[:(block + 1) * BLK]).astype(BF16)


def attn_bwd_kernel(q_ref, k_ref, v_ref, r_ref, u_ref, w_ref, dc_ref,
                    dq_ref, dk_ref, dv_ref, dr_ref, du_ref, dw_ref, dk_acc, dv_acc, *, heads, head_dim):
    seq_len = q_ref.shape[1]
    tril = tril_mask()
    flip = (lax.broadcasted_iota(jnp.int32, (BLK, BLK), 0) + lax.broadcasted_iota(jnp.int32, (BLK, BLK), 1)
            == BLK - 1).astype(F32).astype(BF16)
    scale = head_dim ** -0.5

    @pl.when(pl.program_id(1) == 0)
    def _():
        dr_ref[...] = jnp.zeros_like(dr_ref)
        du_ref[...] = jnp.zeros_like(du_ref)
        dw_ref[...] = jnp.zeros_like(dw_ref)

    for n in range(heads):
        cols = slice(n * head_dim, (n + 1) * head_dim)
        q_f32 = q_ref[0, :, cols].astype(F32)
        q_u = (q_f32 + u_ref[0, :, cols]).astype(BF16)
        q_w = (q_f32 + w_ref[0, :, cols]).astype(BF16)
        keys, vals, rel = k_ref[0, :, cols], v_ref[0, :, cols], r_ref[0, :, cols]
        d_ctx = dc_ref[0, :, cols]
        rel_back = jnp.concatenate(
            [dot_nn(flip, rel[c * BLK:(c + 1) * BLK]).astype(BF16) for c in range(seq_len // BLK)], axis=0)
        dk_acc[...] = jnp.zeros_like(dk_acc)
        dv_acc[...] = jnp.zeros_like(dv_acc)
        for block in range(seq_len // BLK):
            top = (block + 1) * BLK
            rows = slice(block * BLK, top)
            probs = block_probs(q_u[rows], q_w[rows], keys, rel, block, seq_len, head_dim, tril)
            d_probs = dot_nt(d_ctx[rows], vals[:top]).astype(BF16).astype(F32)
            inner = jnp.sum(probs * d_probs, axis=1, keepdims=True)
            d_logits = (probs * (d_probs - inner) * scale).astype(BF16)
            dv_acc[:top] += dot_tn(probs.astype(BF16), d_ctx[rows])
            dk_acc[:top] += dot_tn(d_logits, q_u[rows])
            d_qu = dot_nn(d_logits, keys[:top]).astype(BF16).astype(F32)
            parts = []
            for c in range(block + 1):
                turned = shear(dot_nn(d_logits[:, c * BLK:(c + 1) * BLK], flip))
                parts.append(jnp.where(tril, turned, before if c else 0.0).astype(BF16))
                before = turned
            d_table = jnp.concatenate(parts, axis=1) if block else parts[0]
            d_qw = dot_nn(d_table, rel_back[seq_len - top:]).astype(BF16).astype(F32)
            dr_ref[0, seq_len - top:, cols] += dot_tn(d_table, q_w[rows])
            dq_ref[0, rows, cols] = (d_qu + d_qw).astype(BF16)
            du_ref[0, :, cols] += jnp.sum(d_qu.reshape(BLK // 8, 8, head_dim), axis=0)
            dw_ref[0, :, cols] += jnp.sum(d_qw.reshape(BLK // 8, 8, head_dim), axis=0)
        dk_ref[0, :, cols] = dk_acc[...].astype(BF16)
        dv_ref[0, :, cols] = dv_acc[...].astype(BF16)


def attn_specs(seq_len, width, groups):
    span = width // groups
    act = pl.BlockSpec((1, seq_len, span), lambda g, b: (b, 0, g))
    rel = pl.BlockSpec((1, seq_len, span), lambda g, b: (g, 0, 0))
    vec = pl.BlockSpec((1, 1, span), lambda g, b: (g, 0, 0))
    return span, act, rel, vec


def attn_fwd(q, k, v, rel, bias_u, bias_w, head_dim):
    batch, seq_len, width = q.shape
    groups = rel.shape[0]
    span, act, rspec, vec = attn_specs(seq_len, width, groups)
    work = batch * (width // head_dim) * seq_len * seq_len * head_dim
    return pl.pallas_call(
        functools.partial(attn_fwd_kernel, heads=span // head_dim, head_dim=head_dim),
        grid=(groups, batch),
        in_specs=[act, act, act, rspec, vec, vec],
        out_specs=act,
        out_shape=jax.ShapeDtypeStruct(q.shape, BF16),
        compiler_params=pltpu.CompilerParams(dimension_semantics=("arbitrary", "arbitrary")),
        cost_estimate=pl.CostEstimate(flops=8 * work, bytes_accessed=8 * batch * seq_len * width, transcendentals=0),
        name="attn_fwd",
    )(q, k, v, rel, bias_u, bias_w)


def attn_bwd(q, k, v, rel, bias_u, bias_w, d_ctx, head_dim):
    batch, seq_len, width = q.shape
    groups = rel.shape[0]
    span, act, rspec, vec = attn_specs(seq_len, width, groups)
    vec8 = pl.BlockSpec((1, 8, span), lambda g, b: (g, 0, 0))
    work = batch * (width // head_dim) * seq_len * seq_len * head_dim
    flat = jax.ShapeDtypeStruct(q.shape, BF16)
    small = jax.ShapeDtypeStruct((groups, 8, span), F32)
    return pl.pallas_call(
        functools.partial(attn_bwd_kernel, heads=span // head_dim, head_dim=head_dim),
        grid=(groups, batch),
        in_specs=[act, act, act, rspec, vec, vec, act],
        out_specs=[act, act, act, rspec, vec8, vec8],
        out_shape=[flat, flat, flat, jax.ShapeDtypeStruct(rel.shape, F32), small, small],
        scratch_shapes=[pltpu.VMEM((seq_len, head_dim), F32), pltpu.VMEM((seq_len, head_dim), F32)],
        compiler_params=pltpu.CompilerParams(dimension_semantics=("arbitrary", "arbitrary")),
        cost_estimate=pl.CostEstimate(flops=20 * work, bytes_accessed=14 * batch * seq_len * width, transcendentals=0),
        name="attn_bwd",
    )(q, k, v, rel, bias_u, bias_w, d_ctx)


def solution(mesh):
    axis_name = mesh.axis_names[0]
    group_size = mesh.shape[axis_name]
    chips = group_size // 2
    pairs = [(d, d ^ 1) for d in range(group_size)]
    same_core = [[2 * c + core for c in range(chips)] for core in range(2)]

    def gather(local_shard):
        return lax.all_gather(local_shard, axis_name, axis=0, tiled=True)

    def local_step(x_in, grad_out, norm_attn, w_query, w_key, w_value, w_rel, bias_u, bias_w, w_attn_out, norm_mlp, w_up, w_down):
        batch_local, seq_len, width = x_in.shape
        num_heads, head_dim = w_query.shape[1], w_query.shape[2]
        hidden = num_heads * head_dim
        tokens = batch_local * seq_len
        span = hidden // group_size
        scale = 1.0 / (batch_local * group_size)
        me = lax.axis_index(axis_name)
        core = lax.rem(me, 2)

        def shares(acts, kind, half, halves):
            rows = acts.shape[1] // group_size
            part = rows // halves
            return jnp.concatenate(
                [lax.dynamic_slice(acts, (0, (2 * c + kind) * rows + half * part), (tokens, part)) for c in range(chips)],
                axis=1)

        def theirs(acts, cots, half=0, halves=1):
            mine = dot_tn(shares(acts, 1 - core, half, halves), cots)
            return mine, lax.ppermute(mine, axis_name, pairs)

        def ours(acts, cots, received, half=0, halves=1):
            return (dot_tn(shares(acts, core, half, halves), cots) + received) * scale

        def spread(summed):
            return lax.psum_scatter(summed, axis_name, scatter_dimension=0, axis_index_groups=same_core, tiled=True)

        x_f32 = x_in.reshape(tokens, width).astype(F32)
        dy = grad_out.reshape(tokens, width)
        vecs = lax.all_gather(jnp.stack([norm_attn, bias_u, bias_w, norm_mlp]), axis_name, axis=0)
        gain_attn = vecs[:, 0].reshape(width).astype(F32)
        u_full = vecs[:, 1:2].astype(F32)
        w_full = vecs[:, 2:3].astype(F32)
        gain_mlp = vecs[:, 3].reshape(width).astype(F32)

        query_full = gather(w_query.reshape(-1, hidden))
        key_full = gather(w_key.reshape(-1, hidden))
        value_full = gather(w_value.reshape(-1, hidden))
        out_full = gather(w_attn_out)
        up_full = gather(w_up)
        down_full = gather(w_down)

        pos_table = sin_table(seq_len, width)
        rel_cols = lax.all_to_all(w_rel.reshape(-1, hidden), axis_name, split_axis=1, concat_axis=0, tiled=True)
        rel_heads = lax.all_gather(dot_nn(pos_table, rel_cols).astype(BF16), axis_name, axis=0)

        h_attn = rms_norm(x_f32, gain_attn)
        shape3 = (batch_local, seq_len, hidden)
        q = dot_nn(h_attn, query_full).astype(BF16)
        k = dot_nn(h_attn, key_full).astype(BF16)
        v = dot_nn(h_attn, value_full).astype(BF16)
        q3, k3, v3 = q.reshape(shape3), k.reshape(shape3), v.reshape(shape3)
        context = attn_fwd(q3, k3, v3, rel_heads, u_full, w_full, head_dim).reshape(tokens, hidden)
        x1_f32 = (x_f32 + dot_nn(context, out_full)).astype(BF16).astype(F32)
        h_mlp = rms_norm(x1_f32, gain_mlp)
        pre_act = dot_nn(h_mlp, up_full).astype(BF16)
        gelu_out, gelu_pull = jax.vjp(gelu_tanh, pre_act.astype(F32))
        activated = gelu_out.astype(BF16)

        sent0, got0 = theirs(activated, dy, 0, 2)
        sent1, got1 = theirs(activated, dy, 1, 2)
        dy_own = after(dy, sent1)
        down0 = ours(activated, dy_own, got0, 0, 2)
        down1 = ours(activated, after(dy_own, down0), got1, 1, 2)
        grad_down = jnp.concatenate([spread(down0), spread(down1)], axis=0)

        d_act = dot_nt(after(dy, down1), down_full).astype(BF16)
        d_pre = gelu_pull(d_act.astype(F32))[0].astype(BF16)
        sent0, got0 = theirs(h_mlp, d_pre, 0, 2)
        sent1, got1 = theirs(h_mlp, d_pre, 1, 2)
        d_pre_own = after(d_pre, sent1)
        up0 = ours(h_mlp, d_pre_own, got0, 0, 2)
        up1 = ours(h_mlp, after(d_pre_own, up0), got1, 1, 2)
        grad_up = jnp.concatenate([spread(up0), spread(up1)], axis=0)

        d_h_mlp = dot_nt(after(d_pre, up1), up_full).astype(BF16)
        d_x1_norm, grad_norm_mlp = jax.vjp(rms_norm, x1_f32, gain_mlp)[1](d_h_mlp)
        d_x1 = (dy.astype(F32) + d_x1_norm).astype(BF16)
        d_context = dot_nt(d_x1, out_full).astype(BF16)
        d_q, d_k, d_v, d_rel, d_u, d_w = attn_bwd(
            q3, k3, v3, rel_heads, u_full, w_full, d_context.reshape(shape3), head_dim)
        d_q, d_k, d_v = (z.reshape(tokens, hidden) for z in (d_q, d_k, d_v))
        d_rel_own = lax.psum_scatter(d_rel, axis_name, scatter_dimension=0, tiled=True)[0]

        sent_q, got_q = theirs(h_attn, d_q)
        sent_k, got_k = theirs(h_attn, after(d_k, sent_q))
        sum_q = ours(h_attn, after(d_q, sent_k), got_q)
        sent_v, got_v = theirs(h_attn, after(d_v, sum_q))
        sum_k = ours(h_attn, after(d_k, sent_v), got_k)
        sent_o, got_o = theirs(context, after(d_x1, sum_k))
        sum_v = ours(h_attn, after(d_v, sent_o), got_v)
        grad_query, grad_key, grad_value = spread(sum_q), spread(sum_k), spread(sum_v)

        y_out = (x1_f32 + dot_nn(after(activated, sum_v), down_full)).astype(BF16)

        d_rel_own = after(d_rel_own, y_out)
        d_rel_own = jnp.flip(d_rel_own.reshape(seq_len // BLK, BLK, span), axis=1).reshape(seq_len, span).astype(BF16)
        d_rel_all = lax.all_gather(d_rel_own, axis_name, axis=0)
        table_own = lax.dynamic_slice(pos_table, (0, me * (width // group_size)), (seq_len, width // group_size))
        grad_rel = dot_tn(table_own, jnp.swapaxes(d_rel_all, 0, 1).reshape(seq_len, hidden)) * scale

        sum_o = ours(context, after(d_x1, d_rel_own), got_o)
        grad_attn_out = spread(sum_o)

        d_q_h, d_k_h, d_v_h = (after(z, sum_o) for z in (d_q, d_k, d_v))
        d_h_attn = (dot_nt(d_q_h, query_full) + dot_nt(d_k_h, key_full) + dot_nt(d_v_h, value_full)).astype(BF16)
        d_x_norm, grad_norm_attn = jax.vjp(rms_norm, x_f32, gain_attn)[1](d_h_attn)
        grad_x = (d_x1.astype(F32) + d_x_norm).astype(BF16)

        small = jnp.stack([grad_norm_attn.reshape(group_size, span), jnp.sum(d_u, axis=1), jnp.sum(d_w, axis=1),
                           grad_norm_mlp.reshape(group_size, span)], axis=1)
        small = lax.psum_scatter(small * scale, axis_name, scatter_dimension=0, tiled=True)[0]

        heads3 = (-1, num_heads, head_dim)
        return (y_out.reshape(x_in.shape), grad_x.reshape(x_in.shape), small[0], grad_query.reshape(heads3),
                grad_key.reshape(heads3), grad_value.reshape(heads3), grad_rel.reshape(heads3), small[1], small[2],
                grad_attn_out, small[3], grad_up, grad_down)

    sharded = P(axis_name)
    return jax.shard_map(local_step, mesh=mesh, in_specs=(sharded,) * 13, out_specs=(sharded,) * 13, check_vma=False)
```

time: 2690 us -> 2260 us (0.84)
  Pallas kernels: 0 us -> 356 us
  local copies, waits for them, and re-layouts: 370 us -> 76.2 us
  matrix products: 1160 us -> 932 us
  waiting for transfers between devices: 920 us -> 759 us
  other arithmetic: 132 us -> 71.8 us
  blocking collectives: 84.2 us -> 35.1 us
    pallas_call x0 -> x2, Pallas kernels: none -> 356 us  [the longest x1 238 us: attn_bwd(): pl.pallas_call(functools.partial(attn_bwd_kernel, heads=span // head_dim,...]
    reshape x2 -> x0, local copies, waits for them, and re-layouts: 185 us -> none  [rel_shift(): padded = padded.reshape(lead_dims + (num_keys + 1, num_keys))]
    dot_general x27 -> x30, matrix products: 1100 us -> 932 us  [the longest x17 346 us: dot_tn(): lax.dot_general(a, b, (((0,), (0,)), ((), ())), preferred_element_type=F32)]
    reduce_scatter x7 -> x9, waiting for transfers between devices: 715 us -> 616 us  [the longest x8 616 us: spread(): lax.psum_scatter(summed, axis_name, scatter_dimension=0, axis_index_group...]
    all_gather x13 -> x6, waiting for transfers between devices: 202 us -> 105 us  [gather(): return lax.all_gather(local_shard, axis_name, axis=0, tiled=True)]
    unnamed x101 -> x113, local copies, waits for them, and re-layouts: 105 us -> 23.4 us
    pad x2 -> x0, local copies, waits for them, and re-layouts: 76.5 us -> none  [the longest x1 52.7 us: rel_shift(): padded = jnp.pad(scores, [(0, 0)] * len(lead_dims) + [(0, 0), (1, 0)])]
    sub x1 -> x0, matrix products: 60.8 us -> none  [attention(): jax.nn.softmax(jnp.where(causal, logits, MASK_VALUE), axis=-1)]
  transfers between devices with their start and end apart: 20 -> 26, of which waited for: 5 -> 14; matrix products, arithmetic and copies ran while one was open for 58% -> 35% of each run, Pallas kernels for 0% -> 5%
where the time goes in v1:
time: 2260 us; the launch traced here: 2250 us
  matrix products  932 us (41%)
  waiting for transfers between devices  759 us (34%)
  Pallas kernels  356 us (16%)
  local copies, waits for them, and re-layouts  76.2 us (3%)
  other arithmetic  71.8 us (3%)
  blocking collectives  35.1 us (2%)
    reduce_scatter x8, waiting for transfers between devices, spread(): lax.psum_scatter(summed, axis_name, scatter_dimension=0, axis_index_group...  616 us
    dot_general x17, matrix products, dot_tn(): lax.dot_general(a, b, (((0,), (0,)), ((), ())), preferred_element_type=F32)  346 us
    dot_general x6, matrix products, dot_nt(): lax.dot_general(a, b, (((1,), (1,)), ((), ())), preferred_element_type=F32)  311 us
    dot_general x7, matrix products, dot_nn(): lax.dot_general(a, b, (((1,), (0,)), ((), ())), preferred_element_type=F32)  275 us
    pallas_call x1, Pallas kernels, attn_bwd(): pl.pallas_call(functools.partial(attn_bwd_kernel, heads=span // head_dim,...  238 us
    pallas_call x1, Pallas kernels, attn_fwd(): pl.pallas_call(functools.partial(attn_fwd_kernel, heads=span // head_dim,...  118 us
    all_gather x6, waiting for transfers between devices, gather(): return lax.all_gather(local_shard, axis_name, axis=0, tiled=True)  105 us
  transfers between devices with their start and end apart: 26, of which 14 were waited for; matrix products, arithmetic and copies ran while one was open for 35% of the time, Pallas kernels for 5%

profile of v1, /device:TPU:0, one launch (start us, length us, event | category | flops | bytes accessed | tf_op | source)
XLA Modules:
  0.0 2253.0 jit_solution(4039707901104404258)
XLA Ops:
  77.1 24.6 %convolution_convert_fusion.3 = bf16[2048,2048]{1,0:T(8,128)(2,1)} fusion(bf16[2048,2048]{1,0:T(8,128)(2,1)} %fusion.27, bf16[2048,2048]{1,0:T(8,128)(2,1)} %all-gather.16.cloned.1.call-done), kind=kOutput, calls=%fused_computation.95 | convolution fusion | flops 17184063488 | bytes 25165824 | tf_op jit(solution)/shard_map/dot_general | solution.py:35
  101.7 22.7 %all-gather.14.cloned.1.call-done = bf16[2048,2048]{1,0:T(8,128)(2,1)} async-done(((bf16[256,2048]{1,0:T(8,128)(2,1)}), bf16[2048,2048]{1,0:T(8,128)(2,1)}) %all-gather.14.cloned.1.call-update) | async-done | bytes 8388624 | tf_op jit(solution)/shard_map/all_gather | solution.py:196
  124.4 23.5 %convolution_convert_fusion.4 = bf16[2048,2048]{1,0:T(8,128)(2,1)} fusion(bf16[2048,2048]{1,0:T(8,128)(2,1)} %fusion.27, bf16[2048,2048]{1,0:T(8,128)(2,1)} %all-gather.14.cloned.1.call-done), kind=kOutput, calls=%fused_computation.96 | convolution fusion | flops 17184063488 | bytes 25165824 | tf_op jit(solution)/shard_map/dot_general | solution.py:35
  147.9 27.6 %all-gather.12.cloned.1.call-done = bf16[2048,2048]{1,0:T(8,128)(2,1)} async-done(((bf16[256,2048]{1,0:T(8,128)(2,1)}), bf16[2048,2048]{1,0:T(8,128)(2,1)}) %all-gather.12.cloned.1.call-update) | async-done | bytes 8388624 | tf_op jit(solution)/shard_map/all_gather | solution.py:196
  175.5 23.5 %convolution_convert_fusion.5 = bf16[2048,2048]{1,0:T(8,128)(2,1)} fusion(bf16[2048,2048]{1,0:T(8,128)(2,1)} %fusion.27, bf16[2048,2048]{1,0:T(8,128)(2,1)} %all-gather.12.cloned.1.call-done), kind=kOutput, calls=%fused_computation.97 | convolution fusion | flops 17184063488 | bytes 25165824 | tf_op jit(solution)/shard_map/dot_general | solution.py:35
  200.0 118.3 %attn_fwd.1 = bf16[4,512,2048]{2,1,0:T(8,128)(2,1)} custom-call(bf16[4,512,2048]{2,1,0:T(8,128)(2,1)} %bitcast.159, bf16[4,512,2048]{2,1,0:T(8,128)(2,1)} %bitcast.157, bf16[4,512,2048]{2,1,0:T(8,128)(2,1)} %bitcast.155, bf16[8,512,256]{2,1,0:T(8,128)(2,1)} %bitcast.153, f32[8,1,256]{2,1,0:T(1,128)} %get-tuple-element.117.u_ref, ...), custom_call_target="tpu_custom_call" | custom-call | flops 17179869184 | bytes 33554432 | tf_op jit(solution)/shard_map/attn_fwd/pallas_call | solution.py:155
  318.3 24.6 %fusion.23 = (f32[2048]{0:T(1024)S(1)}, bf16[2048,2048]{1,0:T(8,128)(2,1)}) fusion(bf16[2048,2048]{1,0:T(8,128)(2,1)} %bitcast.113, bf16[2048,2048]{1,0:T(8,128)(2,1)} %all-gather.18.cloned.1.call-done, bf16[4,512,2048]{2,1,0:T(8,128)(2,1)} %param.13), kind=kOutput, calls=%fused_computation.41 | convolution fusion | flops 17205032960 | bytes 33562624 | tf_op jit(solution)/shard_map/dot_general | solution.py:35
  352.8 54.6 %all-gather.20.cloned.1.call-done = bf16[2048,8192]{1,0:T(8,128)(2,1)} async-done(((bf16[256,8192]{1,0:T(8,128)(2,1)}), bf16[2048,8192]{1,0:T(8,128)(2,1)}) %all-gather.20.cloned.1.call-update) | async-done | bytes 33554448 | tf_op jit(solution)/shard_map/all_gather | solution.py:196
  407.4 94.2 %fusion.8 = (bf16[2048,8192]{1,0:T(8,128)(2,1)}, bf16[2048,8192]{1,0:T(8,128)(2,1)}) fusion(bf16[2048,2048]{1,0:T(8,128)(2,1)} %fusion.15, bf16[2048,8192]{1,0:T(8,128)(2,1)} %all-gather.20.cloned.1.call-done), kind=kOutput, calls=%fused_computation.14 | convolution fusion | flops 68904026112 | bytes 109051904 | tf_op jit(solution)/shard_map/dot_general | solution.py:35
  501.6 23.2 %constant_dynamic-slice_fusion.43 = (bf16[2048,512]{1,0:T(8,128)(2,1)S(1)}, bf16[2048,512]{1,0:T(8,128)(2,1)}, bf16[2048,512]{1,0:T(8,128)(2,1)}, bf16[2048,512]...) fusion(bf16[2048,8192]{1,0:T(8,128)(2,1)} %get-tuple-element.51, ...), kind=kLoop, calls=%fused_computation.206 | loop fusion | bytes 67108928 | tf_op jit(solution)/shard_map/dynamic_slice | solution.py:212
  524.8 28.6 %fusion.52 = f32[2048,2048]{1,0:T(8,128)} fusion(bf16[2048,2048]{1,0:T(8,128)(2,1)} %bitcast.116, bf16[2048,512]{1,0:T(8,128)(2,1)} %get-tuple-element.64, bf16[2048,512]{1,0:T(8,128)(2,1)} %get-tuple-element.65, bf16[2048,512]{1,0:T(8,128)(2,1)} %get-tuple-element.66, bf16[2048,512]{1,0:T(8,128)(2,1)} %get-tuple-element.67), kind=kOutput, calls=%fused_computation.79 | convolution fusion | flops 17213423616 | bytes 33554432 | tf_op jit(solution)/shard_map/dot_general | solution.py:43
  554.0 28.6 %fusion.37 = f32[2048,2048]{1,0:T(8,128)} fusion(bf16[2048,2048]{1,0:T(8,128)(2,1)} %bitcast.117, bf16[2048,512]{1,0:T(8,128)(2,1)} %get-tuple-element.72, bf16[2048,512]{1,0:T(8,128)(2,1)} %get-tuple-element.73, bf16[2048,512]{1,0:T(8,128)(2,1)} %get-tuple-element.74, bf16[2048,512]{1,0:T(8,128)(2,1)} %get-tuple-element.75), kind=kOutput, calls=%fused_computation.64 | convolution fusion | flops 17213423616 | bytes 33554432 | tf_op jit(solution)/shard_map/dot_general | solution.py:43
  590.1 27.3 %add_multiply_fusion.3 = f32[2048,2048]{1,0:T(8,128)} fusion(f32[2048,2048]{1,0:T(8,128)} %collective-permute-done, bf16[2048,2048]{1,0:T(8,128)(2,1)} %bitcast.118, bf16[2048,512]{1,0:T(8,128)(2,1)S(1)} %copy-done.4, bf16[2048,512]{1,0:T(8,128)(2,1)S(1)} %copy-done.5, bf16[2048,512]{1,0:T(8,128)(2,1)S(1)} %copy-done.6, bf16[2048,512]{1,0:T(8,128)(2,1)} %get-tuple-element.71), kind=kOutput, calls=%fused_computation.56 | convolution fusion | flops 17221812224 | bytes 50331648 | tf_op jit(solution)/shard_map/dot_general | solution.py:43
  617.4 28.0 %add_multiply_fusion.2 = f32[2048,2048]{1,0:T(8,128)} fusion(f32[2048,2048]{1,0:T(8,128)} %collective-permute-done.1, bf16[2048,2048]{1,0:T(8,128)(2,1)} %bitcast.119, bf16[2048,512]{1,0:T(8,128)(2,1)} %get-tuple-element.76, bf16[2048,512]{1,0:T(8,128)(2,1)} %get-tuple-element.77, bf16[2048,512]{1,0:T(8,128)(2,1)} %get-tuple-element.78, ...), kind=kOutput, calls=%fused_computation.55 | convolution fusion | flops 17221812224 | bytes 50331648 | tf_op jit(solution)/shard_map/dot_general | solution.py:43
  645.5 121.3 %fusion.3 = bf16[2048,8192]{1,0:T(8,128)(2,1)} fusion(bf16[2048,8192]{1,0:T(8,128)(2,1)} %get-tuple-element.124, bf16[2048,2048]{1,0:T(8,128)(2,1)} %bitcast.120, bf16[8192,2048]{1,0:T(8,128)(2,1)} %all-gather.22.cloned.1.call-done), kind=kOutput, calls=%fused_computation.9 | convolution fusion | flops 69105352704 | bytes 109051904 | tf_op jit(solution)/shard_map/dot_general | solution.py:39
  766.9 27.3 %fusion.103 = f32[512,8192]{1,0:T(8,128)} fusion(bf16[2048,8192]{1,0:T(8,128)(2,1)} %fusion.3, bf16[2048,128]{1,0:T(8,128)(2,1)S(1)} %copy-done.28, bf16[2048,128]{1,0:T(8,128)(2,1)S(1)} %copy-done.29, bf16[2048,128]{1,0:T(8,128)(2,1)} %get-tuple-element.98, bf16[2048,128]{1,0:T(8,128)(2,1)} %get-tuple-element.99), kind=kOutput, calls=%fused_computation.147 | convolution fusion | flops 17188257792 | bytes 52428800 | tf_op jit(solution)/shard_map/dot_general | solution.py:43
  794.8 27.4 %fusion.88 = f32[512,8192]{1,0:T(8,128)} fusion(bf16[2048,8192]{1,0:T(8,128)(2,1)} %fusion.3, bf16[2048,128]{1,0:T(8,128)(2,1)S(1)} %copy-done.24, bf16[2048,128]{1,0:T(8,128)(2,1)S(1)} %copy-done.25, bf16[2048,128]{1,0:T(8,128)(2,1)S(1)} %copy-done.26, bf16[2048,128]{1,0:T(8,128)(2,1)S(1)} %copy-done.27), kind=kOutput, calls=%fused_computation.132 | convolution fusion | flops 17188257792 | bytes 52428800 | tf_op jit(solution)/shard_map/dot_general | solution.py:43
  822.3 29.5 %add_multiply_fusion.1 = f32[512,8192]{1,0:T(8,128)} fusion(f32[512,8192]{1,0:T(8,128)} %collective-permute-done.2, bf16[2048,8192]{1,0:T(8,128)(2,1)} %fusion.3, bf16[2048,128]{1,0:T(8,128)(2,1)S(1)} %copy-done.22, bf16[2048,128]{1,0:T(8,128)(2,1)S(1)} %copy-done.23, bf16[2048,128]{1,0:T(8,128)(2,1)} %get-tuple-element.102, ...), kind=kOutput, calls=%fused_computation.54 | convolution fusion | flops 17196646400 | bytes 69206016 | tf_op jit(solution)/shard_map/dot_general | solution.py:43
  851.9 29.4 %add_multiply_fusion = f32[512,8192]{1,0:T(8,128)} fusion(f32[512,8192]{1,0:T(8,128)} %collective-permute-done.3, bf16[2048,8192]{1,0:T(8,128)(2,1)} %fusion.3, bf16[2048,128]{1,0:T(8,128)(2,1)S(1)} %copy-done.19, bf16[2048,128]{1,0:T(8,128)(2,1)S(1)} %copy-done.20, bf16[2048,128]{1,0:T(8,128)(2,1)S(1)} %copy-done.21, bf16[2048,128]{1,0:T(8,128)(2,1)S(1)} %copy-done.18), kind=kOutput, calls=%fused_computation.53 | convolution fusion | flops 17196646400 | bytes 69206016 | tf_op jit(solution)/shard_map/dot_general | solution.py:43
  881.3 86.3 %fusion.17 = (f32[2048]{0:T(1024)}, f32[2048]{0:T(1024)S(1)}, bf16[2048,2048]{1,0:T(8,128)(2,1)}) fusion(bf16[2048,2048]{1,0:T(8,128)(2,1)} %get-tuple-element.122, f32[2048]{0:T(1024)S(1)} %copy-done.33, f32[2048]{0:T(1024)S(1)} %bitcast.143, bf16[2048,8192]{1,0:T(8,128)(2,1)} %fusion.3, bf16[2048,8192]{1,0:T(8,128)(2,1)} %all-gather.20.cloned.1.call-done), kind=kOutput, calls=%fused_computation.35 | convolution fusion | flops 68757225472 | bytes 83918848 | tf_op jit(solution)/shard_map/dot_general | solution.py:39
  999.2 238.2 %attn_bwd.1 = (bf16[4,512,2048]{2,1,0:T(8,128)(2,1)}, bf16[4,512,2048]{2,1,0:T(8,128)(2,1)}, bf16[4,512,2048]{2,1,0:T(8,128)(2,1)}, f32[8,512,256]{2,1,0:T(8,128...) custom-call(bf16[4,512,2048]{2,1,0:T(8,128)(2,1)} %bitcast.160, bf16[4,512,2048]{2,1,0:T(8,128)(2,1)} %bitcast.158, ...), custom_call_target="tpu_custom_call" | custom-call | flops 42949672960 | bytes 58720256 | tf_op jit(solution)/shard_map/attn_bwd/pallas_call | solution.py:175
  1355.9 81.6 %fusion.25 = bf16[2048,2048]{1,0:T(8,128)(2,1)} fusion(bf16[2048,2048]{1,0:T(8,128)(2,1)} %get-tuple-element.122, bf16[2048,8192]{1,0:T(8,128)(2,1)} %get-tuple-element.51, bf16[8192,2048]{1,0:T(8,128)(2,1)} %all-gather.22.cloned.1.call-done), kind=kOutput, calls=%fused_computation.43 | convolution fusion | flops 68732059648 | bytes 83886080 | tf_op jit(solution)/shard_map/dot_general | solution.py:35
  1475.2 24.8 %fusion.133 = f32[2048,2048]{1,0:T(8,128)} fusion(bf16[2048,2048]{1,0:T(8,128)(2,1)} %bitcast.169, bf16[2048,2048]{1,0:T(8,128)(2,1)} %all-gather.14.cloned.1.call-done), kind=kOutput, calls=%fused_computation.243 | convolution fusion | flops 17179869184 | bytes 33554432 | tf_op jit(solution)/shard_map/dot_general | solution.py:39
  1500.0 25.2 %fusion.132 = f32[2048,2048]{1,0:T(8,128)} fusion(bf16[2048,2048]{1,0:T(8,128)(2,1)} %bitcast.166, bf16[2048,2048]{1,0:T(8,128)(2,1)} %all-gather.12.cloned.1.call-done), kind=kOutput, calls=%fused_computation.242 | convolution fusion | flops 17179869184 | bytes 33554432 | tf_op jit(solution)/shard_map/dot_general | solution.py:39
  1525.2 32.9 %fusion.18 = (f32[2048]{0:T(1024)S(1)}, f32[2048]{0:T(1024)S(1)}, bf16[2048,2048]{1,0:T(8,128)(2,1)}) fusion(bf16[4,512,2048]{2,1,0:T(8,128)(2,1)} %param.13, f32[2048]{0:T(1024)S(1)} %copy-done.31, f32[2048]{0:T(1024)S(1)} %bitcast.140, bf16[2048,2048]{1,0:T(8,128)(2,1)} %bitcast.163, bf16[2048,2048]{1,0:T(8,128)(2,1)} %all-gather.16.cloned.1.call-done, ...), kind=kOutput, calls=%fused_computation.36 | convolution fusion | flops 17226002432 | bytes 67141632 | tf_op jit(solution)/shard_map/dot_general | solution.py:39
  1558.2 23.8 %all-reduce = f32[8,4,256]{2,1,0:T(4,128)S(1)} all-reduce(f32[8,4,256]{2,1,0:T(4,128)S(1)} %maximum_multiply_fusion), channel_id=4, replica_groups=mesh['fsdp'=8] {'fsdp'}, use_global_device_ids=true, to_apply=%region_8.0.clone | all-reduce | flops 8192 | bytes 65536
  1614.3 78.3 %reduce-scatter.10.cloned.1.call-done = f32[256,2048]{1,0:T(8,128)} async-done(((f32[1024,2048]{1,0:T(8,128)}), f32[256,2048]{1,0:T(8,128)}) %reduce-scatter.10.cloned.1.call-update) | async-done | bytes 2097168 | tf_op jit(solution)/shard_map/reduce_scatter | solution.py:223
  1695.8 80.5 %reduce-scatter.12.cloned.1.call-done = f32[256,2048]{1,0:T(8,128)} async-done(((f32[1024,2048]{1,0:T(8,128)}), f32[256,2048]{1,0:T(8,128)}) %reduce-scatter.12.cloned.1.call-update) | async-done | bytes 2097168 | tf_op jit(solution)/shard_map/reduce_scatter | solution.py:223
  1779.6 80.4 %reduce-scatter.14.cloned.1.call-done = f32[256,2048]{1,0:T(8,128)} async-done(((f32[1024,2048]{1,0:T(8,128)}), f32[256,2048]{1,0:T(8,128)}) %reduce-scatter.14.cloned.1.call-update) | async-done | bytes 2097168 | tf_op jit(solution)/shard_map/reduce_scatter | solution.py:223
  1863.3 147.8 %reduce-scatter.20.cloned.1.call-done = f32[128,8192]{1,0:T(8,128)} async-done(((f32[512,8192]{1,0:T(8,128)}), f32[128,8192]{1,0:T(8,128)}) %reduce-scatter.20.cloned.1.call-update) | async-done | bytes 4194320 | tf_op jit(solution)/shard_map/reduce_scatter | solution.py:223
  2011.0 151.1 %reduce-scatter.22.cloned.1.call-done = f32[128,8192]{1,0:T(8,128)} async-done(((f32[512,8192]{1,0:T(8,128)}), f32[128,8192]{1,0:T(8,128)}) %reduce-scatter.22.cloned.1.call-update) | async-done | bytes 4194320 | tf_op jit(solution)/shard_map/reduce_scatter | solution.py:223
  2170.0 76.4 %reduce-scatter.18.cloned.1.call-done = f32[256,2048]{1,0:T(8,128)} async-done(((f32[1024,2048]{1,0:T(8,128)}), f32[256,2048]{1,0:T(8,128)}) %reduce-scatter.18.cloned.1.call-update) | async-done | bytes 2097168 | tf_op jit(solution)/shard_map/reduce_scatter | solution.py:223
  (217 shorter events, 326.8 us)
Async XLA Ops:
  7.2 69.9 %all-gather.16.cloned.1.call-start = ((), (), s32[]{:S(2)}) async-start(), calls=%async_computation.12 | async-start | bytes 9437184 | tf_op jit(solution)/shard_map/all_gather | solution.py:196
  9.8 114.6 %all-gather.14.cloned.1.call-start = ((), (), s32[]{:S(2)}) async-start(), calls=%async_computation.11 | async-start | bytes 9437184 | tf_op jit(solution)/shard_map/all_gather | solution.py:196
  12.3 163.2 %all-gather.12.cloned.1.call-start = ((), (), s32[]{:S(2)}) async-start(), calls=%async_computation.10 | async-start | bytes 9437184 | tf_op jit(solution)/shard_map/all_gather | solution.py:196
  16.5 27.8 %all-to-all-start = ((bf16[256,8,256]{0,2,1:T(8,128)(2,1)}), bf16[256,8,256]{0,2,1:T(8,128)(2,1)S(1)}, u32[]{:S(2)}, u32[]{:S(2)}) async-start(bf16[256,8,256]{0,2,1:T(8,128)(2,1)} %bitcast.6), calls=%async_computation | async-start | bytes 2097152 | tf_op jit(solution)/shard_map/all_to_all | solution.py:241
  20.7 179.3 %all-gather.26.cloned.1.call-start = ((), (), s32[]{:S(2)}) async-start(), calls=%async_computation.26 | async-start | bytes 2359296 | tf_op jit(solution)/shard_map/all_gather | solution.py:242
  48.4 269.8 %all-gather.18.cloned.1.call-start = ((), (), s32[]{:S(2)}) async-start(), calls=%async_computation.13 | async-start | bytes 9437184 | tf_op jit(solution)/shard_map/all_gather | solution.py:196
  49.0 358.4 %all-gather.20.cloned.1.call-start = ((), (), s32[]{:S(2)}) async-start(), calls=%async_computation.14 | async-start | bytes 37748736 | tf_op jit(solution)/shard_map/all_gather | solution.py:196
  49.6 595.9 %all-gather.22.cloned.1.call-start = ((), (), s32[]{:S(2)}) async-start(), calls=%async_computation.15 | async-start | bytes 37748736 | tf_op jit(solution)/shard_map/all_gather | solution.py:196
  50.4 1387.2 %reduce-scatter.16.cloned.1.call-start = ((), (), s32[]{:S(2)}) async-start(), calls=%async_computation.19 | async-start | bytes 4718592 | tf_op jit(solution)/shard_map/reduce_scatter | solution.py:280
  553.4 36.7 %collective-permute-start = (f32[2048,2048]{1,0:T(8,128)}, f32[2048,2048]{1,0:T(8,128)}, u32[]{:S(2)}, u32[]{:S(2)}) collective-permute-start(f32[2048,2048]{1,0:T(8,128)} %fusion.52), channel_id=1, source_target_pairs={{0,1},{1,0},{2,3},{3,2},{4,5},{5,4},{6,7},{7,6}} | collective-permute-start | bytes 50331656 | tf_op jit(solution)/shard_map/ppermute | solution.py:217
  582.6 34.8 %collective-permute-start.1 = (f32[2048,2048]{1,0:T(8,128)}, f32[2048,2048]{1,0:T(8,128)}, u32[]{:S(2)}, u32[]{:S(2)}) collective-permute-start(f32[2048,2048]{1,0:T(8,128)} %fusion.37), channel_id=1, source_target_pairs={{0,1},{1,0},{2,3},{3,2},{4,5},{5,4},{6,7},{7,6}} | collective-permute-start | bytes 50331656 | tf_op jit(solution)/shard_map/ppermute | solution.py:217
  645.5 121.4 %copy-start.28 = (bf16[2048,128]{1,0:T(8,128)(2,1)S(1)}, bf16[2048,128]{1,0:T(8,128)(2,1)}, u32[]{:S(2)}) copy-start(bf16[2048,128]{1,0:T(8,128)(2,1)} %get-tuple-element.96) | copy-start | bytes 1572868
  645.5 121.4 %copy-start.29 = (bf16[2048,128]{1,0:T(8,128)(2,1)S(1)}, bf16[2048,128]{1,0:T(8,128)(2,1)}, u32[]{:S(2)}) copy-start(bf16[2048,128]{1,0:T(8,128)(2,1)} %get-tuple-element.97) | copy-start | bytes 1572868
  794.2 28.1 %collective-permute-start.2 = (f32[512,8192]{1,0:T(8,128)}, f32[512,8192]{1,0:T(8,128)}, u32[]{:S(2)}, u32[]{:S(2)}) collective-permute-start(f32[512,8192]{1,0:T(8,128)} %fusion.103), channel_id=1, source_target_pairs={{0,1},{1,0},{2,3},{3,2},{4,5},{5,4},{6,7},{7,6}} | collective-permute-start | bytes 50331656 | tf_op jit(solution)/shard_map/ppermute | solution.py:217
  822.2 29.6 %collective-permute-start.3 = (f32[512,8192]{1,0:T(8,128)}, f32[512,8192]{1,0:T(8,128)}, u32[]{:S(2)}, u32[]{:S(2)}) collective-permute-start(f32[512,8192]{1,0:T(8,128)} %fusion.88), channel_id=1, source_target_pairs={{0,1},{1,0},{2,3},{3,2},{4,5},{5,4},{6,7},{7,6}} | collective-permute-start | bytes 50331656 | tf_op jit(solution)/shard_map/ppermute | solution.py:217
  881.3 86.3 %copy-start.43 = (f32[2048]{0:T(1024)S(1)}, f32[2048]{0:T(1024)}, u32[]{:S(2)}) copy-start(f32[2048]{0:T(1024)} %copy-done.42) | copy-start | bytes 24580
  1237.4 345.2 %reduce-scatter.24.cloned.1.call-start = ((), (), s32[]{:S(2)}) async-start(), calls=%async_computation.24 | async-start | bytes 20971520 | tf_op jit(solution)/shard_map/reduce_scatter | solution.py:223
  1238.2 346.1 %reduce-scatter.26.cloned.1.call-start = ((), (), s32[]{:S(2)}) async-start(), calls=%async_computation.25 | async-start | bytes 20971520 | tf_op jit(solution)/shard_map/reduce_scatter | solution.py:223
  1264.7 15.4 collective-permute-start.4
  1265.3 343.6 %all-gather.24.cloned.1.call-start = ((), (), s32[]{:S(2)}) async-start(), calls=%async_computation.20 | async-start | bytes 2359296 | tf_op jit(solution)/shard_map/all_gather | solution.py:295
  1280.2 30.7 %collective-permute-start.5 = (f32[1024,2048]{1,0:T(8,128)}, f32[1024,2048]{1,0:T(8,128)}, u32[]{:S(2)}, u32[]{:S(2)}) collective-permute-start(f32[1024,2048]{1,0:T(8,128)} %fusion.130), channel_id=1, source_target_pairs={{0,1},{1,0},{2,3},{3,2},{4,5},{5,4},{6,7},{7,6}} | collective-permute-start | bytes 25165832 | tf_op jit(solution)/shard_map/ppermute | solution.py:217
  1310.3 30.6 %collective-permute-start.6 = (f32[1024,2048]{1,0:T(8,128)}, f32[1024,2048]{1,0:T(8,128)}, u32[]{:S(2)}, u32[]{:S(2)}) collective-permute-start(f32[1024,2048]{1,0:T(8,128)} %fusion.129), channel_id=1, source_target_pairs={{0,1},{1,0},{2,3},{3,2},{4,5},{5,4},{6,7},{7,6}} | collective-permute-start | bytes 25165832 | tf_op jit(solution)/shard_map/ppermute | solution.py:217
  1442.3 250.3 %reduce-scatter.10.cloned.1.call-start = ((), (), s32[]{:S(2)}) async-start(), calls=%async_computation.16 | async-start | bytes 10485760 | tf_op jit(solution)/shard_map/reduce_scatter | solution.py:223
  1442.9 333.5 %reduce-scatter.12.cloned.1.call-start = ((), (), s32[]{:S(2)}) async-start(), calls=%async_computation.17 | async-start | bytes 10485760 | tf_op jit(solution)/shard_map/reduce_scatter | solution.py:223
  1443.6 416.4 %reduce-scatter.14.cloned.1.call-start = ((), (), s32[]{:S(2)}) async-start(), calls=%async_computation.18 | async-start | bytes 10485760 | tf_op jit(solution)/shard_map/reduce_scatter | solution.py:223
  1444.2 566.8 %reduce-scatter.20.cloned.1.call-start = ((), (), s32[]{:S(2)}) async-start(), calls=%async_computation.22 | async-start | bytes 20971520 | tf_op jit(solution)/shard_map/reduce_scatter | solution.py:223
  1444.8 717.3 %reduce-scatter.22.cloned.1.call-start = ((), (), s32[]{:S(2)}) async-start(), calls=%async_computation.23 | async-start | bytes 20971520 | tf_op jit(solution)/shard_map/reduce_scatter | solution.py:223
  1445.4 800.9 %reduce-scatter.18.cloned.1.call-start = ((), (), s32[]{:S(2)}) async-start(), calls=%async_computation.21 | async-start | bytes 10485760 | tf_op jit(solution)/shard_map/reduce_scatter | solution.py:223
  1445.4 13.4 collective-permute-start.7
  1525.2 32.9 %copy-start.44 = (f32[8,1,256]{2,1,0:T(1,128)S(1)}, f32[8,1,256]{2,1,0:T(1,128)}, u32[]{:S(2)}) copy-start(f32[8,1,256]{2,1,0:T(1,128)} %stack.30) | copy-start | bytes 24580
  1525.2 32.9 %copy-start.45 = (f32[8,1,256]{2,1,0:T(1,128)S(1)}, f32[8,1,256]{2,1,0:T(1,128)}, u32[]{:S(2)}) copy-start(f32[8,1,256]{2,1,0:T(1,128)} %stack.29) | copy-start | bytes 24580
  1525.2 57.3 %copy-start.39 = (f32[1,4,4,128]{3,1,2,0:T(4,128)S(1)}, f32[1,4,4,128]{3,1,2,0:T(4,128)}, u32[]{:S(2)}) copy-start(f32[1,4,4,128]{3,1,2,0:T(4,128)} %copy-done.38) | copy-start | bytes 24580
  (46 other events, 777.7 us)
Sparse Core Ops, SparseCore 0:
  10.4 62.8 all-gather.15
  75.7 48.6 all-gather.13
  126.8 48.6 all-gather.11
  177.8 22.2 all-gather.25
  201.7 48.8 all-gather.17
  252.2 155.1 all-gather.19
  409.2 157.3 all-gather.21
  1237.5 42.9 reduce-scatter.15
  1283.6 148.1 reduce-scatter.23
  1434.6 149.5 reduce-scatter.25
  1586.6 22.2 all-gather.23
  1611.8 80.7 reduce-scatter.9
  1695.5 80.7 reduce-scatter.11
  1779.2 80.7 reduce-scatter.13
  1862.8 148.1 reduce-scatter.19
  2013.9 148.1 reduce-scatter.21
  2165.5 80.7 reduce-scatter.17

commit v2 on v1

v2 whole, which is shorter than its diff:
```python
import functools

import jax
import jax.numpy as jnp
from jax import lax
from jax.experimental import pallas as pl
from jax.experimental.layout import Layout, with_layout_constraint
from jax.experimental.pallas import tpu as pltpu
from jax.sharding import PartitionSpec as P


EPS = 1e-6
MASK_VALUE = -1e30
BLK = 128
SUB = 64
SEQ = 512
F32 = jnp.float32
BF16 = jnp.bfloat16


def sin_table(seq_len, model_width):
    distance = (seq_len - 1 - jnp.arange(seq_len)).astype(F32)
    inv_freq = 10000.0 ** (-jnp.arange(0, model_width, 2).astype(F32) / model_width)
    angles = distance[:, None] * inv_freq[None, :]
    return jnp.concatenate([jnp.sin(angles), jnp.cos(angles)], axis=-1).astype(BF16)


def rms_norm(x_f32, gain_vec):
    mean_sq = jnp.mean(x_f32 * x_f32, axis=-1, keepdims=True)
    return (x_f32 * lax.rsqrt(mean_sq + EPS) * gain_vec).astype(BF16)


def gelu_tanh(pre_f32):
    return jax.nn.gelu(pre_f32, approximate=True)


def dot_nn(a, b):
    return lax.dot_general(a, b, (((1,), (0,)), ((), ())), preferred_element_type=F32)


def dot_nt(a, b):
    return lax.dot_general(a, b, (((1,), (1,)), ((), ())), preferred_element_type=F32)


def dot_tn(a, b):
    return lax.dot_general(a, b, (((0,), (0,)), ((), ())), preferred_element_type=F32)


def after(value, *earlier):
    return lax.optimization_barrier((value, *earlier))[0]


def tril_mask(first):
    shape = (SUB, BLK)
    return lax.broadcasted_iota(jnp.int32, shape, 0) + first >= lax.broadcasted_iota(jnp.int32, shape, 1)


def shear(x, first):
    return pltpu.roll(x, 1 + first, axis=1, stride=1, stride_axis=0)


def halves_of(seq_len):
    half = seq_len // 2
    return [(slice(h * half, (h + 1) * half), (h + 1) * half) for h in range(2)]


def fill_scores(q_u, q_w, keys, rel, s_ref, t_ref):
    seq_len = q_u.shape[0]
    for rows, top in halves_of(seq_len):
        s_ref[rows, :top] = dot_nt(q_u[rows], keys[:top])
        t_ref[rows, :top] = dot_nt(q_w[rows], rel[seq_len - top:])


def row_pieces(seq_len):
    return [(slice(at, at + SUB), at // BLK, at % BLK) for at in range(0, seq_len, SUB)]


def piece_probs(s_ref, t_ref, piece, head_dim):
    rows, block, first = piece
    tril = tril_mask(first)
    skip = 1 - block % 2
    scale = head_dim ** -0.5
    turned = [shear(t_ref[rows, (skip + c) * BLK:(skip + c + 1) * BLK], first) for c in range(block + 1)]
    parts = []
    for c in range(block + 1):
        part = s_ref[rows, c * BLK:(c + 1) * BLK]
        if c < block:
            part = (part + jnp.where(tril, turned[c], turned[c + 1])) * scale
        else:
            part = jnp.where(tril, (part + turned[c]) * scale, MASK_VALUE)
        parts.append(part)
    logits = jnp.concatenate(parts, axis=1) if block else parts[0]
    grown = jnp.exp(logits - jnp.max(logits, axis=1, keepdims=True))
    return grown * (1.0 / jnp.sum(grown, axis=1, keepdims=True))


def put_piece(ref, piece, value, front):
    rows, block, _ = piece
    width = (block + 1) * BLK
    skip = BLK if front and block % 2 == 0 else 0
    ref[rows, skip:skip + width] = value
    if block % 2 == 0:
        rest = 0 if front else width
        ref[rows, rest:rest + BLK] = jnp.zeros((SUB, BLK), ref.dtype)


def unpack_rel(r_ref):
    width = r_ref.shape[1] * r_ref.shape[2] // SEQ
    return jnp.concatenate([r_ref[0, :, at:at + width] for at in range(0, r_ref.shape[2], width)], axis=0)


def attn_fwd_kernel(qkv_ref, r_ref, u_ref, w_ref, c_ref, s_all, t_all, p_all, *, heads, head_dim):
    seq_len = qkv_ref.shape[1]
    q_ref, k_ref, v_ref = (qkv_ref.at[:, :, part * heads * head_dim:(part + 1) * heads * head_dim] for part in range(3))
    rel_pair = unpack_rel(r_ref)
    all_cols = [slice(n * head_dim, (n + 1) * head_dim) for n in range(heads)]
    for n, cols in enumerate(all_cols):
        q_f32 = q_ref[0, :, cols].astype(F32)
        q_u = (q_f32 + u_ref[0, :, cols]).astype(BF16)
        q_w = (q_f32 + w_ref[0, :, cols]).astype(BF16)
        fill_scores(q_u, q_w, k_ref[0, :, cols], rel_pair[:, cols], s_all.at[n], t_all.at[n])
    for piece in row_pieces(seq_len):
        for n in range(heads):
            put_piece(p_all.at[n], piece, piece_probs(s_all.at[n], t_all.at[n], piece, head_dim).astype(BF16), False)
    for n, cols in enumerate(all_cols):
        for rows, top in halves_of(seq_len):
            c_ref[0, rows, cols] = dot_nn(p_all[n, rows, :top], v_ref[0, :top, cols]).astype(BF16)


def attn_bwd_kernel(qkv_ref, r_ref, u_ref, w_ref, dc_ref, dqkv_ref, dr_ref, du_ref, dw_ref,
                    s_all, t_all, dp_all, p_all, ds_all, dt_all, qu_all, qw_all, rb_all, *, heads, head_dim):
    seq_len = qkv_ref.shape[1]
    parts = [slice(part * heads * head_dim, (part + 1) * heads * head_dim) for part in range(3)]
    q_ref, k_ref, v_ref = (qkv_ref.at[:, :, part] for part in parts)
    dq_ref, dk_ref, dv_ref = (dqkv_ref.at[:, :, part] for part in parts)
    rel_pair = unpack_rel(r_ref)
    blocks = seq_len // BLK
    flip = (lax.broadcasted_iota(jnp.int32, (BLK, BLK), 0) + lax.broadcasted_iota(jnp.int32, (BLK, BLK), 1)
            == BLK - 1).astype(F32).astype(BF16)
    scale = head_dim ** -0.5
    all_cols = [slice(n * head_dim, (n + 1) * head_dim) for n in range(heads)]

    @pl.when(pl.program_id(1) == 0)
    def _():
        dr_ref[...] = jnp.zeros_like(dr_ref)
        du_ref[...] = jnp.zeros_like(du_ref)
        dw_ref[...] = jnp.zeros_like(dw_ref)

    for n, cols in enumerate(all_cols):
        q_f32 = q_ref[0, :, cols].astype(F32)
        qu_all[n] = (q_f32 + u_ref[0, :, cols]).astype(BF16)
        qw_all[n] = (q_f32 + w_ref[0, :, cols]).astype(BF16)
        rel = rel_pair[:, cols]
        fill_scores(qu_all[n], qw_all[n], k_ref[0, :, cols], rel, s_all.at[n], t_all.at[n])
        for rows, top in halves_of(seq_len):
            dp_all[n, rows, :top] = dot_nt(dc_ref[0, rows, cols], v_ref[0, :top, cols]).astype(BF16)
        for c in range(blocks):
            rb_all[n, c * BLK:(c + 1) * BLK] = dot_nn(flip, rel[c * BLK:(c + 1) * BLK]).astype(BF16)
    for piece in row_pieces(seq_len):
        for n in range(heads):
            probs = piece_probs(s_all.at[n], t_all.at[n], piece, head_dim)
            d_probs = dp_all[n, piece[0], :(piece[1] + 1) * BLK].astype(F32)
            inner = jnp.sum(probs * d_probs, axis=1, keepdims=True)
            put_piece(p_all.at[n], piece, probs.astype(BF16), False)
            put_piece(ds_all.at[n], piece, (probs * (d_probs - inner) * scale).astype(BF16), False)
    for n in range(heads):
        for rows, top in halves_of(seq_len):
            for c in range(top // BLK):
                t_all[n, rows, c * BLK:(c + 1) * BLK] = dot_nn(ds_all[n, rows, c * BLK:(c + 1) * BLK], flip)
    for piece in row_pieces(seq_len):
        rows, block, first = piece
        tril = tril_mask(first)
        for n in range(heads):
            turned = [shear(t_all[n, rows, c * BLK:(c + 1) * BLK], first) for c in range(block + 1)]
            parts = [jnp.where(tril, turned[c], turned[c - 1] if c else 0.0).astype(BF16) for c in range(block + 1)]
            put_piece(dt_all.at[n], piece, jnp.concatenate(parts, axis=1) if block else parts[0], True)
    (low, near), (high, far) = halves_of(seq_len)
    for n, cols in enumerate(all_cols):
        for rows, top in halves_of(seq_len):
            d_qu = dot_nn(ds_all[n, rows, :top], k_ref[0, :top, cols]).astype(BF16).astype(F32)
            d_qw = dot_nn(dt_all[n, rows, :top], rb_all[n, seq_len - top:]).astype(BF16).astype(F32)
            dq_ref[0, rows, cols] = (d_qu + d_qw).astype(BF16)
            du_ref[0, :, cols] += jnp.sum(d_qu.reshape(-1, 8, head_dim), axis=0)
            dw_ref[0, :, cols] += jnp.sum(d_qw.reshape(-1, 8, head_dim), axis=0)
        for out_ref, left, right in ((dk_ref, ds_all.at[n], qu_all[n]), (dv_ref, p_all.at[n], dc_ref[0, :, cols])):
            whole = dot_tn(left[high, :], right[high])
            out_ref[0, :near, cols] = (whole[:near] + dot_tn(left[low, :near], right[low])).astype(BF16)
            out_ref[0, near:, cols] = whole[near:].astype(BF16)
        dr_ref[0, :, cols] += dot_tn(dt_all[n, high, :], qw_all[n, high])
        dr_ref[0, near:, cols] += dot_tn(dt_all[n, low, :near], qw_all[n, low])


def attn_args(qkv, rel, bias_u, head_dim, first):
    _, seq_len, width = qkv.shape
    groups, _, span = bias_u.shape
    lines = seq_len * span // rel.shape[2]
    at = rel.shape[1] // lines - 1
    specs = [
        pl.BlockSpec((1, seq_len, width // groups), lambda g, b: (b, 0, g + first)),
        pl.BlockSpec((1, lines, rel.shape[2]), lambda g, b: (g + first, at, 0)),
        pl.BlockSpec((1, 1, span), lambda g, b: (g + first, 0, 0)),
        pl.BlockSpec((1, 1, span), lambda g, b: (g + first, 0, 0)),
    ]
    heads = span // head_dim

    def square(*dtypes):
        return [pltpu.VMEM((heads, seq_len, seq_len), dtype) for dtype in dtypes]

    return specs, square, heads, span


def attn_fwd(qkv, rel, bias_u, bias_w, head_dim):
    batch, seq_len, width = qkv.shape
    groups = bias_u.shape[0]
    specs, square, heads, span = attn_args(qkv, rel, bias_u, head_dim, 0)
    work = batch * groups * heads * seq_len * seq_len * head_dim
    return pl.pallas_call(
        functools.partial(attn_fwd_kernel, heads=heads, head_dim=head_dim),
        grid=(groups, batch),
        in_specs=specs,
        out_specs=pl.BlockSpec((1, seq_len, span), lambda g, b: (b, 0, g)),
        out_shape=jax.ShapeDtypeStruct((batch, seq_len, groups * span), BF16),
        scratch_shapes=square(F32, F32, BF16),
        compiler_params=pltpu.CompilerParams(
            dimension_semantics=("arbitrary", "arbitrary")),
        cost_estimate=pl.CostEstimate(flops=8 * work, bytes_accessed=8 * batch * seq_len * width // 3, transcendentals=0),
        name="attn_fwd",
    )(qkv, rel, bias_u, bias_w)


def attn_bwd(qkv, rel, bias_u, bias_w, d_ctx, head_dim, first, count):
    batch, seq_len, _ = qkv.shape
    specs, square, heads, span = attn_args(qkv, rel, bias_u, head_dim, first)
    work = batch * count * heads * seq_len * seq_len * head_dim
    small = jax.ShapeDtypeStruct((count, 8, span), F32)
    vec8 = pl.BlockSpec((1, 8, span), lambda g, b: (g, 0, 0))
    return pl.pallas_call(
        functools.partial(attn_bwd_kernel, heads=heads, head_dim=head_dim),
        grid=(count, batch),
        in_specs=specs + [pl.BlockSpec((1, seq_len, span), lambda g, b: (b, 0, g + first))],
        out_specs=[pl.BlockSpec((1, seq_len, 3 * span), lambda g, b: (b, 0, g)),
                   pl.BlockSpec((1, seq_len, span), lambda g, b: (g, 0, 0)), vec8, vec8],
        out_shape=[jax.ShapeDtypeStruct((batch, seq_len, 3 * count * span), BF16),
                   jax.ShapeDtypeStruct((count, seq_len, span), F32), small, small],
        scratch_shapes=square(F32, F32, BF16, BF16, BF16, BF16) + [pltpu.VMEM((heads, seq_len, head_dim), BF16)] * 3,
        compiler_params=pltpu.CompilerParams(dimension_semantics=("arbitrary", "arbitrary")),
        cost_estimate=pl.CostEstimate(flops=20 * work, bytes_accessed=14 * batch * seq_len * count * span, transcendentals=0),
        name="attn_bwd",
    )(qkv, rel, bias_u, bias_w, d_ctx)


def interleave_kernel(*refs):
    out_ref = refs[-1]
    for n, ref in enumerate(refs[:-1]):
        width = ref.shape[-1]
        out_ref[..., n * width:(n + 1) * width] = ref[...]


def interleave(arrays, width):
    rows, cols = arrays[0].shape
    spec = pl.BlockSpec((rows, width), lambda i: (0, i))
    total = len(arrays) * cols
    return pl.pallas_call(
        interleave_kernel,
        grid=(cols // width,),
        in_specs=[spec] * len(arrays),
        out_specs=pl.BlockSpec((rows, len(arrays) * width), lambda i: (0, i)),
        out_shape=jax.ShapeDtypeStruct((rows, total), arrays[0].dtype),
        cost_estimate=pl.CostEstimate(flops=rows * total, bytes_accessed=4 * rows * total, transcendentals=0),
        name="interleave",
    )(*arrays)


def separate_kernel(in_ref, out_ref):
    width = out_ref.shape[-1]
    for n in range(out_ref.shape[0]):
        out_ref[n] = in_ref[:, n * width:(n + 1) * width]


def separate(array, count, width):
    rows, cols = array.shape
    return pl.pallas_call(
        separate_kernel,
        grid=(cols // (count * width),),
        in_specs=[pl.BlockSpec((rows, count * width), lambda i: (0, i))],
        out_specs=pl.BlockSpec((count, rows, width), lambda i: (0, 0, i)),
        out_shape=jax.ShapeDtypeStruct((count, rows, cols // count), array.dtype),
        cost_estimate=pl.CostEstimate(flops=rows * cols, bytes_accessed=4 * rows * cols, transcendentals=0),
        name="separate",
    )(array)


def solution(mesh):
    axis_name = mesh.axis_names[0]
    group_size = mesh.shape[axis_name]
    chips = group_size // 2
    pairs = [(d, d ^ 1) for d in range(group_size)]
    same_core = [[2 * c + core for c in range(chips)] for core in range(2)]

    def gather(local_shard):
        return lax.all_gather(local_shard, axis_name, axis=0, tiled=True)

    def local_step(x_in, grad_out, norm_attn, w_query, w_key, w_value, w_rel, bias_u, bias_w, w_attn_out, norm_mlp, w_up, w_down):
        batch_local, seq_len, width = x_in.shape
        num_heads, head_dim = w_query.shape[1], w_query.shape[2]
        hidden = num_heads * head_dim
        tokens = batch_local * seq_len
        span = hidden // group_size
        scale = 1.0 / (batch_local * group_size)
        me = lax.axis_index(axis_name)
        core = lax.rem(me, 2)

        def shares(acts, kind):
            part = acts.shape[1] // group_size
            return jnp.concatenate(
                [lax.dynamic_slice(acts, (0, (2 * c + kind) * part), (tokens, part)) for c in range(chips)], axis=1)

        def theirs(acts, cots):
            mine = dot_tn(shares(acts, 1 - core), cots)
            return mine, lax.ppermute(mine, axis_name, pairs)

        def ours(acts, cots, received):
            return (dot_tn(shares(acts, core), cots) + received) * scale

        def spread(summed):
            return lax.psum_scatter(summed, axis_name, scatter_dimension=0, axis_index_groups=same_core, tiled=True)

        def gather_halves(stacked):
            full = lax.all_gather(stacked, axis_name, axis=1, tiled=True)
            return with_layout_constraint(full, Layout(major_to_minor=(0, 1, 2)))

        x_f32 = x_in.reshape(tokens, width).astype(F32)
        dy = grad_out.reshape(tokens, width)
        vecs = lax.all_gather(jnp.stack([norm_attn, bias_u, bias_w, norm_mlp]), axis_name, axis=0)
        gain_attn = vecs[:, 0].reshape(width).astype(F32)
        u_full = vecs[:, 1:2].astype(F32)
        w_full = vecs[:, 2:3].astype(F32)
        gain_mlp = vecs[:, 3].reshape(width).astype(F32)

        qkv_own = interleave([z.reshape(-1, hidden) for z in (w_query, w_key, w_value)], span)
        qkv_full = gather(qkv_own)

        pos_table = sin_table(seq_len, width)
        rel_rows = after(w_rel, qkv_own).reshape(-1, hidden)
        rel_cols = lax.all_to_all(rel_rows, axis_name, split_axis=1, concat_axis=0, tiled=True)
        rel_own = dot_nn(pos_table, rel_cols).astype(BF16)
        lines = seq_len * span // width
        folded = jnp.concatenate([rel_own[at:at + lines] for at in range(0, seq_len, lines)], axis=1)
        out_rel = lax.all_gather(jnp.concatenate([w_attn_out, folded], axis=0), axis_name, axis=0)
        out_full = out_rel[:, :-lines].reshape(hidden, width)

        ff_half = w_up.shape[1] // 2
        part = ff_half // group_size
        up_own = separate(after(w_up, qkv_own), 2, part)
        up_full = gather_halves(up_own)
        down_full = gather_halves(after(w_down, up_own).reshape(2, part, width))

        h_attn = rms_norm(x_f32, gain_attn)
        shape3 = (batch_local, seq_len, -1)
        qkv = dot_nn(h_attn, qkv_full).astype(BF16).reshape(shape3)
        context = attn_fwd(qkv, out_rel, u_full, w_full, head_dim).reshape(tokens, hidden)
        x1_f32 = (x_f32 + dot_nn(context, out_full)).astype(BF16).astype(F32)
        h_mlp = rms_norm(x1_f32, gain_mlp)

        def feed(acts, weight):
            pre = dot_nn(acts, weight).astype(BF16)
            return pre, gelu_tanh(pre.astype(F32)).astype(BF16)

        def unfeed(cots, weight, pre):
            d_act = dot_nt(cots, weight).astype(BF16)
            return jax.vjp(gelu_tanh, pre.astype(F32))[1](d_act.astype(F32))[0].astype(BF16)

        pre0, act0 = feed(h_mlp, up_full[0])
        sent, got = theirs(act0, dy)
        pre1, act1 = feed(after(h_mlp, sent), up_full[1])
        sum_down0 = ours(after(act0, act1), dy, got)
        sent, got = theirs(act1, after(dy, sum_down0))
        d_pre0 = unfeed(after(dy, sent), down_full[0], pre0)
        sum_down1 = ours(after(act1, d_pre0), dy, got)
        sent, got = theirs(h_mlp, after(d_pre0, sum_down1))
        d_pre1 = unfeed(after(dy, sent), down_full[1], pre1)
        sum_up0 = ours(h_mlp, after(d_pre0, d_pre1), got)
        sent, got = theirs(h_mlp, after(d_pre1, sum_up0))
        d_h_part = dot_nt(after(d_pre0, sent), up_full[0])
        sum_up1 = ours(h_mlp, after(d_pre1, d_h_part), got)
        d_h_mlp = (d_h_part + dot_nt(after(d_pre1, sum_up1), up_full[1])).astype(BF16)
        grad_down = jnp.concatenate([spread(sum_down0), spread(sum_down1)], axis=0)
        grad_up0, grad_up1 = spread(sum_up0), spread(sum_up1)

        d_x1_norm, grad_norm_mlp = jax.vjp(rms_norm, x1_f32, gain_mlp)[1](d_h_mlp)
        d_x1 = (dy.astype(F32) + d_x1_norm).astype(BF16)
        d_context = dot_nt(d_x1, out_full).astype(BF16).reshape(shape3)
        pairs_half = group_size // 2
        d_low, d_rel_low, d_u_low, d_w_low = attn_bwd(
            qkv, out_rel, u_full, w_full, d_context, head_dim, 0, pairs_half)
        d_low = d_low.reshape(tokens, -1)
        sent, got = theirs(h_attn, d_low)
        sent_o, got_o = theirs(context, after(d_x1, sent))
        sum_low = ours(h_attn, after(d_low, sent_o), got)
        d_high, d_rel_high, d_u_high, d_w_high = attn_bwd(
            qkv, out_rel, u_full, w_full, after(d_context, sum_low), head_dim, pairs_half, pairs_half)
        d_high = d_high.reshape(tokens, -1)
        d_rel_own = lax.psum_scatter(
            jnp.concatenate([d_rel_low, d_rel_high], axis=0), axis_name, scatter_dimension=0, tiled=True)[0]
        sent, got = theirs(h_attn, d_high)
        sum_o = ours(context, after(d_x1, sent), got_o)
        sum_high = ours(h_attn, after(d_high, sum_o), got)
        grad_low, grad_high = spread(sum_low), spread(sum_high)
        y_out = (x1_f32 + dot_nn(after(act0, sum_high), down_full[0]) + dot_nn(act1, down_full[1])).astype(BF16)
        d_rel_own = after(d_rel_own, y_out)
        d_rel_own = jnp.flip(d_rel_own.reshape(seq_len // BLK, BLK, span), axis=1).reshape(seq_len, span).astype(BF16)
        d_rel_all = lax.all_gather(d_rel_own, axis_name, axis=0)
        grad_attn_out = spread(after(sum_o, d_rel_own))

        cut = qkv_full.shape[1] // 2
        d_h_attn = (dot_nt(after(d_low, d_rel_own), qkv_full[:, :cut]) + dot_nt(d_high, qkv_full[:, cut:])).astype(BF16)
        d_x_norm, grad_norm_attn = jax.vjp(rms_norm, x_f32, gain_attn)[1](d_h_attn)
        grad_x = (d_x1.astype(F32) + d_x_norm).astype(BF16)

        table_own = lax.dynamic_slice(pos_table, (0, me * (width // group_size)), (seq_len, width // group_size))
        grad_rel = dot_tn(table_own, jnp.swapaxes(d_rel_all, 0, 1).reshape(seq_len, hidden)) * scale
        grad_up = interleave([grad_up0, grad_up1], part)
        grad_parts = [z.reshape(-1, pairs_half, 3, span) for z in (grad_low, grad_high)]
        grad_query, grad_key, grad_value = (
            jnp.concatenate([z[:, :, n] for z in grad_parts], axis=1) for n in range(3))
        d_u = jnp.concatenate([d_u_low, d_u_high], axis=0)
        d_w = jnp.concatenate([d_w_low, d_w_high], axis=0)

        small = jnp.stack([grad_norm_attn.reshape(group_size, span), jnp.sum(d_u, axis=1), jnp.sum(d_w, axis=1),
                           grad_norm_mlp.reshape(group_size, span)], axis=1)
        small = lax.psum_scatter(small * scale, axis_name, scatter_dimension=0, tiled=True)[0]

        heads3 = (-1, num_heads, head_dim)
        return (y_out.reshape(x_in.shape), grad_x.reshape(x_in.shape), small[0], grad_query.reshape(heads3),
                grad_key.reshape(heads3), grad_value.reshape(heads3), grad_rel.reshape(heads3), small[1], small[2],
                grad_attn_out, small[3], grad_up, grad_down)

    sharded = P(axis_name)
    return jax.shard_map(local_step, mesh=mesh, in_specs=(sharded,) * 13, out_specs=(sharded,) * 13, check_vma=False)
```

time: 2260 us -> 2190 us (0.969)
  Pallas kernels: 356 us -> 208 us
  waiting for transfers between devices: 759 us -> 824 us
    pallas_call x2 -> x6, Pallas kernels: 356 us -> 208 us  [the longest x2 119 us: attn_bwd(): pl.pallas_call(functools.partial(attn_bwd_kernel, heads=heads, head_dim=h...]
    dot_general x17 -> x15, matrix products: 346 us -> 315 us  [dot_tn(): lax.dot_general(a, b, (((0,), (0,)), ((), ())), preferred_element_type=F32)]
    reduce_scatter x8 -> x7, waiting for transfers between devices: 616 us -> 646 us  [spread(): lax.psum_scatter(summed, axis_name, scatter_dimension=0, axis_index_group...]
    dot_general x6 -> x7, matrix products: 311 us -> 328 us  [dot_nt(): lax.dot_general(a, b, (((1,), (1,)), ((), ())), preferred_element_type=F32)]
    all_gather x6 -> x1, waiting for transfers between devices: 105 us -> 112 us  [gather(): return lax.all_gather(local_shard, axis_name, axis=0, tiled=True)]
    dynamic_slice x3 -> x7, local copies, waits for them, and re-layouts: 42.1 us -> 45.6 us  [shares(): lax.dynamic_slice(acts, (0, (2 * c + kind) * part), (tokens, part))]
  transfers between devices with their start and end apart: 26 -> 21, of which waited for: 14 -> 11; matrix products, arithmetic and copies ran while one was open for 35% -> 38% of each run, Pallas kernels for 5% -> 4%
where the time goes in v2:
time: 2190 us; the launch traced here: 2180 us
  matrix products  928 us (42%)
  waiting for transfers between devices  824 us (38%)
  Pallas kernels  208 us (9%)
  local copies, waits for them, and re-layouts  94.2 us (4%)
  other arithmetic  72.4 us (3%)
  blocking collectives  34.9 us (2%)
    reduce_scatter x7, waiting for transfers between devices, spread(): lax.psum_scatter(summed, axis_name, scatter_dimension=0, axis_index_group...  646 us
    dot_general x7, matrix products, dot_nt(): lax.dot_general(a, b, (((1,), (1,)), ((), ())), preferred_element_type=F32)  328 us
    dot_general x15, matrix products, dot_tn(): lax.dot_general(a, b, (((0,), (0,)), ((), ())), preferred_element_type=F32)  315 us
    dot_general x7, matrix products, dot_nn(): lax.dot_general(a, b, (((1,), (0,)), ((), ())), preferred_element_type=F32)  285 us
    pallas_call x2, Pallas kernels, attn_bwd(): pl.pallas_call(functools.partial(attn_bwd_kernel, heads=heads, head_dim=h...  119 us
    all_gather x1, waiting for transfers between devices, gather(): return lax.all_gather(local_shard, axis_name, axis=0, tiled=True)  112 us
    pallas_call x1, Pallas kernels, attn_fwd(): pl.pallas_call(functools.partial(attn_fwd_kernel, heads=heads, head_dim=h...  66.8 us
    dynamic_slice x7, local copies, waits for them, and re-layouts, shares(): lax.dynamic_slice(acts, (0, (2 * c + kind) * part), (tokens, part))  45.6 us
  transfers between devices with their start and end apart: 21, of which 11 were waited for; matrix products, arithmetic and copies ran while one was open for 38% of the time, Pallas kernels for 4%

profile of v2, /device:TPU:0, one launch (start us, length us, event | category | flops | bytes accessed | tf_op | source)
XLA Modules:
  0.0 2182.7 jit_solution(8672668284527752935)
XLA Ops:
  111.7 112.4 %all-gather.9.cloned.1.call-done = bf16[2048,6144]{1,0:T(8,128)(2,1)} async-done(((bf16[256,6144]{1,0:T(8,128)(2,1)}), bf16[2048,6144]{1,0:T(8,128)(2,1)}) %all-gather.9.cloned.1.call-update) | async-done | bytes 25165840 | tf_op jit(solution)/shard_map/all_gather | solution.py:301
  224.1 60.4 %convolution_convert_fusion = bf16[2048,6144]{1,0:T(8,128)(2,1)} fusion(bf16[2048,2048]{1,0:T(8,128)(2,1)} %fusion.39, bf16[2048,6144]{1,0:T(8,128)(2,1)} %all-gather.9.cloned.1.call-done), kind=kOutput, calls=%fused_computation.41 | convolution fusion | flops 51552190464 | bytes 58720256 | tf_op jit(solution)/shard_map/dot_general | solution.py:38
  284.4 66.8 %attn_fwd.1 = bf16[4,512,2048]{2,1,0:T(8,128)(2,1)} custom-call(bf16[4,512,6144]{2,1,0:T(8,128)(2,1)} %bitcast.190, bf16[8,320,2048]{2,1,0:T(8,128)(2,1)} %bitcast.163, f32[8,1,256]{2,1,0:T(1,128)} %get-tuple-element.172.u_ref, f32[8,1,256]{2,1,0:T(1,128)} %get-tuple-element.171.w_ref), custom_call_target="tpu_custom_call" | custom-call | flops 17179869184 | bytes 33554432 | tf_op jit(solution)/shard_map/attn_fwd/pallas_call | solution.py:217
  351.2 24.8 %fusion.34 = (f32[2048]{0:T(1024)S(1)}, bf16[2048,2048]{1,0:T(8,128)(2,1)}) fusion(bf16[2048,2048]{1,0:T(8,128)(2,1)} %bitcast.145, bf16[2048,2048]{1,0:T(8,128)(2,1)} %bitcast.148, bf16[4,512,2048]{2,1,0:T(8,128)(2,1)} %param.13), kind=kOutput, calls=%fused_computation.58 | convolution fusion | flops 17205032960 | bytes 33562624 | tf_op jit(solution)/shard_map/dot_general | solution.py:38
  386.4 53.4 %fusion.13 = (bf16[2048,4096]{1,0:T(8,128)(2,1)}, bf16[2048,4096]{1,0:T(8,128)(2,1)}) fusion(bf16[2048,2048]{1,0:T(8,128)(2,1)} %fusion.26, bf16[2,2048,4096]{2,1,0:T(8,128)(2,1)} %all-gather.11.cloned.1.call-done), kind=kOutput, calls=%fused_computation.25 | convolution fusion | flops 34452013056 | bytes 58720256 | tf_op jit(solution)/shard_map/dot_general | solution.py:38
  448.3 28.0 %fusion.50 = f32[2048,2048]{1,0:T(8,128)} fusion(bf16[2048,2048]{1,0:T(8,128)(2,1)} %bitcast.153, bf16[2048,512]{1,0:T(8,128)(2,1)} %get-tuple-element.133, bf16[2048,512]{1,0:T(8,128)(2,1)} %get-tuple-element.134, bf16[2048,512]{1,0:T(8,128)(2,1)} %get-tuple-element.135, bf16[2048,512]{1,0:T(8,128)(2,1)S(1)} %get-tuple-element.132), kind=kOutput, calls=%fused_computation.92 | convolution fusion | flops 17213423616 | bytes 33554432 | tf_op jit(solution)/shard_map/dot_general | solution.py:46
  476.5 51.1 %fusion.19 = (bf16[2048,4096]{1,0:T(8,128)(2,1)}, bf16[2048,4096]{1,0:T(8,128)(2,1)}) fusion(bf16[2048,2048]{1,0:T(8,128)(2,1)} %fusion.26, bf16[2,2048,4096]{2,1,0:T(8,128)(2,1)} %all-gather.11.cloned.1.call-done), kind=kOutput, calls=%fused_computation.31 | convolution fusion | flops 34452013056 | bytes 58720256 | tf_op jit(solution)/shard_map/dot_general | solution.py:38
  542.2 27.1 %add_multiply_fusion.3 = f32[2048,2048]{1,0:T(8,128)} fusion(f32[2048,2048]{1,0:T(8,128)} %collective-permute-done, bf16[2048,2048]{1,0:T(8,128)(2,1)S(1)} %bitcast.159, bf16[2048,512]{1,0:T(8,128)(2,1)} %get-tuple-element.129, bf16[2048,512]{1,0:T(8,128)(2,1)} %get-tuple-element.130, bf16[2048,512]{1,0:T(8,128)(2,1)} %get-tuple-element.131, ...), kind=kOutput, calls=%fused_computation.79 | convolution fusion | flops 17221812224 | bytes 50331648 | tf_op jit(solution)/shard_map/dot_general | solution.py:46
  569.3 28.2 %fusion.58 = f32[2048,2048]{1,0:T(8,128)} fusion(bf16[2048,2048]{1,0:T(8,128)(2,1)} %bitcast.154, bf16[2048,512]{1,0:T(8,128)(2,1)} %get-tuple-element.125, bf16[2048,512]{1,0:T(8,128)(2,1)} %get-tuple-element.126, bf16[2048,512]{1,0:T(8,128)(2,1)} %get-tuple-element.127, bf16[2048,512]{1,0:T(8,128)(2,1)} %get-tuple-element.124), kind=kOutput, calls=%fused_computation.100 | convolution fusion | flops 17213423616 | bytes 33554432 | tf_op jit(solution)/shard_map/dot_general | solution.py:46
  604.5 64.8 %fusion.4 = bf16[2048,4096]{1,0:T(8,128)(2,1)} fusion(bf16[2048,4096]{1,0:T(8,128)(2,1)} %get-tuple-element.179, bf16[2048,2048]{1,0:T(8,128)(2,1)} %bitcast.155, bf16[2,4096,2048]{2,1,0:T(8,128)(2,1)} %all-gather.13.cloned.1.call-done), kind=kOutput, calls=%fused_computation.16 | convolution fusion | flops 34552676352 | bytes 58720256 | tf_op jit(solution)/shard_map/dot_general | solution.py:42
  677.8 27.0 %add_multiply_fusion.2 = f32[2048,2048]{1,0:T(8,128)} fusion(f32[2048,2048]{1,0:T(8,128)} %collective-permute-done.1, bf16[2048,2048]{1,0:T(8,128)(2,1)S(1)} %bitcast.160, bf16[2048,512]{1,0:T(8,128)(2,1)} %get-tuple-element.121, bf16[2048,512]{1,0:T(8,128)(2,1)} %get-tuple-element.122, bf16[2048,512]{1,0:T(8,128)(2,1)} %get-tuple-element.123, ...), kind=kOutput, calls=%fused_computation.78 | convolution fusion | flops 17221812224 | bytes 50331648 | tf_op jit(solution)/shard_map/dot_general | solution.py:46
  728.8 65.0 %fusion.7 = bf16[2048,4096]{1,0:T(8,128)(2,1)} fusion(bf16[2048,4096]{1,0:T(8,128)(2,1)} %get-tuple-element.181, bf16[2048,2048]{1,0:T(8,128)(2,1)} %bitcast.156, bf16[2,4096,2048]{2,1,0:T(8,128)(2,1)} %all-gather.13.cloned.1.call-done), kind=kOutput, calls=%fused_computation.19 | convolution fusion | flops 34552676352 | bytes 58720256 | tf_op jit(solution)/shard_map/dot_general | solution.py:42
  793.8 24.4 %add_multiply_fusion.1 = f32[1024,4096]{1,0:T(8,128)} fusion(f32[1024,4096]{1,0:T(8,128)} %collective-permute-done.2, bf16[2048,4096]{1,0:T(8,128)(2,1)} %fusion.4, bf16[2048,256]{1,0:T(8,128)(2,1)S(1)} %copy-done.26, bf16[2048,256]{1,0:T(8,128)(2,1)S(1)} %copy-done.27, bf16[2048,256]{1,0:T(8,128)(2,1)} %get-tuple-element.155, ...), kind=kOutput, calls=%fused_computation.77 | convolution fusion | flops 17205035008 | bytes 54525952 | tf_op jit(solution)/shard_map/dot_general | solution.py:46
  818.3 23.9 %fusion.107 = f32[1024,4096]{1,0:T(8,128)} fusion(bf16[2048,4096]{1,0:T(8,128)(2,1)} %fusion.7, bf16[2048,256]{1,0:T(8,128)(2,1)} %get-tuple-element.156, bf16[2048,256]{1,0:T(8,128)(2,1)} %get-tuple-element.157, bf16[2048,256]{1,0:T(8,128)(2,1)} %get-tuple-element.158, bf16[2048,256]{1,0:T(8,128)(2,1)} %get-tuple-element.159), kind=kOutput, calls=%fused_computation.172 | convolution fusion | flops 17196646400 | bytes 37748736 | tf_op jit(solution)/shard_map/dot_general | solution.py:46
  845.6 43.3 %fusion.42 = f32[2048,2048]{1,0:T(8,128)} fusion(bf16[2048,4096]{1,0:T(8,128)(2,1)} %fusion.4, bf16[2,2048,4096]{2,1,0:T(8,128)(2,1)} %all-gather.11.cloned.1.call-done), kind=kOutput, calls=%fused_computation.82 | convolution fusion | flops 34359738368 | bytes 50331648 | tf_op jit(solution)/shard_map/dot_general | solution.py:42
  888.9 24.4 %add_multiply_fusion = f32[1024,4096]{1,0:T(8,128)} fusion(f32[1024,4096]{1,0:T(8,128)} %collective-permute-done.3, bf16[2048,4096]{1,0:T(8,128)(2,1)} %fusion.7, bf16[2048,256]{1,0:T(8,128)(2,1)S(1)} %copy-done.26, bf16[2048,256]{1,0:T(8,128)(2,1)S(1)} %copy-done.27, bf16[2048,256]{1,0:T(8,128)(2,1)} %get-tuple-element.155, ...), kind=kOutput, calls=%fused_computation.76 | convolution fusion | flops 17205035008 | bytes 54525952 | tf_op jit(solution)/shard_map/dot_general | solution.py:46
  913.4 53.0 %fusion.28 = (f32[2048]{0:T(1024)}, f32[2048]{0:T(1024)S(1)}, bf16[2048,2048]{1,0:T(8,128)(2,1)}) fusion(bf16[2048,2048]{1,0:T(8,128)(2,1)} %get-tuple-element.177, f32[2048]{0:T(1024)S(1)} %copy-done.34, f32[2048]{0:T(1024)S(1)} %bitcast.180, f32[2048,2048]{1,0:T(8,128)} %fusion.42, bf16[2048,4096]{1,0:T(8,128)(2,1)} %fusion.7, ...), kind=kOutput, calls=%fused_computation.52 | convolution fusion | flops 34401681408 | bytes 67141632 | tf_op jit(solution)/shard_map/dot_general | solution.py:42
  975.4 23.7 %convolution_convert_fusion.3 = bf16[2048,2048]{1,0:T(8,128)(2,1)} fusion(bf16[2048,2048]{1,0:T(8,128)(2,1)S(1)} %fusion.31, bf16[2048,2048]{1,0:T(8,128)(2,1)} %bitcast.149), kind=kOutput, calls=%fused_computation.124 | convolution fusion | flops 17184063488 | bytes 25165824 | tf_op jit(solution)/shard_map/dot_general | solution.py:42
  999.1 59.4 %attn_bwd.2 = (bf16[4,512,3072]{2,1,0:T(8,128)(2,1)}, f32[4,512,256]{2,1,0:T(8,128)}, f32[4,8,256]{2,1,0:T(8,128)}, f32[4,8,256]{2,1,0:T(8,128)}) custom-call(bf16[4,512,6144]{2,1,0:T(8,128)(2,1)} %bitcast.191, bf16[8,320,2048]{2,1,0:T(8,128)(2,1)} %bitcast.164, f32[8,1,256]{2,1,0:T(1,128)} %get-tuple-element.172.u_ref, ...), custom_call_target="tpu_custom_call" | custom-call | flops 21474836480 | bytes 29360128 | tf_op jit(solution)/shard_map/attn_bwd/pallas_call | solution.py:237
  1118.2 59.3 %attn_bwd.3 = (bf16[4,512,3072]{2,1,0:T(8,128)(2,1)}, f32[4,512,256]{2,1,0:T(8,128)}, f32[4,8,256]{2,1,0:T(8,128)}, f32[4,8,256]{2,1,0:T(8,128)}) custom-call(bf16[4,512,6144]{2,1,0:T(8,128)(2,1)} %bitcast.192, bf16[8,320,2048]{2,1,0:T(8,128)(2,1)} %bitcast.165, f32[8,1,256]{2,1,0:T(1,128)} %get-tuple-element.172.u_ref, ...), custom_call_target="tpu_custom_call" | custom-call | flops 21474836480 | bytes 29360128 | tf_op jit(solution)/shard_map/attn_bwd/pallas_call | solution.py:237
  1203.1 30.9 %collective-permute-done.5 = f32[1024,2048]{1,0:T(8,128)S(1)} collective-permute-done((f32[1024,2048]{1,0:T(8,128)}, f32[1024,2048]{1,0:T(8,128)S(1)}, u32[]{:S(2)}, u32[]{:S(2)}) %collective-permute-start.5) | collective-permute-done | bytes 8388640 | tf_op jit(solution)/shard_map/ppermute | solution.py:320
  1269.9 43.6 %fusion.44 = f32[2048,2048]{1,0:T(8,128)} fusion(bf16[2048,4096]{1,0:T(8,128)(2,1)} %get-tuple-element.67, bf16[2,4096,2048]{2,1,0:T(8,128)(2,1)} %all-gather.13.cloned.1.call-done), kind=kOutput, calls=%fused_computation.84 | convolution fusion | flops 34359738368 | bytes 50331648 | tf_op jit(solution)/shard_map/dot_general | solution.py:38
  1313.4 49.5 %fusion.37 = bf16[2048,2048]{1,0:T(8,128)(2,1)} fusion(f32[2048,2048]{1,0:T(8,128)} %fusion.44, bf16[2048,2048]{1,0:T(8,128)(2,1)} %get-tuple-element.177, bf16[2,4096,2048]{2,1,0:T(8,128)(2,1)} %all-gather.13.cloned.1.call-done, bf16[2048,4096]{1,0:T(8,128)(2,1)} %get-tuple-element.181), kind=kOutput, calls=%fused_computation.61 | convolution fusion | flops 34460401664 | bytes 67108864 | tf_op jit(solution)/shard_map/dot_general | solution.py:38
  1375.7 151.2 %reduce-scatter.23.cloned.1.call-done = f32[512,2048]{1,0:T(8,128)} async-done(((f32[2048,2048]{1,0:T(8,128)}), f32[512,2048]{1,0:T(8,128)}) %reduce-scatter.23.cloned.1.call-update) | async-done | bytes 4194320 | tf_op jit(solution)/shard_map/reduce_scatter | solution.py:326
  1536.1 34.8 %fusion.46 = f32[2048,2048]{1,0:T(8,128)} fusion(bf16[2048,3072]{1,0:T(8,128)(2,1)} %bitcast.198, bf16[2048,6144]{1,0:T(8,128)(2,1)} %all-gather.9.cloned.1.call-done), kind=kOutput, calls=%fused_computation.86 | convolution fusion | flops 25769803776 | bytes 41943040 | tf_op jit(solution)/shard_map/dot_general | solution.py:42
  1570.9 43.0 %fusion.29 = (f32[2048]{0:T(1024)S(1)}, f32[2048]{0:T(1024)S(1)}, bf16[2048,2048]{1,0:T(8,128)(2,1)}) fusion(bf16[4,512,2048]{2,1,0:T(8,128)(2,1)} %param.13, f32[2048]{0:T(1024)S(1)} %copy-done.32, f32[2048]{0:T(1024)S(1)} %bitcast.177, f32[2048,2048]{1,0:T(8,128)} %fusion.46, bf16[2048,3072]{1,0:T(8,128)(2,1)} %bitcast.195, ...), kind=kOutput, calls=%fused_computation.53 | convolution fusion | flops 25811742720 | bytes 58753024 | tf_op jit(solution)/shard_map/dot_general | solution.py:42
  1614.0 23.9 %all-reduce = f32[8,4,256]{2,1,0:T(4,128)S(1)} all-reduce(f32[8,4,256]{2,1,0:T(4,128)S(1)} %maximum_multiply_fusion), channel_id=5, replica_groups=mesh['fsdp'=8] {'fsdp'}, use_global_device_ids=true, to_apply=%region_9.0.clone | all-reduce | flops 8192 | bytes 65536
  1657.7 46.4 %reduce-scatter.17.cloned.1.call-done.refs_0_ = f32[256,4096]{1,0:T(8,128)} async-done(((f32[1024,4096]{1,0:T(8,128)}), f32[256,4096]{1,0:T(8,128)}) %reduce-scatter.17.cloned.1.call-update) | async-done | bytes 4194320 | tf_op jit(solution)/shard_map/reduce_scatter | solution.py:326
  1704.1 151.1 %reduce-scatter.19.cloned.1.call-done.refs_1_ = f32[256,4096]{1,0:T(8,128)} async-done(((f32[1024,4096]{1,0:T(8,128)}), f32[256,4096]{1,0:T(8,128)}) %reduce-scatter.19.cloned.1.call-update) | async-done | bytes 4194320 | tf_op jit(solution)/shard_map/reduce_scatter | solution.py:326
  1864.4 108.9 %reduce-scatter.11.cloned.1.call-done = f32[256,3072]{1,0:T(8,128)} async-done(((f32[1024,3072]{1,0:T(8,128)}), f32[256,3072]{1,0:T(8,128)}) %reduce-scatter.11.cloned.1.call-update) | async-done | bytes 3145744 | tf_op jit(solution)/shard_map/reduce_scatter | solution.py:326
  1977.4 113.8 %reduce-scatter.13.cloned.1.call-done = f32[256,3072]{1,0:T(8,128)} async-done(((f32[1024,3072]{1,0:T(8,128)}), f32[256,3072]{1,0:T(8,128)}) %reduce-scatter.13.cloned.1.call-update) | async-done | bytes 3145744 | tf_op jit(solution)/shard_map/reduce_scatter | solution.py:326
  2106.0 69.7 %reduce-scatter.15.cloned.1.call-done = f32[256,2048]{1,0:T(8,128)} async-done(((f32[1024,2048]{1,0:T(8,128)}), f32[256,2048]{1,0:T(8,128)}) %reduce-scatter.15.cloned.1.call-update) | async-done | bytes 2097168 | tf_op jit(solution)/shard_map/reduce_scatter | solution.py:326
  (235 shorter events, 380.5 us)
Async XLA Ops:
  20.9 19.6 all-to-all-start
  25.1 76.9 %all-gather.17.cloned.1.call-start = ((), (), s32[]{:S(2)}) async-start(), calls=%async_computation.21 | async-start | bytes 11796480 | tf_op jit(solution)/shard_map/all_gather | solution.py:349
  45.1 178.9 %all-gather.9.cloned.1.call-start = ((), (), s32[]{:S(2)}) async-start(), calls=%async_computation.9 | async-start | bytes 28311552 | tf_op jit(solution)/shard_map/all_gather | solution.py:301
  46.0 340.4 %all-gather.11.cloned.1.call-start = ((), (), s32[]{:S(2)}) async-start(), calls=%async_computation.10 | async-start | bytes 37748736 | tf_op jit(solution)/shard_map/all_gather | solution.py:329
  53.0 551.5 %all-gather.13.cloned.1.call-start = ((), (), s32[]{:S(2)}) async-start(), calls=%async_computation.11 | async-start | bytes 37748736 | tf_op jit(solution)/shard_map/all_gather | solution.py:329
  53.5 1309.4 %reduce-scatter.9.cloned.1.call-start = ((), (), s32[]{:S(2)}) async-start(), calls=%async_computation.12 | async-start | bytes 4718592 | tf_op jit(solution)/shard_map/reduce_scatter | solution.py:403
  476.3 65.9 %collective-permute-start = (f32[2048,2048]{1,0:T(8,128)}, f32[2048,2048]{1,0:T(8,128)}, u32[]{:S(2)}, u32[]{:S(2)}) collective-permute-start(f32[2048,2048]{1,0:T(8,128)} %fusion.50), channel_id=1, source_target_pairs={{0,1},{1,0},{2,3},{3,2},{4,5},{5,4},{6,7},{7,6}} | collective-permute-start | bytes 50331656 | tf_op jit(solution)/shard_map/ppermute | solution.py:320
  597.6 79.6 %collective-permute-start.1 = (f32[2048,2048]{1,0:T(8,128)}, f32[2048,2048]{1,0:T(8,128)}, u32[]{:S(2)}, u32[]{:S(2)}) collective-permute-start(f32[2048,2048]{1,0:T(8,128)} %fusion.58), channel_id=1, source_target_pairs={{0,1},{1,0},{2,3},{3,2},{4,5},{5,4},{6,7},{7,6}} | collective-permute-start | bytes 50331656 | tf_op jit(solution)/shard_map/ppermute | solution.py:320
  728.3 65.5 %collective-permute-start.2 = (f32[1024,4096]{1,0:T(8,128)}, f32[1024,4096]{1,0:T(8,128)}, u32[]{:S(2)}, u32[]{:S(2)}) collective-permute-start(f32[1024,4096]{1,0:T(8,128)} %fusion.108), channel_id=1, source_target_pairs={{0,1},{1,0},{2,3},{3,2},{4,5},{5,4},{6,7},{7,6}} | collective-permute-start | bytes 50331656 | tf_op jit(solution)/shard_map/ppermute | solution.py:320
  728.8 65.0 %copy-start.25 = (bf16[2048,256]{1,0:T(8,128)(2,1)S(1)}, bf16[2048,256]{1,0:T(8,128)(2,1)}, u32[]{:S(2)}) copy-start(bf16[2048,256]{1,0:T(8,128)(2,1)} %get-tuple-element.152) | copy-start | bytes 3145732
  728.8 65.0 %copy-start.26 = (bf16[2048,256]{1,0:T(8,128)(2,1)S(1)}, bf16[2048,256]{1,0:T(8,128)(2,1)}, u32[]{:S(2)}) copy-start(bf16[2048,256]{1,0:T(8,128)(2,1)} %get-tuple-element.153) | copy-start | bytes 3145732
  728.8 65.0 %copy-start.27 = (bf16[2048,256]{1,0:T(8,128)(2,1)S(1)}, bf16[2048,256]{1,0:T(8,128)(2,1)}, u32[]{:S(2)}) copy-start(bf16[2048,256]{1,0:T(8,128)(2,1)} %get-tuple-element.154) | copy-start | bytes 3145732
  842.1 46.8 %collective-permute-start.3 = (f32[1024,4096]{1,0:T(8,128)}, f32[1024,4096]{1,0:T(8,128)}, u32[]{:S(2)}, u32[]{:S(2)}) collective-permute-start(f32[1024,4096]{1,0:T(8,128)} %fusion.107), channel_id=1, source_target_pairs={{0,1},{1,0},{2,3},{3,2},{4,5},{5,4},{6,7},{7,6}} | collective-permute-start | bytes 50331656 | tf_op jit(solution)/shard_map/ppermute | solution.py:320
  999.1 59.4 %copy-start.16 = (bf16[2048,256]{1,0:T(8,128)(2,1)S(1)}, bf16[2048,256]{1,0:T(8,128)(2,1)}, u32[]{:S(2)}) copy-start(bf16[2048,256]{1,0:T(8,128)(2,1)} %get-tuple-element.145) | copy-start | bytes 3145732
  999.1 59.4 %copy-start.18 = (bf16[2048,256]{1,0:T(8,128)(2,1)S(1)}, bf16[2048,256]{1,0:T(8,128)(2,1)}, u32[]{:S(2)}) copy-start(bf16[2048,256]{1,0:T(8,128)(2,1)} %get-tuple-element.146) | copy-start | bytes 3145732
  999.1 59.4 %copy-start.20 = (bf16[2048,256]{1,0:T(8,128)(2,1)S(1)}, bf16[2048,256]{1,0:T(8,128)(2,1)}, u32[]{:S(2)}) copy-start(bf16[2048,256]{1,0:T(8,128)(2,1)} %get-tuple-element.147) | copy-start | bytes 3145732
  1076.9 20.1 collective-permute-start.4
  1181.4 194.2 %reduce-scatter.21.cloned.1.call-start = ((), (), s32[]{:S(2)}) async-start(), calls=%async_computation.19 | async-start | bytes 20971520 | tf_op jit(solution)/shard_map/reduce_scatter | solution.py:326
  1182.0 344.8 %reduce-scatter.23.cloned.1.call-start = ((), (), s32[]{:S(2)}) async-start(), calls=%async_computation.20 | async-start | bytes 20971520 | tf_op jit(solution)/shard_map/reduce_scatter | solution.py:326
  1182.8 469.5 %all-gather.15.cloned.1.call-start = ((), (), s32[]{:S(2)}) async-start(), calls=%async_computation.15 | async-start | bytes 2359296 | tf_op jit(solution)/shard_map/all_gather | solution.py:412
  1202.6 45.3 %collective-permute-start.6 = (f32[1024,3072]{1,0:T(8,128)}, f32[1024,3072]{1,0:T(8,128)}, u32[]{:S(2)}, u32[]{:S(2)}) collective-permute-start(f32[1024,3072]{1,0:T(8,128)} %fusion.105), channel_id=1, source_target_pairs={{0,1},{1,0},{2,3},{3,2},{4,5},{5,4},{6,7},{7,6}} | collective-permute-start | bytes 37748744 | tf_op jit(solution)/shard_map/ppermute | solution.py:320
  1203.1 31.0 %collective-permute-start.5 = (f32[1024,2048]{1,0:T(8,128)}, f32[1024,2048]{1,0:T(8,128)S(1)}, u32[]{:S(2)}, u32[]{:S(2)}) collective-permute-start(f32[1024,2048]{1,0:T(8,128)} %fusion.82), channel_id=1, source_target_pairs={{0,1},{1,0},{2,3},{3,2},{4,5},{5,4},{6,7},{7,6}} | collective-permute-start | bytes 25165832 | tf_op jit(solution)/shard_map/ppermute | solution.py:320
  1367.6 336.5 %reduce-scatter.17.cloned.1.call-start = ((), (), s32[]{:S(2)}) async-start(), calls=%async_computation.17 | async-start | bytes 20971520 | tf_op jit(solution)/shard_map/reduce_scatter | solution.py:326
  1368.4 486.8 %reduce-scatter.19.cloned.1.call-start = ((), (), s32[]{:S(2)}) async-start(), calls=%async_computation.18 | async-start | bytes 20971520 | tf_op jit(solution)/shard_map/reduce_scatter | solution.py:326
  1368.9 604.4 %reduce-scatter.11.cloned.1.call-start = ((), (), s32[]{:S(2)}) async-start(), calls=%async_computation.13 | async-start | bytes 15728640 | tf_op jit(solution)/shard_map/reduce_scatter | solution.py:326
  1369.7 721.6 %reduce-scatter.13.cloned.1.call-start = ((), (), s32[]{:S(2)}) async-start(), calls=%async_computation.14 | async-start | bytes 15728640 | tf_op jit(solution)/shard_map/reduce_scatter | solution.py:326
  1370.3 805.4 %reduce-scatter.15.cloned.1.call-start = ((), (), s32[]{:S(2)}) async-start(), calls=%async_computation.16 | async-start | bytes 10485760 | tf_op jit(solution)/shard_map/reduce_scatter | solution.py:326
  1370.3 164.5 %copy-start.44 = (f32[4,8,256]{2,1,0:T(8,128)S(1)}, f32[4,8,256]{2,1,0:T(8,128)}, u32[]{:S(2)}) copy-start(f32[4,8,256]{2,1,0:T(8,128)} %get-tuple-element.74) | copy-start | bytes 98308
  1370.3 164.5 %copy-start.46 = (f32[4,8,256]{2,1,0:T(8,128)S(1)}, f32[4,8,256]{2,1,0:T(8,128)}, u32[]{:S(2)}) copy-start(f32[4,8,256]{2,1,0:T(8,128)} %get-tuple-element.75) | copy-start | bytes 98308
  1370.3 165.1 %copy-start.43 = (f32[4,8,256]{2,1,0:T(8,128)S(1)}, f32[4,8,256]{2,1,0:T(8,128)}, u32[]{:S(2)}) copy-start(f32[4,8,256]{2,1,0:T(8,128)} %get-tuple-element.72) | copy-start | bytes 98308
  1370.3 165.1 %copy-start.45 = (f32[4,8,256]{2,1,0:T(8,128)S(1)}, f32[4,8,256]{2,1,0:T(8,128)}, u32[]{:S(2)}) copy-start(f32[4,8,256]{2,1,0:T(8,128)} %get-tuple-element.73) | copy-start | bytes 98308
  1570.9 67.5 %copy-start.40 = (f32[1,4,4,128]{3,1,2,0:T(4,128)S(1)}, f32[1,4,4,128]{3,1,2,0:T(4,128)}, u32[]{:S(2)}) copy-start(f32[1,4,4,128]{3,1,2,0:T(4,128)} %copy-done.39) | copy-start | bytes 24580
  (45 other events, 968.4 us)
Sparse Core Ops, SparseCore 0:
  45.3 56.7 all-gather.16
  104.4 119.6 all-gather.8
  225.9 155.0 all-gather.10
  382.7 155.0 all-gather.12
  1181.6 43.0 reduce-scatter.8
  1227.5 148.1 reduce-scatter.20
  1378.7 148.1 reduce-scatter.22
  1529.2 22.2 all-gather.14
  1554.5 149.5 reduce-scatter.16
  1707.0 148.1 reduce-scatter.18
  1858.2 115.0 reduce-scatter.10
  1976.2 115.0 reduce-scatter.12
  2094.9 80.7 reduce-scatter.14

commit v3 on v2

--- a/solution.py
+++ b/solution.py
@@ -256,14 +256,13 @@
         out_ref[..., n * width:(n + 1) * width] = ref[...]
 
 
-def interleave(arrays, width):
+def interleave(arrays, width, place=lambda i: i):
     rows, cols = arrays[0].shape
-    spec = pl.BlockSpec((rows, width), lambda i: (0, i))
     total = len(arrays) * cols
     return pl.pallas_call(
         interleave_kernel,
         grid=(cols // width,),
-        in_specs=[spec] * len(arrays),
+        in_specs=[pl.BlockSpec((rows, width), lambda i: (0, place(i)))] * len(arrays),
         out_specs=pl.BlockSpec((rows, len(arrays) * width), lambda i: (0, i)),
         out_shape=jax.ShapeDtypeStruct((rows, total), arrays[0].dtype),
         cost_estimate=pl.CostEstimate(flops=rows * total, bytes_accessed=4 * rows * total, transcendentals=0),
@@ -277,17 +276,84 @@
         out_ref[n] = in_ref[:, n * width:(n + 1) * width]
 
 
-def separate(array, count, width):
+def separate(array, count, width, place=lambda i: i):
     rows, cols = array.shape
     return pl.pallas_call(
         separate_kernel,
         grid=(cols // (count * width),),
         in_specs=[pl.BlockSpec((rows, count * width), lambda i: (0, i))],
-        out_specs=pl.BlockSpec((count, rows, width), lambda i: (0, 0, i)),
+        out_specs=pl.BlockSpec((count, rows, width), lambda i: (0, 0, place(i))),
         out_shape=jax.ShapeDtypeStruct((count, rows, cols // count), array.dtype),
         cost_estimate=pl.CostEstimate(flops=rows * cols, bytes_accessed=4 * rows * cols, transcendentals=0),
         name="separate",
     )(array)
+
+
+def heads_kernel(low_ref, high_ref, *out_refs, span, head_dim):
+    rows = low_ref.shape[0]
+    per = span // head_dim
+    count = low_ref.shape[1] // (len(out_refs) * span)
+    heads = 2 * count * per
+    for half, ref in enumerate((low_ref, high_ref)):
+        for pair in range(count):
+            for part, out_ref in enumerate(out_refs):
+                for n in range(per):
+                    at = (pair * len(out_refs) + part) * span + n * head_dim
+                    head = (half * count + pair) * per + n
+                    out_ref[pl.ds(head, rows, stride=heads), :] = ref[:, at:at + head_dim]
+
+
+def to_heads(low, high, span, head_dim):
+    rows, cols = low.shape
+    heads = 2 * cols // (3 * head_dim)
+    step = rows // 4
+    return pl.pallas_call(
+        functools.partial(heads_kernel, span=span, head_dim=head_dim),
+        grid=(4,),
+        in_specs=[pl.BlockSpec((step, cols), lambda i: (i, 0))] * 2,
+        out_specs=[pl.BlockSpec((step * heads, head_dim), lambda i: (i, 0))] * 3,
+        out_shape=[jax.ShapeDtypeStruct((rows * heads, head_dim), F32)] * 3,
+        cost_estimate=pl.CostEstimate(flops=2 * rows * cols, bytes_accessed=16 * rows * cols, transcendentals=0),
+        name="to_heads",
+    )(low, high)
+
+
+def wgrad_kernel(kind_ref, *refs, chips, scale):
+    del kind_ref
+    a_refs, (a2_ref, b1_ref, b2_ref, out_ref, t1, t2) = refs[:chips], refs[chips:]
+
+    @pl.when(pl.program_id(0) == 0)
+    def _():
+        part = a_refs[0].shape[1]
+        for c, ref in enumerate(a_refs):
+            t1[c * part:(c + 1) * part] = ref[...].T
+            t2[c * part:(c + 1) * part] = a2_ref[:, c * part:(c + 1) * part].T
+
+    out_ref[...] = (dot_nn(t1[...], b1_ref[...]) + dot_nn(t2[...], b2_ref[...])) * scale
+
+
+def wgrad(kind, acts, acts2, cots, cots2, chips, scale, width):
+    tokens, cols = acts.shape
+    part = cols // (2 * chips)
+    rows, total = chips * part, cots.shape[1]
+    share = [pl.BlockSpec((tokens, part), lambda j, k, c=c: (0, 2 * c + k[0])) for c in range(chips)]
+    whole = pl.BlockSpec((tokens, rows), lambda j, k: (0, 0))
+    block = pl.BlockSpec((tokens, width), lambda j, k: (0, j))
+    return pl.pallas_call(
+        functools.partial(wgrad_kernel, chips=chips, scale=scale),
+        grid_spec=pltpu.PrefetchScalarGridSpec(
+            num_scalar_prefetch=1,
+            grid=(total // width,),
+            in_specs=share + [whole, block, block],
+            out_specs=pl.BlockSpec((rows, width), lambda j, k: (0, j)),
+            scratch_shapes=[pltpu.VMEM((rows, tokens), BF16)] * 2,
+        ),
+        out_shape=jax.ShapeDtypeStruct((rows, total), F32),
+        compiler_params=pltpu.CompilerParams(dimension_semantics=("arbitrary",), vmem_limit_bytes=56 * 2**20),
+        cost_estimate=pl.CostEstimate(
+            flops=4 * tokens * rows * total, bytes_accessed=4 * (tokens * total + rows * total), transcendentals=0),
+        name="wgrad",
+    )(kind, *([acts] * chips), acts2, cots, cots2)
 
 
 def solution(mesh):
@@ -315,19 +381,29 @@
             return jnp.concatenate(
                 [lax.dynamic_slice(acts, (0, (2 * c + kind) * part), (tokens, part)) for c in range(chips)], axis=1)
 
-        def theirs(acts, cots):
-            mine = dot_tn(shares(acts, 1 - core), cots)
-            return mine, lax.ppermute(mine, axis_name, pairs)
-
-        def ours(acts, cots, received):
-            return (dot_tn(shares(acts, core), cots) + received) * scale
+        def block_of(acts, kind):
+            half = acts.shape[1] // 2
+            return lax.dynamic_slice(acts, (0, kind * half), (tokens, half))
+
+        def swap(value):
+            return lax.ppermute(value, axis_name, pairs)
+
+        def theirs(acts, cots, pick=shares):
+            mine = dot_tn(pick(acts, 1 - core), cots)
+            return mine, swap(mine)
+
+        def ours(acts, cots, received, pick=shares):
+            return (dot_tn(pick(acts, core), cots) + received) * scale
 
         def spread(summed):
             return lax.psum_scatter(summed, axis_name, scatter_dimension=0, axis_index_groups=same_core, tiled=True)
 
-        def gather_halves(stacked):
-            full = lax.all_gather(stacked, axis_name, axis=1, tiled=True)
+        def gather_halves(stacked, groups=None):
+            full = lax.all_gather(stacked, axis_name, axis=1, tiled=True, axis_index_groups=groups)
             return with_layout_constraint(full, Layout(major_to_minor=(0, 1, 2)))
+
+        def by_kind(device):
+            return lax.rem(device, 2) * chips + lax.div(device, 2)
 
         x_f32 = x_in.reshape(tokens, width).astype(F32)
         dy = grad_out.reshape(tokens, width)
@@ -340,8 +416,12 @@
         qkv_own = interleave([z.reshape(-1, hidden) for z in (w_query, w_key, w_value)], span)
         qkv_full = gather(qkv_own)
 
+        ff_half = w_up.shape[1] // 2
+        part = ff_half // group_size
+        up_own = separate(after(w_up, qkv_own), 2, part, by_kind)
+
         pos_table = sin_table(seq_len, width)
-        rel_rows = after(w_rel, qkv_own).reshape(-1, hidden)
+        rel_rows = after(w_rel, up_own).reshape(-1, hidden)
         rel_cols = lax.all_to_all(rel_rows, axis_name, split_axis=1, concat_axis=0, tiled=True)
         rel_own = dot_nn(pos_table, rel_cols).astype(BF16)
         lines = seq_len * span // width
@@ -349,11 +429,8 @@
         out_rel = lax.all_gather(jnp.concatenate([w_attn_out, folded], axis=0), axis_name, axis=0)
         out_full = out_rel[:, :-lines].reshape(hidden, width)
 
-        ff_half = w_up.shape[1] // 2
-        part = ff_half // group_size
-        up_own = separate(after(w_up, qkv_own), 2, part)
         up_full = gather_halves(up_own)
-        down_full = gather_halves(after(w_down, up_own).reshape(2, part, width))
+        down_full = gather_halves(after(w_down, up_own).reshape(2, part, width), [same_core[0] + same_core[1]])
 
         h_attn = rms_norm(x_f32, gain_attn)
         shape3 = (batch_local, seq_len, -1)
@@ -371,18 +448,20 @@
             return jax.vjp(gelu_tanh, pre.astype(F32))[1](d_act.astype(F32))[0].astype(BF16)
 
         pre0, act0 = feed(h_mlp, up_full[0])
-        sent, got = theirs(act0, dy)
+        sent, got = theirs(act0, dy, block_of)
+        hidden_theirs = swap(shares(h_mlp, 1 - core))
         pre1, act1 = feed(after(h_mlp, sent), up_full[1])
-        sum_down0 = ours(after(act0, act1), dy, got)
-        sent, got = theirs(act1, after(dy, sum_down0))
+        sum_down0 = ours(after(act0, act1), dy, got, block_of)
+        sent, got = theirs(act1, after(dy, sum_down0), block_of)
         d_pre0 = unfeed(after(dy, sent), down_full[0], pre0)
-        sum_down1 = ours(after(act1, d_pre0), dy, got)
-        sent, got = theirs(h_mlp, after(d_pre0, sum_down1))
-        d_pre1 = unfeed(after(dy, sent), down_full[1], pre1)
-        sum_up0 = ours(h_mlp, after(d_pre0, d_pre1), got)
-        sent, got = theirs(h_mlp, after(d_pre1, sum_up0))
-        d_h_part = dot_nt(after(d_pre0, sent), up_full[0])
-        sum_up1 = ours(h_mlp, after(d_pre1, d_h_part), got)
+        d_pre0_theirs = swap(d_pre0)
+        sum_down1 = ours(after(act1, d_pre0), dy, got, block_of)
+        d_pre1 = unfeed(after(dy, sum_down1), down_full[1], pre1)
+        d_pre1_theirs = swap(d_pre1)
+        kind = core[None]
+        sum_up0 = wgrad(kind, h_mlp, hidden_theirs, after(d_pre0, d_pre1), d_pre0_theirs, chips, scale, 512)
+        d_h_part = dot_nt(after(d_pre0, sum_up0), up_full[0])
+        sum_up1 = wgrad(kind, h_mlp, hidden_theirs, after(d_pre1, d_h_part), d_pre1_theirs, chips, scale, 512)
         d_h_mlp = (d_h_part + dot_nt(after(d_pre1, sum_up1), up_full[1])).astype(BF16)
         grad_down = jnp.concatenate([spread(sum_down0), spread(sum_down1)], axis=0)
         grad_up0, grad_up1 = spread(sum_up0), spread(sum_up1)
@@ -400,29 +479,34 @@
         d_high, d_rel_high, d_u_high, d_w_high = attn_bwd(
             qkv, out_rel, u_full, w_full, after(d_context, sum_low), head_dim, pairs_half, pairs_half)
         d_high = d_high.reshape(tokens, -1)
-        d_rel_own = lax.psum_scatter(
-            jnp.concatenate([d_rel_low, d_rel_high], axis=0), axis_name, scatter_dimension=0, tiled=True)[0]
+        d_rel = jnp.concatenate([d_rel_low, d_rel_high], axis=0).reshape(chips, 2, seq_len, span)
+        got_rel = swap(lax.dynamic_index_in_dim(d_rel, 1 - core, 1, keepdims=False))
         sent, got = theirs(h_attn, d_high)
         sum_o = ours(context, after(d_x1, sent), got_o)
-        sum_high = ours(h_attn, after(d_high, sum_o), got)
+        d_rel = lax.dynamic_index_in_dim(d_rel, core, 1, keepdims=False) + got_rel
+        d_rel = jnp.concatenate([d_rel[:, at:at + lines] for at in range(0, seq_len, lines)], axis=2)
+        sum_o_rel = jnp.concatenate([sum_o.reshape(chips, -1, width), d_rel], axis=1).reshape(-1, width)
+        grad_o_rel = spread(sum_o_rel)
+        sum_high = ours(h_attn, after(d_high, sum_o_rel), got)
         grad_low, grad_high = spread(sum_low), spread(sum_high)
         y_out = (x1_f32 + dot_nn(after(act0, sum_high), down_full[0]) + dot_nn(act1, down_full[1])).astype(BF16)
-        d_rel_own = after(d_rel_own, y_out)
-        d_rel_own = jnp.flip(d_rel_own.reshape(seq_len // BLK, BLK, span), axis=1).reshape(seq_len, span).astype(BF16)
-        d_rel_all = lax.all_gather(d_rel_own, axis_name, axis=0)
-        grad_attn_out = spread(after(sum_o, d_rel_own))
 
         cut = qkv_full.shape[1] // 2
-        d_h_attn = (dot_nt(after(d_low, d_rel_own), qkv_full[:, :cut]) + dot_nt(d_high, qkv_full[:, cut:])).astype(BF16)
+        d_h_attn = (dot_nt(after(d_low, y_out), qkv_full[:, :cut]) + dot_nt(d_high, qkv_full[:, cut:])).astype(BF16)
         d_x_norm, grad_norm_attn = jax.vjp(rms_norm, x_f32, gain_attn)[1](d_h_attn)
         grad_x = (d_x1.astype(F32) + d_x_norm).astype(BF16)
 
+        grad_o_rel = after(grad_o_rel, d_h_attn)
+        grad_attn_out = grad_o_rel[:-lines]
+        d_rel_own = jnp.concatenate(
+            [grad_o_rel[-lines:, at:at + span] for at in range(0, width, span)], axis=0).reshape(seq_len // BLK, BLK, span)
+        d_rel_own = jnp.flip(d_rel_own, axis=1).reshape(1, seq_len, span).astype(BF16)
+        d_rel_all = lax.all_to_all(
+            jnp.broadcast_to(d_rel_own, (group_size, seq_len, span)), axis_name, split_axis=0, concat_axis=0, tiled=True)
         table_own = lax.dynamic_slice(pos_table, (0, me * (width // group_size)), (seq_len, width // group_size))
         grad_rel = dot_tn(table_own, jnp.swapaxes(d_rel_all, 0, 1).reshape(seq_len, hidden)) * scale
-        grad_up = interleave([grad_up0, grad_up1], part)
-        grad_parts = [z.reshape(-1, pairs_half, 3, span) for z in (grad_low, grad_high)]
-        grad_query, grad_key, grad_value = (
-            jnp.concatenate([z[:, :, n] for z in grad_parts], axis=1) for n in range(3))
+        grad_up = interleave([grad_up0, grad_up1], part, by_kind)
+        grad_query, grad_key, grad_value = to_heads(grad_low, grad_high, span, head_dim)
         d_u = jnp.concatenate([d_u_low, d_u_high], axis=0)
         d_w = jnp.concatenate([d_w_low, d_w_high], axis=0)
 

time: 2190 us -> 1880 us (0.86)
  waiting for transfers between devices: 824 us -> 550 us
  matrix products: 928 us -> 825 us
  Pallas kernels: 208 us -> 305 us
  local copies, waits for them, and re-layouts: 94.2 us -> 53.1 us
    reduce_scatter x7, waiting for transfers between devices: 646 us -> 380 us  [spread(): lax.psum_scatter(summed, axis_name, scatter_dimension=0, axis_index_group...]
    dot_general x15 -> x11, matrix products: 315 us -> 211 us  [dot_tn(): lax.dot_general(a, b, (((0,), (0,)), ((), ())), preferred_element_type=F32)]
    pallas_call x2 -> x5, Pallas kernels: 15.4 us -> 113 us  [the longest x2 90.4 us: wgrad(): pl.pallas_call(functools.partial(wgrad_kernel, chips=chips, scale=scale),...]
    dynamic_slice x7 -> x3, local copies, waits for them, and re-layouts: 45.6 us -> 13.7 us  [shares(): lax.dynamic_slice(acts, (0, (2 * c + kind) * part), (tokens, part))]
  transfers between devices with their start and end apart: 21 -> 22, of which waited for: 11 -> 8; matrix products, arithmetic and copies ran while one was open for 38% -> 50% of each run, Pallas kernels for 4% -> 15%
where the time goes in v3:
time: 1880 us; the launch traced here: 1870 us
  matrix products  825 us (44%)
  waiting for transfers between devices  550 us (29%)
  Pallas kernels  305 us (16%)
  other arithmetic  79.5 us (4%)
  local copies, waits for them, and re-layouts  53.1 us (3%)
  blocking collectives  34.9 us (2%)
    reduce_scatter x7, waiting for transfers between devices, spread(): lax.psum_scatter(summed, axis_name, scatter_dimension=0, axis_index_group...  380 us
    dot_general x7, matrix products, dot_nt(): lax.dot_general(a, b, (((1,), (1,)), ((), ())), preferred_element_type=F32)  328 us
    dot_general x7, matrix products, dot_nn(): lax.dot_general(a, b, (((1,), (0,)), ((), ())), preferred_element_type=F32)  286 us
    dot_general x11, matrix products, dot_tn(): lax.dot_general(a, b, (((0,), (0,)), ((), ())), preferred_element_type=F32)  211 us
    pallas_call x2, Pallas kernels, attn_bwd(): pl.pallas_call(functools.partial(attn_bwd_kernel, heads=heads, head_dim=h...  118 us
    all_gather x1, waiting for transfers between devices, gather(): return lax.all_gather(local_shard, axis_name, axis=0, tiled=True)  112 us
    pallas_call x2, Pallas kernels, wgrad(): pl.pallas_call(functools.partial(wgrad_kernel, chips=chips, scale=scale),...  90.4 us
    pallas_call x1, Pallas kernels, attn_fwd(): pl.pallas_call(functools.partial(attn_fwd_kernel, heads=heads, head_dim=h...  66.6 us
  transfers between devices with their start and end apart: 22, of which 8 were waited for; matrix products, arithmetic and copies ran while one was open for 50% of the time, Pallas kernels for 15%

profile of v3, /device:TPU:0, one launch (start us, length us, event | category | flops | bytes accessed | tf_op | source)
XLA Modules:
  0.0 1873.2 jit_solution(7094658343532324848)
XLA Ops:
  82.7 27.4 %all-gather.14.cloned.1.call-done = bf16[2560,2048]{1,0:T(8,128)(2,1)} async-done(((bf16[320,2048]{1,0:T(8,128)(2,1)}), bf16[2560,2048]{1,0:T(8,128)(2,1)}) %all-gather.14.cloned.1.call-update) | async-done | bytes 10485776 | tf_op jit(solution)/shard_map/all_gather | solution.py:429
  119.7 112.4 %all-gather.8.cloned.1.call-done = bf16[2048,6144]{1,0:T(8,128)(2,1)} async-done(((bf16[256,6144]{1,0:T(8,128)(2,1)}), bf16[2048,6144]{1,0:T(8,128)(2,1)}) %all-gather.8.cloned.1.call-update) | async-done | bytes 25165840 | tf_op jit(solution)/shard_map/all_gather | solution.py:367
  232.1 60.1 %convolution_convert_fusion = bf16[2048,6144]{1,0:T(8,128)(2,1)} fusion(bf16[2048,2048]{1,0:T(8,128)(2,1)} %fusion.39, bf16[2048,6144]{1,0:T(8,128)(2,1)} %all-gather.8.cloned.1.call-done), kind=kOutput, calls=%fused_computation.41 | convolution fusion | flops 51552190464 | bytes 58720256 | tf_op jit(solution)/shard_map/dot_general | solution.py:38
  292.2 66.6 %attn_fwd.1 = bf16[4,512,2048]{2,1,0:T(8,128)(2,1)} custom-call(bf16[4,512,6144]{2,1,0:T(8,128)(2,1)} %bitcast.174, bf16[8,320,2048]{2,1,0:T(8,128)(2,1)} %bitcast.144, f32[8,1,256]{2,1,0:T(1,128)} %get-tuple-element.107.u_ref, f32[8,1,256]{2,1,0:T(1,128)} %get-tuple-element.106.w_ref), custom_call_target="tpu_custom_call" | custom-call | flops 17179869184 | bytes 33554432 | tf_op jit(solution)/shard_map/attn_fwd/pallas_call | solution.py:217
  358.8 25.0 %fusion.34 = (f32[2048]{0:T(1024)S(1)}, bf16[2048,2048]{1,0:T(8,128)(2,1)}) fusion(bf16[2048,2048]{1,0:T(8,128)(2,1)} %bitcast.130, bf16[2048,2048]{1,0:T(8,128)(2,1)} %bitcast.133, bf16[4,512,2048]{2,1,0:T(8,128)(2,1)} %param.13), kind=kOutput, calls=%fused_computation.58 | convolution fusion | flops 17205032960 | bytes 33562624 | tf_op jit(solution)/shard_map/dot_general | solution.py:38
  394.3 53.4 %fusion.13 = (bf16[2048,4096]{1,0:T(8,128)(2,1)}, bf16[2048,4096]{1,0:T(8,128)(2,1)}) fusion(bf16[2048,2048]{1,0:T(8,128)(2,1)} %fusion.26.refs_0_.refs_1_.refs_2_.refs_3_, bf16[2,2048,4096]{2,1,0:T(8,128)(2,1)} %all-gather.10.cloned.1.call-done), kind=kOutput, calls=%fused_computation.25 | convolution fusion | flops 34452013056 | bytes 58720256 | tf_op jit(solution)/shard_map/dot_general | solution.py:38
  447.7 25.9 %fusion.54 = f32[2048,2048]{1,0:T(8,128)} fusion(bf16[2048,2048]{1,0:T(8,128)(2,1)} %bitcast.136, bf16[2048,4096]{1,0:T(8,128)(2,1)} %get-tuple-element.67, s32[]{:T(128)S(6)} %select_n.33), kind=kOutput, calls=%fused_computation.97 | convolution fusion | flops 17179869184 | bytes 33554436 | tf_op jit(solution)/shard_map/dot_general | solution.py:46
  473.7 51.5 %fusion.19 = (bf16[2048,4096]{1,0:T(8,128)(2,1)}, bf16[2048,4096]{1,0:T(8,128)(2,1)}) fusion(bf16[2048,2048]{1,0:T(8,128)(2,1)} %fusion.26.refs_0_.refs_1_.refs_2_.refs_3_, bf16[2,2048,4096]{2,1,0:T(8,128)(2,1)} %all-gather.10.cloned.1.call-done), kind=kOutput, calls=%fused_computation.31 | convolution fusion | flops 34452013056 | bytes 58720256 | tf_op jit(solution)/shard_map/dot_general | solution.py:38
  525.2 26.3 %add_multiply_fusion.1 = f32[2048,2048]{1,0:T(8,128)} fusion(f32[2048,2048]{1,0:T(8,128)} %collective-permute-done, bf16[2048,2048]{1,0:T(8,128)(2,1)} %bitcast.137, bf16[2048,4096]{1,0:T(8,128)(2,1)} %get-tuple-element.67, s32[]{:T(128)S(6)} %select_n.34), kind=kOutput, calls=%fused_computation.77 | convolution fusion | flops 17188257792 | bytes 50331652 | tf_op jit(solution)/shard_map/dot_general | solution.py:46
  551.5 24.3 %fusion.52 = f32[2048,2048]{1,0:T(8,128)} fusion(bf16[2048,2048]{1,0:T(8,128)(2,1)} %bitcast.138, bf16[2048,4096]{1,0:T(8,128)(2,1)} %get-tuple-element.52, s32[]{:T(128)S(6)} %select_n.33), kind=kOutput, calls=%fused_computation.95 | convolution fusion | flops 17179869184 | bytes 33554436 | tf_op jit(solution)/shard_map/dot_general | solution.py:46
  576.1 65.1 %fusion.4.refs_5_ = bf16[2048,4096]{1,0:T(8,128)(2,1)} fusion(bf16[2048,4096]{1,0:T(8,128)(2,1)} %get-tuple-element.114, bf16[2048,2048]{1,0:T(8,128)(2,1)} %bitcast.139, bf16[2,4096,2048]{2,1,0:T(8,128)(2,1)} %all-gather.12.cloned.1.call-done), kind=kOutput, calls=%fused_computation.16 | convolution fusion | flops 34552676352 | bytes 58720256 | tf_op jit(solution)/shard_map/dot_general | solution.py:42
  641.6 26.1 %add_multiply_fusion = f32[2048,2048]{1,0:T(8,128)} fusion(f32[2048,2048]{1,0:T(8,128)} %collective-permute-done.2, bf16[2048,2048]{1,0:T(8,128)(2,1)} %bitcast.140, bf16[2048,4096]{1,0:T(8,128)(2,1)} %get-tuple-element.52, s32[]{:T(128)S(6)} %select_n.34), kind=kOutput, calls=%fused_computation.76 | convolution fusion | flops 17188257792 | bytes 50331652 | tf_op jit(solution)/shard_map/dot_general | solution.py:46
  667.7 65.0 %fusion.7.refs_5_ = bf16[2048,4096]{1,0:T(8,128)(2,1)} fusion(bf16[2048,4096]{1,0:T(8,128)(2,1)} %get-tuple-element.116, bf16[2048,2048]{1,0:T(8,128)(2,1)} %bitcast.141, bf16[2,4096,2048]{2,1,0:T(8,128)(2,1)} %all-gather.12.cloned.1.call-done), kind=kOutput, calls=%fused_computation.19 | convolution fusion | flops 34552676352 | bytes 58720256 | tf_op jit(solution)/shard_map/dot_general | solution.py:42
  745.0 19.2 %collective-permute-done.1.refs_4_ = bf16[2048,1024]{1,0:T(8,128)(2,1)} collective-permute-done((bf16[2048,1024]{1,0:T(8,128)(2,1)}, bf16[2048,1024]{1,0:T(8,128)(2,1)}, u32[]{:S(2)}, u32[]{:S(2)}) %collective-permute-start.1) | collective-permute-done | bytes 4194336 | tf_op jit(solution)/shard_map/ppermute | solution.py:389
  764.2 45.0 %wgrad.2 = f32[1024,4096]{1,0:T(8,128)} custom-call(s32[1]{0:T(128)} %bitcast.16.kind_ref, bf16[2048,2048]{1,0:T(8,128)(2,1)} %fusion.26.refs_0_.refs_1_.refs_2_.refs_3_, bf16[2048,2048]{1,0:T(8,128)(2,1)} %fusion.26.refs_0_.refs_1_.refs_2_.refs_3_, bf16[2048,2048]{1,0:T(8,128)(2,1)} %fusion.26.refs_0_.refs_1_.refs_2_.refs_3_, ...), custom_call_target="tpu_custom_call" | custom-call | flops 34359738368 | bytes 50331648 | tf_op jit(solution)/shard_map/wgrad/pallas_call | solution.py:342
  809.2 43.7 %fusion.42 = f32[2048,2048]{1,0:T(8,128)} fusion(bf16[2048,4096]{1,0:T(8,128)(2,1)} %fusion.4.refs_5_, bf16[2,2048,4096]{2,1,0:T(8,128)(2,1)} %all-gather.10.cloned.1.call-done), kind=kOutput, calls=%fused_computation.80 | convolution fusion | flops 34359738368 | bytes 50331648 | tf_op jit(solution)/shard_map/dot_general | solution.py:42
  852.9 45.4 %wgrad.3 = f32[1024,4096]{1,0:T(8,128)} custom-call(s32[1]{0:T(128)} %bitcast.16.kind_ref, bf16[2048,2048]{1,0:T(8,128)(2,1)} %fusion.26.refs_0_.refs_1_.refs_2_.refs_3_, bf16[2048,2048]{1,0:T(8,128)(2,1)} %fusion.26.refs_0_.refs_1_.refs_2_.refs_3_, bf16[2048,2048]{1,0:T(8,128)(2,1)} %fusion.26.refs_0_.refs_1_.refs_2_.refs_3_, ...), custom_call_target="tpu_custom_call" | custom-call | flops 34359738368 | bytes 50331648 | tf_op jit(solution)/shard_map/wgrad/pallas_call | solution.py:342
  898.4 52.8 %fusion.28 = (f32[2048]{0:T(1024)}, f32[2048]{0:T(1024)S(1)}, bf16[2048,2048]{1,0:T(8,128)(2,1)}) fusion(bf16[2048,2048]{1,0:T(8,128)(2,1)} %get-tuple-element.112, f32[2048]{0:T(1024)S(1)} %copy-done.26, f32[2048]{0:T(1024)S(1)} %bitcast.161, f32[2048,2048]{1,0:T(8,128)} %fusion.42, bf16[2048,4096]{1,0:T(8,128)(2,1)} %fusion.7.refs_5_, ...), kind=kOutput, calls=%fused_computation.52 | convolution fusion | flops 34401681408 | bytes 67141632 | tf_op jit(solution)/shard_map/dot_general | solution.py:42
  960.2 24.1 %convolution_convert_fusion.3 = bf16[2048,2048]{1,0:T(8,128)(2,1)} fusion(bf16[2048,2048]{1,0:T(8,128)(2,1)S(1)} %fusion.31, bf16[2048,2048]{1,0:T(8,128)(2,1)} %bitcast.134), kind=kOutput, calls=%fused_computation.99 | convolution fusion | flops 17184063488 | bytes 25165824 | tf_op jit(solution)/shard_map/dot_general | solution.py:42
  984.3 58.9 %attn_bwd.2 = (bf16[4,512,3072]{2,1,0:T(8,128)(2,1)}, f32[4,512,256]{2,1,0:T(8,128)}, f32[4,8,256]{2,1,0:T(8,128)}, f32[4,8,256]{2,1,0:T(8,128)}) custom-call(bf16[4,512,6144]{2,1,0:T(8,128)(2,1)} %bitcast.175, bf16[8,320,2048]{2,1,0:T(8,128)(2,1)} %bitcast.145, f32[8,1,256]{2,1,0:T(1,128)} %get-tuple-element.107.u_ref, ...), custom_call_target="tpu_custom_call" | custom-call | flops 21474836480 | bytes 29360128 | tf_op jit(solution)/shard_map/attn_bwd/pallas_call | solution.py:237
  1043.2 18.5 fusion.82
  1081.8 21.0 %add_multiply_fusion.3 = f32[1024,3072]{1,0:T(8,128)} fusion(f32[1024,3072]{1,0:T(8,128)} %collective-permute-done.5, bf16[2048,3072]{1,0:T(8,128)(2,1)} %bitcast.178, bf16[2048,256]{1,0:T(8,128)(2,1)S(1)} %copy-done.10, bf16[2048,256]{1,0:T(8,128)(2,1)S(1)} %copy-done.12, bf16[2048,256]{1,0:T(8,128)(2,1)} %get-tuple-element.96, ...), kind=kOutput, calls=%fused_computation.89 | convolution fusion | flops 12907970560 | bytes 41943040 | tf_op jit(solution)/shard_map/dot_general | solution.py:46
  1102.8 59.3 %attn_bwd.3 = (bf16[4,512,3072]{2,1,0:T(8,128)(2,1)}, f32[4,512,256]{2,1,0:T(8,128)}, f32[4,8,256]{2,1,0:T(8,128)}, f32[4,8,256]{2,1,0:T(8,128)}) custom-call(bf16[4,512,6144]{2,1,0:T(8,128)(2,1)} %bitcast.176, bf16[8,320,2048]{2,1,0:T(8,128)(2,1)} %bitcast.146, f32[8,1,256]{2,1,0:T(1,128)} %get-tuple-element.107.u_ref, ...), custom_call_target="tpu_custom_call" | custom-call | flops 21474836480 | bytes 29360128 | tf_op jit(solution)/shard_map/attn_bwd/pallas_call | solution.py:237
  1212.7 34.7 %fusion.46 = f32[2048,2048]{1,0:T(8,128)} fusion(bf16[2048,3072]{1,0:T(8,128)(2,1)} %bitcast.181, bf16[2048,6144]{1,0:T(8,128)(2,1)} %all-gather.8.cloned.1.call-done), kind=kOutput, calls=%fused_computation.84 | convolution fusion | flops 25769803776 | bytes 41943040 | tf_op jit(solution)/shard_map/dot_general | solution.py:42
  1255.8 21.6 %add_multiply_fusion.2 = f32[1024,3072]{1,0:T(8,128)} fusion(f32[1024,3072]{1,0:T(8,128)} %collective-permute-done.8, bf16[2048,3072]{1,0:T(8,128)(2,1)} %bitcast.182, bf16[2048,256]{1,0:T(8,128)(2,1)S(1)} %copy-done.11, bf16[2048,256]{1,0:T(8,128)(2,1)S(1)} %copy-done.13, bf16[2048,256]{1,0:T(8,128)(2,1)} %get-tuple-element.96, ...), kind=kOutput, calls=%fused_computation.88 | convolution fusion | flops 12907970560 | bytes 41943040 | tf_op jit(solution)/shard_map/dot_general | solution.py:46
  1277.4 43.3 %fusion.44 = f32[2048,2048]{1,0:T(8,128)} fusion(bf16[2048,4096]{1,0:T(8,128)(2,1)} %get-tuple-element.67, bf16[2,4096,2048]{2,1,0:T(8,128)(2,1)} %all-gather.12.cloned.1.call-done), kind=kOutput, calls=%fused_computation.82 | convolution fusion | flops 34359738368 | bytes 50331648 | tf_op jit(solution)/shard_map/dot_general | solution.py:38
  1320.7 50.1 %fusion.37 = bf16[2048,2048]{1,0:T(8,128)(2,1)} fusion(f32[2048,2048]{1,0:T(8,128)} %fusion.44, bf16[2048,2048]{1,0:T(8,128)(2,1)} %get-tuple-element.112, bf16[2,4096,2048]{2,1,0:T(8,128)(2,1)} %all-gather.12.cloned.1.call-done, bf16[2048,4096]{1,0:T(8,128)(2,1)} %get-tuple-element.116), kind=kOutput, calls=%fused_computation.61 | convolution fusion | flops 34460401664 | bytes 67108864 | tf_op jit(solution)/shard_map/dot_general | solution.py:38
  1370.9 42.7 %fusion.29 = (f32[2048]{0:T(1024)S(1)}, f32[2048]{0:T(1024)S(1)}, bf16[2048,2048]{1,0:T(8,128)(2,1)}) fusion(bf16[4,512,2048]{2,1,0:T(8,128)(2,1)} %param.13, f32[2048]{0:T(1024)S(1)} %copy-done.24, f32[2048]{0:T(1024)S(1)} %bitcast.158, f32[2048,2048]{1,0:T(8,128)} %fusion.46, bf16[2048,3072]{1,0:T(8,128)(2,1)} %bitcast.179, ...), kind=kOutput, calls=%fused_computation.53 | convolution fusion | flops 25811742720 | bytes 58753024 | tf_op jit(solution)/shard_map/dot_general | solution.py:42
  1413.7 23.5 %all-reduce = f32[8,4,256]{2,1,0:T(4,128)S(1)} all-reduce(f32[8,4,256]{2,1,0:T(4,128)S(1)} %maximum_multiply_fusion), channel_id=4, replica_groups=mesh['fsdp'=8] {'fsdp'}, use_global_device_ids=true, to_apply=%region_8.0.clone | all-reduce | flops 8192 | bytes 65536
  1464.2 158.6 %reduce-scatter.16.cloned.1.call-done.refs_1_ = f32[256,4096]{1,0:T(8,128)} async-done(((f32[1024,4096]{1,0:T(8,128)}), f32[256,4096]{1,0:T(8,128)}) %reduce-scatter.16.cloned.1.call-update) | async-done | bytes 4194320 | tf_op jit(solution)/shard_map/reduce_scatter | solution.py:399
  1637.7 103.1 %reduce-scatter.8.cloned.1.call-done.low_ref = f32[256,3072]{1,0:T(8,128)} async-done(((f32[1024,3072]{1,0:T(8,128)}), f32[256,3072]{1,0:T(8,128)}) %reduce-scatter.8.cloned.1.call-update) | async-done | bytes 3145744 | tf_op jit(solution)/shard_map/reduce_scatter | solution.py:399
  1740.8 118.1 %reduce-scatter.10.cloned.1.call-done.high_ref = f32[256,3072]{1,0:T(8,128)} async-done(((f32[1024,3072]{1,0:T(8,128)}), f32[256,3072]{1,0:T(8,128)}) %reduce-scatter.10.cloned.1.call-update) | async-done | bytes 3145744 | tf_op jit(solution)/shard_map/reduce_scatter | solution.py:399
  (226 shorter events, 245.2 us)
Async XLA Ops:
  27.6 19.6 %all-to-all-start = ((bf16[256,8,256]{0,2,1:T(8,128)(2,1)}), bf16[256,8,256]{0,2,1:T(8,128)(2,1)S(1)}, u32[]{:S(2)}, u32[]{:S(2)}) async-start(bf16[256,8,256]{0,2,1:T(8,128)(2,1)} %bitcast.4), calls=%async_computation | async-start | bytes 2097152 | tf_op jit(solution)/shard_map/all_to_all | solution.py:425
  31.9 78.2 %all-gather.14.cloned.1.call-start = ((), (), s32[]{:S(2)}) async-start(), calls=%async_computation.19 | async-start | bytes 11796480 | tf_op jit(solution)/shard_map/all_gather | solution.py:429
  53.1 179.0 %all-gather.8.cloned.1.call-start = ((), (), s32[]{:S(2)}) async-start(), calls=%async_computation.9 | async-start | bytes 28311552 | tf_op jit(solution)/shard_map/all_gather | solution.py:367
  53.8 340.4 %all-gather.10.cloned.1.call-start = ((), (), s32[]{:S(2)}) async-start(), calls=%async_computation.10 | async-start | bytes 37748736 | tf_op jit(solution)/shard_map/all_gather | solution.py:402
  54.6 521.6 %all-gather.12.cloned.1.call-start = ((), (), s32[]{:S(2)}) async-start(), calls=%async_computation.11 | async-start | bytes 37748736 | tf_op jit(solution)/shard_map/all_gather | solution.py:402
  55.1 1192.2 %reduce-scatter.18.cloned.1.call-start = ((), (), s32[]{:S(2)}) async-start(), calls=%async_computation.17 | async-start | bytes 20971520 | tf_op jit(solution)/shard_map/reduce_scatter | solution.py:399
  61.9 57.8 %copy-start.23 = (f32[2048]{0:T(1024)}, f32[2048]{0:T(1024)S(1)}, u32[]{:S(2)}) copy-start(f32[2048]{0:T(1024)S(1)} %rsqrt.22) | copy-start | bytes 24580
  473.6 51.7 %collective-permute-start = (f32[2048,2048]{1,0:T(8,128)}, f32[2048,2048]{1,0:T(8,128)}, u32[]{:S(2)}, u32[]{:S(2)}) collective-permute-start(f32[2048,2048]{1,0:T(8,128)} %fusion.54), channel_id=1, source_target_pairs={{0,1},{1,0},{2,3},{3,2},{4,5},{5,4},{6,7},{7,6}} | collective-permute-start | bytes 50331656 | tf_op jit(solution)/shard_map/ppermute | solution.py:389
  575.8 65.8 %collective-permute-start.2 = (f32[2048,2048]{1,0:T(8,128)}, f32[2048,2048]{1,0:T(8,128)}, u32[]{:S(2)}, u32[]{:S(2)}) collective-permute-start(f32[2048,2048]{1,0:T(8,128)} %fusion.52), channel_id=1, source_target_pairs={{0,1},{1,0},{2,3},{3,2},{4,5},{5,4},{6,7},{7,6}} | collective-permute-start | bytes 50331656 | tf_op jit(solution)/shard_map/ppermute | solution.py:389
  576.0 671.4 %reduce-scatter.20.cloned.1.call-start = ((), (), s32[]{:S(2)}) async-start(), calls=%async_computation.18 | async-start | bytes 20971520 | tf_op jit(solution)/shard_map/reduce_scatter | solution.py:399
  641.2 123.0 %collective-permute-start.3 = (bf16[2048,4096]{1,0:T(8,128)(2,1)}, bf16[2048,4096]{1,0:T(8,128)(2,1)}, u32[]{:S(2)}, u32[]{:S(2)}) collective-permute-start(bf16[2048,4096]{1,0:T(8,128)(2,1)} %fusion.4.refs_5_), channel_id=1, source_target_pairs={{0,1},{1,0},{2,3},{3,2},{4,5},{5,4},{6,7},{7,6}} | collective-permute-start | bytes 50331656 | tf_op jit(solution)/shard_map/ppermute | solution.py:389
  732.7 120.2 %collective-permute-start.4 = (bf16[2048,4096]{1,0:T(8,128)(2,1)}, bf16[2048,4096]{1,0:T(8,128)(2,1)}, u32[]{:S(2)}, u32[]{:S(2)}) collective-permute-start(bf16[2048,4096]{1,0:T(8,128)(2,1)} %fusion.7.refs_5_), channel_id=1, source_target_pairs={{0,1},{1,0},{2,3},{3,2},{4,5},{5,4},{6,7},{7,6}} | collective-permute-start | bytes 50331656 | tf_op jit(solution)/shard_map/ppermute | solution.py:389
  737.6 26.6 %collective-permute-start.1 = (bf16[2048,1024]{1,0:T(8,128)(2,1)}, bf16[2048,1024]{1,0:T(8,128)(2,1)}, u32[]{:S(2)}, u32[]{:S(2)}) collective-permute-start(bf16[2048,1024]{1,0:T(8,128)(2,1)} %pad_maximum_fusion.3), channel_id=1, source_target_pairs={{0,1},{1,0},{2,3},{3,2},{4,5},{5,4},{6,7},{7,6}} | collective-permute-start | bytes 12582920 | tf_op jit(solution)/shard_map/ppermute | solution.py:389
  745.0 692.3 %reduce-scatter.12.cloned.1.call-start = ((), (), s32[]{:S(2)}) async-start(), calls=%async_computation.14 | async-start | bytes 13107200 | tf_op jit(solution)/shard_map/reduce_scatter | solution.py:399
  898.4 52.8 %copy-start.34 = (f32[2048]{0:T(1024)S(1)}, f32[2048]{0:T(1024)}, u32[]{:S(2)}) copy-start(f32[2048]{0:T(1024)} %copy-done.33) | copy-start | bytes 24580
  898.4 52.9 %copy-start = (bf16[2048,2048]{1,0:T(8,128)(2,1)S(1)}, bf16[2048,2048]{1,0:T(8,128)(2,1)}, u32[]{:S(2)}) copy-start(bf16[2048,2048]{1,0:T(8,128)(2,1)} %get-tuple-element.112) | copy-start | bytes 25165828
  984.3 58.9 %copy-start.14 = (bf16[2048,256]{1,0:T(8,128)(2,1)S(1)}, bf16[2048,256]{1,0:T(8,128)(2,1)}, u32[]{:S(2)}) copy-start(bf16[2048,256]{1,0:T(8,128)(2,1)} %get-tuple-element.90) | copy-start | bytes 3145732
  984.3 58.9 %copy-start.16 = (bf16[2048,256]{1,0:T(8,128)(2,1)S(1)}, bf16[2048,256]{1,0:T(8,128)(2,1)}, u32[]{:S(2)}) copy-start(bf16[2048,256]{1,0:T(8,128)(2,1)} %get-tuple-element.91) | copy-start | bytes 3145732
  984.3 58.9 %copy-start.18 = (bf16[2048,256]{1,0:T(8,128)(2,1)S(1)}, bf16[2048,256]{1,0:T(8,128)(2,1)}, u32[]{:S(2)}) copy-start(bf16[2048,256]{1,0:T(8,128)(2,1)} %get-tuple-element.92) | copy-start | bytes 3145732
  1061.8 20.0 %collective-permute-start.5 = (f32[1024,3072]{1,0:T(8,128)}, f32[1024,3072]{1,0:T(8,128)}, u32[]{:S(2)}, u32[]{:S(2)}) collective-permute-start(f32[1024,3072]{1,0:T(8,128)} %fusion.82), channel_id=1, source_target_pairs={{0,1},{1,0},{2,3},{3,2},{4,5},{5,4},{6,7},{7,6}} | collective-permute-start | bytes 37748744 | tf_op jit(solution)/shard_map/ppermute | solution.py:389
  1081.7 102.7 %collective-permute-start.6 = (f32[1024,2048]{1,0:T(8,128)}, f32[1024,2048]{1,0:T(8,128)}, u32[]{:S(2)}, u32[]{:S(2)}) collective-permute-start(f32[1024,2048]{1,0:T(8,128)} %fusion.58), channel_id=1, source_target_pairs={{0,1},{1,0},{2,3},{3,2},{4,5},{5,4},{6,7},{7,6}} | collective-permute-start | bytes 25165832 | tf_op jit(solution)/shard_map/ppermute | solution.py:389
  1102.8 59.3 %copy-start.7 = (f32[4,512,256]{2,1,0:T(8,128)S(1)}, f32[4,512,256]{2,1,0:T(8,128)}, u32[]{:S(2)}) copy-start(f32[4,512,256]{2,1,0:T(8,128)} %get-tuple-element.64) | copy-start | bytes 6291460
  1165.7 33.7 %collective-permute-start.7 = (f32[4,512,256]{2,1,0:T(8,128)}, f32[4,512,256]{2,1,0:T(8,128)S(1)}, u32[]{:S(2)}, u32[]{:S(2)}) collective-permute-start(f32[4,512,256]{2,1,0:T(8,128)} %dynamic-slice_bitcast_fusion), channel_id=1, source_target_pairs={{0,1},{1,0},{2,3},{3,2},{4,5},{5,4},{6,7},{7,6}} | collective-permute-start | bytes 6291464 | tf_op jit(solution)/shard_map/ppermute | solution.py:389
  1208.9 255.3 %reduce-scatter.14.cloned.1.call-start = ((), (), s32[]{:S(2)}) async-start(), calls=%async_computation.15 | async-start | bytes 20971520 | tf_op jit(solution)/shard_map/reduce_scatter | solution.py:399
  1209.7 413.2 %reduce-scatter.16.cloned.1.call-start = ((), (), s32[]{:S(2)}) async-start(), calls=%async_computation.16 | async-start | bytes 20971520 | tf_op jit(solution)/shard_map/reduce_scatter | solution.py:399
  1210.4 530.4 %reduce-scatter.8.cloned.1.call-start = ((), (), s32[]{:S(2)}) async-start(), calls=%async_computation.12 | async-start | bytes 15728640 | tf_op jit(solution)/shard_map/reduce_scatter | solution.py:399
  1211.0 647.9 %reduce-scatter.10.cloned.1.call-start = ((), (), s32[]{:S(2)}) async-start(), calls=%async_computation.13 | async-start | bytes 15728640 | tf_op jit(solution)/shard_map/reduce_scatter | solution.py:399
  1211.1 44.7 %collective-permute-start.8 = (f32[1024,3072]{1,0:T(8,128)}, f32[1024,3072]{1,0:T(8,128)}, u32[]{:S(2)}, u32[]{:S(2)}) collective-permute-start(f32[1024,3072]{1,0:T(8,128)} %fusion.81), channel_id=1, source_target_pairs={{0,1},{1,0},{2,3},{3,2},{4,5},{5,4},{6,7},{7,6}} | collective-permute-start | bytes 37748744 | tf_op jit(solution)/shard_map/ppermute | solution.py:389
  1320.7 50.1 %copy-start.28 = (f32[8,1,256]{2,1,0:T(1,128)S(1)}, f32[8,1,256]{2,1,0:T(1,128)}, u32[]{:S(2)}) copy-start(f32[8,1,256]{2,1,0:T(1,128)} %copy-done.27) | copy-start | bytes 24580
  1370.9 66.3 %copy-start.32 = (f32[1,4,4,128]{3,1,2,0:T(4,128)S(1)}, f32[1,4,4,128]{3,1,2,0:T(4,128)}, u32[]{:S(2)}) copy-start(f32[1,4,4,128]{3,1,2,0:T(4,128)} %copy-done.31) | copy-start | bytes 24580
  1446.0 189.3 %all-to-all-start.1 = ((bf16[8,512,256]{1,2,0:T(8,128)(2,1)}), bf16[8,512,256]{1,2,0:T(8,128)(2,1)S(1)}, u32[]{:S(2)}, u32[]{:S(2)}) async-start(bf16[8,512,256]{1,2,0:T(8,128)(2,1)} %broadcast_in_dim.11), calls=%async_computation.4 | async-start | bytes 4194304 | tf_op jit(solution)/shard_map/all_to_all | solution.py:504
  1464.0 171.2 %copy-start.5 = (bf16[512,1024]{1,0:T(8,128)(2,1)S(1)}, bf16[512,1024]{1,0:T(8,128)(2,1)}, u32[]{:S(2)}) copy-start(bf16[512,1024]{1,0:T(8,128)(2,1)} %copy-done.4) | copy-start | bytes 3145732
  (38 other events, 615.7 us)
Sparse Core Ops, SparseCore 0:
  53.2 56.7 all-gather.13
  112.4 119.6 all-gather.7
  233.9 155.0 all-gather.9
  390.7 155.0 all-gather.11
  576.2 147.9 reduce-scatter.17
  745.1 148.0 reduce-scatter.19
  1209.0 97.7 reduce-scatter.11
  1309.8 154.3 reduce-scatter.13
  1467.2 155.5 reduce-scatter.15
  1625.7 115.0 reduce-scatter.7
  1743.9 115.0 reduce-scatter.9

commit v4 on v3

--- a/solution.py
+++ b/solution.py
@@ -256,13 +256,14 @@
         out_ref[..., n * width:(n + 1) * width] = ref[...]
 
 
-def interleave(arrays, width, place=lambda i: i):
-    rows, cols = arrays[0].shape
-    total = len(arrays) * cols
+def interleave(arrays, width, blocks, places=None):
+    rows = arrays[0].shape[0]
+    places = places or [lambda i: i] * len(arrays)
+    total = len(arrays) * width * blocks
     return pl.pallas_call(
         interleave_kernel,
-        grid=(cols // width,),
-        in_specs=[pl.BlockSpec((rows, width), lambda i: (0, place(i)))] * len(arrays),
+        grid=(blocks,),
+        in_specs=[pl.BlockSpec((rows, width), lambda i, f=f: (0, f(i))) for f in places],
         out_specs=pl.BlockSpec((rows, len(arrays) * width), lambda i: (0, i)),
         out_shape=jax.ShapeDtypeStruct((rows, total), arrays[0].dtype),
         cost_estimate=pl.CostEstimate(flops=rows * total, bytes_accessed=4 * rows * total, transcendentals=0),
@@ -289,71 +290,89 @@
     )(array)
 
 
-def heads_kernel(low_ref, high_ref, *out_refs, span, head_dim):
-    rows = low_ref.shape[0]
+def heads_kernel(in_ref, *out_refs, span, head_dim):
+    rows, cols = in_ref.shape
+    heads = cols // (len(out_refs) * head_dim)
     per = span // head_dim
-    count = low_ref.shape[1] // (len(out_refs) * span)
-    heads = 2 * count * per
-    for half, ref in enumerate((low_ref, high_ref)):
-        for pair in range(count):
-            for part, out_ref in enumerate(out_refs):
-                for n in range(per):
-                    at = (pair * len(out_refs) + part) * span + n * head_dim
-                    head = (half * count + pair) * per + n
-                    out_ref[pl.ds(head, rows, stride=heads), :] = ref[:, at:at + head_dim]
-
-
-def to_heads(low, high, span, head_dim):
-    rows, cols = low.shape
-    heads = 2 * cols // (3 * head_dim)
+    for head in range(heads):
+        for part, out_ref in enumerate(out_refs):
+            at = (head // per * len(out_refs) + part) * span + head % per * head_dim
+            out_ref[pl.ds(head, rows, stride=heads), :] = in_ref[:, at:at + head_dim]
+
+
+def to_heads(array, span, head_dim):
+    rows, cols = array.shape
+    heads = cols // (3 * head_dim)
     step = rows // 4
     return pl.pallas_call(
         functools.partial(heads_kernel, span=span, head_dim=head_dim),
         grid=(4,),
-        in_specs=[pl.BlockSpec((step, cols), lambda i: (i, 0))] * 2,
+        in_specs=[pl.BlockSpec((step, cols), lambda i: (i, 0))],
         out_specs=[pl.BlockSpec((step * heads, head_dim), lambda i: (i, 0))] * 3,
         out_shape=[jax.ShapeDtypeStruct((rows * heads, head_dim), F32)] * 3,
-        cost_estimate=pl.CostEstimate(flops=2 * rows * cols, bytes_accessed=16 * rows * cols, transcendentals=0),
+        cost_estimate=pl.CostEstimate(flops=rows * cols, bytes_accessed=8 * rows * cols, transcendentals=0),
         name="to_heads",
-    )(low, high)
-
-
-def wgrad_kernel(kind_ref, *refs, chips, scale):
+    )(array)
+
+
+def wgrad_kernel(kind_ref, *refs, count, scale, blank):
     del kind_ref
-    a_refs, (a2_ref, b1_ref, b2_ref, out_ref, t1, t2) = refs[:chips], refs[chips:]
-
-    @pl.when(pl.program_id(0) == 0)
+    a_refs, (a2_ref, b1_ref, b2_ref) = refs[:count], refs[count:count + 3]
+    out_ref, t1, t2 = refs[count + 3 + blank:]
+
+    @pl.when(pl.program_id(1) == 0)
     def _():
         part = a_refs[0].shape[1]
         for c, ref in enumerate(a_refs):
             t1[c * part:(c + 1) * part] = ref[...].T
             t2[c * part:(c + 1) * part] = a2_ref[:, c * part:(c + 1) * part].T
 
-    out_ref[...] = (dot_nn(t1[...], b1_ref[...]) + dot_nn(t2[...], b2_ref[...])) * scale
-
-
-def wgrad(kind, acts, acts2, cots, cots2, chips, scale, width):
+    total = (dot_nn(t1[...], b1_ref[...]) + dot_nn(t2[...], b2_ref[...])) * scale
+    out_ref[...] = total.reshape(out_ref.shape)
+
+
+def wgrad(kind, acts, acts2, cots, cots2, chips, scale, spread=True, place=(None, None), into=None):
     tokens, cols = acts.shape
-    part = cols // (2 * chips)
-    rows, total = chips * part, cots.shape[1]
-    share = [pl.BlockSpec((tokens, part), lambda j, k, c=c: (0, 2 * c + k[0])) for c in range(chips)]
-    whole = pl.BlockSpec((tokens, rows), lambda j, k: (0, 0))
-    block = pl.BlockSpec((tokens, width), lambda j, k: (0, j))
+    width, tile, depth = 512, 1024, cols // 2
+    tiles = depth // tile
+    if spread:
+        part = tile // chips
+        share = [pl.BlockSpec((tokens, part), lambda i, j, k, c=c: (0, 2 * c + k[0])) for c in range(chips)]
+    else:
+        share = [pl.BlockSpec((tokens, tile), lambda i, j, k: (0, tiles * k[0] + i))]
+    block = pl.BlockSpec((tokens, width), lambda i, j, k: (0, j))
+    specs = share + [pl.BlockSpec((tokens, tile), lambda i, j, k: (0, i)), block, block]
+    args = [acts] * len(share) + [acts2, cots, cots2]
+    at, aliases = 0, {}
+    if into is not None:
+        specs.append(pl.BlockSpec(memory_space=pl.ANY))
+        args.append(into[0])
+        at, aliases = into[1] // width, {len(args): 0}
+    rows, total = place[0], place[1] or cots.shape[1]
+    if rows is None:
+        out_spec = pl.BlockSpec((tile, width), lambda i, j, k: (i, j + at))
+        shape = (depth, total)
+    else:
+        out_spec = pl.BlockSpec((chips, tile // chips, width), lambda i, j, k: (0, 0, j + at))
+        shape = (chips, rows, total)
     return pl.pallas_call(
-        functools.partial(wgrad_kernel, chips=chips, scale=scale),
+        functools.partial(wgrad_kernel, count=len(share), scale=scale, blank=int(into is not None)),
         grid_spec=pltpu.PrefetchScalarGridSpec(
             num_scalar_prefetch=1,
-            grid=(total // width,),
-            in_specs=share + [whole, block, block],
-            out_specs=pl.BlockSpec((rows, width), lambda j, k: (0, j)),
-            scratch_shapes=[pltpu.VMEM((rows, tokens), BF16)] * 2,
+            grid=(tiles, cots.shape[1] // width),
+            in_specs=specs,
+            out_specs=out_spec,
+            scratch_shapes=[pltpu.VMEM((tile, tokens), BF16)] * 2,
         ),
-        out_shape=jax.ShapeDtypeStruct((rows, total), F32),
-        compiler_params=pltpu.CompilerParams(dimension_semantics=("arbitrary",), vmem_limit_bytes=56 * 2**20),
+        out_shape=jax.ShapeDtypeStruct(shape, F32),
+        input_output_aliases=aliases,
+        compiler_params=pltpu.CompilerParams(
+            dimension_semantics=("arbitrary", "arbitrary"), vmem_limit_bytes=56 * 2**20),
         cost_estimate=pl.CostEstimate(
-            flops=4 * tokens * rows * total, bytes_accessed=4 * (tokens * total + rows * total), transcendentals=0),
+            flops=4 * tokens * depth * cots.shape[1],
+            bytes_accessed=4 * cots.shape[1] * (tokens * tiles + depth), transcendentals=0),
         name="wgrad",
-    )(kind, *([acts] * chips), acts2, cots, cots2)
+    )(kind, *args)
 
 
 def solution(mesh):
@@ -388,13 +407,6 @@
         def swap(value):
             return lax.ppermute(value, axis_name, pairs)
 
-        def theirs(acts, cots, pick=shares):
-            mine = dot_tn(pick(acts, 1 - core), cots)
-            return mine, swap(mine)
-
-        def ours(acts, cots, received, pick=shares):
-            return (dot_tn(pick(acts, core), cots) + received) * scale
-
         def spread(summed):
             return lax.psum_scatter(summed, axis_name, scatter_dimension=0, axis_index_groups=same_core, tiled=True)
 
@@ -413,7 +425,7 @@
         w_full = vecs[:, 2:3].astype(F32)
         gain_mlp = vecs[:, 3].reshape(width).astype(F32)
 
-        qkv_own = interleave([z.reshape(-1, hidden) for z in (w_query, w_key, w_value)], span)
+        qkv_own = interleave([z.reshape(-1, hidden) for z in (w_query, w_key, w_value)], span, group_size)
         qkv_full = gather(qkv_own)
 
         ff_half = w_up.shape[1] // 2
@@ -447,52 +459,54 @@
             d_act = dot_nt(cots, weight).astype(BF16)
             return jax.vjp(gelu_tanh, pre.astype(F32))[1](d_act.astype(F32))[0].astype(BF16)
 
+        kind = core[None]
+        dy_theirs = swap(after(dy, h_attn))
+        attn_theirs = swap(shares(after(h_attn, qkv), 1 - core))
+        context_theirs = swap(shares(after(context, x1_f32), 1 - core))
+
         pre0, act0 = feed(h_mlp, up_full[0])
-        sent, got = theirs(act0, dy, block_of)
+        act0_theirs = swap(block_of(act0, 1 - core))
+        pre1, act1 = feed(after(h_mlp, act0), up_full[1])
+        sum_down0 = wgrad(kind, after(act0, act1), act0_theirs, dy, dy_theirs, chips, scale, False)
+        act1_theirs = swap(block_of(after(act1, sum_down0), 1 - core))
+        d_pre0 = unfeed(after(dy, sum_down0), down_full[0], pre0)
+        d_pre0_theirs = swap(d_pre0)
         hidden_theirs = swap(shares(h_mlp, 1 - core))
-        pre1, act1 = feed(after(h_mlp, sent), up_full[1])
-        sum_down0 = ours(after(act0, act1), dy, got, block_of)
-        sent, got = theirs(act1, after(dy, sum_down0), block_of)
-        d_pre0 = unfeed(after(dy, sent), down_full[0], pre0)
-        d_pre0_theirs = swap(d_pre0)
-        sum_down1 = ours(after(act1, d_pre0), dy, got, block_of)
+        sum_down1 = wgrad(kind, after(act1, d_pre0), act1_theirs, dy, dy_theirs, chips, scale, False)
         d_pre1 = unfeed(after(dy, sum_down1), down_full[1], pre1)
         d_pre1_theirs = swap(d_pre1)
-        kind = core[None]
-        sum_up0 = wgrad(kind, h_mlp, hidden_theirs, after(d_pre0, d_pre1), d_pre0_theirs, chips, scale, 512)
-        d_h_part = dot_nt(after(d_pre0, sum_up0), up_full[0])
-        sum_up1 = wgrad(kind, h_mlp, hidden_theirs, after(d_pre1, d_h_part), d_pre1_theirs, chips, scale, 512)
-        d_h_mlp = (d_h_part + dot_nt(after(d_pre1, sum_up1), up_full[1])).astype(BF16)
+        both = (None, 2 * ff_half)
+        sum_up = wgrad(kind, h_mlp, hidden_theirs, after(d_pre0, d_pre1), d_pre0_theirs, chips, scale,
+                       place=both)
+        sum_up = wgrad(kind, h_mlp, hidden_theirs, d_pre1, d_pre1_theirs, chips, scale,
+                       place=both, into=(sum_up, ff_half))
+        d_h_part = dot_nt(after(d_pre0, sum_up), up_full[0])
+        d_h_mlp = (d_h_part + dot_nt(after(d_pre1, d_h_part), up_full[1])).astype(BF16)
         grad_down = jnp.concatenate([spread(sum_down0), spread(sum_down1)], axis=0)
-        grad_up0, grad_up1 = spread(sum_up0), spread(sum_up1)
+        grad_up = spread(sum_up)
 
         d_x1_norm, grad_norm_mlp = jax.vjp(rms_norm, x1_f32, gain_mlp)[1](d_h_mlp)
         d_x1 = (dy.astype(F32) + d_x1_norm).astype(BF16)
+        d_x1_theirs = swap(d_x1)
         d_context = dot_nt(d_x1, out_full).astype(BF16).reshape(shape3)
-        pairs_half = group_size // 2
-        d_low, d_rel_low, d_u_low, d_w_low = attn_bwd(
-            qkv, out_rel, u_full, w_full, d_context, head_dim, 0, pairs_half)
-        d_low = d_low.reshape(tokens, -1)
-        sent, got = theirs(h_attn, d_low)
-        sent_o, got_o = theirs(context, after(d_x1, sent))
-        sum_low = ours(h_attn, after(d_low, sent_o), got)
-        d_high, d_rel_high, d_u_high, d_w_high = attn_bwd(
-            qkv, out_rel, u_full, w_full, after(d_context, sum_low), head_dim, pairs_half, pairs_half)
-        d_high = d_high.reshape(tokens, -1)
-        d_rel = jnp.concatenate([d_rel_low, d_rel_high], axis=0).reshape(chips, 2, seq_len, span)
+        d_qkv, d_rel, d_u, d_w = attn_bwd(
+            qkv, out_rel, u_full, w_full, d_context, head_dim, 0, group_size)
+        d_qkv = d_qkv.reshape(tokens, -1)
+        d_qkv_theirs = swap(d_qkv)
+        d_rel = d_rel.reshape(chips, 2, seq_len, span)
         got_rel = swap(lax.dynamic_index_in_dim(d_rel, 1 - core, 1, keepdims=False))
-        sent, got = theirs(h_attn, d_high)
-        sum_o = ours(context, after(d_x1, sent), got_o)
+        rows = hidden // group_size
+        sum_o = wgrad(kind, context, context_theirs, after(d_x1, d_qkv), d_x1_theirs, chips, scale,
+                      place=(rows + lines, None))
         d_rel = lax.dynamic_index_in_dim(d_rel, core, 1, keepdims=False) + got_rel
         d_rel = jnp.concatenate([d_rel[:, at:at + lines] for at in range(0, seq_len, lines)], axis=2)
-        sum_o_rel = jnp.concatenate([sum_o.reshape(chips, -1, width), d_rel], axis=1).reshape(-1, width)
-        grad_o_rel = spread(sum_o_rel)
-        sum_high = ours(h_attn, after(d_high, sum_o_rel), got)
-        grad_low, grad_high = spread(sum_low), spread(sum_high)
-        y_out = (x1_f32 + dot_nn(after(act0, sum_high), down_full[0]) + dot_nn(act1, down_full[1])).astype(BF16)
-
-        cut = qkv_full.shape[1] // 2
-        d_h_attn = (dot_nt(after(d_low, y_out), qkv_full[:, :cut]) + dot_nt(d_high, qkv_full[:, cut:])).astype(BF16)
+        sum_o = lax.dynamic_update_slice(sum_o, d_rel, (0, rows, 0)).reshape(-1, width)
+        grad_o_rel = spread(sum_o)
+        sum_qkv = wgrad(kind, h_attn, attn_theirs, after(d_qkv, sum_o), d_qkv_theirs, chips, scale)
+        grad_qkv = spread(sum_qkv)
+        y_out = (x1_f32 + dot_nn(after(act0, sum_qkv), down_full[0]) + dot_nn(act1, down_full[1])).astype(BF16)
+
+        d_h_attn = dot_nt(after(d_qkv, y_out), qkv_full).astype(BF16)
         d_x_norm, grad_norm_attn = jax.vjp(rms_norm, x_f32, gain_attn)[1](d_h_attn)
         grad_x = (d_x1.astype(F32) + d_x_norm).astype(BF16)
 
@@ -501,14 +515,16 @@
         d_rel_own = jnp.concatenate(
             [grad_o_rel[-lines:, at:at + span] for at in range(0, width, span)], axis=0).reshape(seq_len // BLK, BLK, span)
         d_rel_own = jnp.flip(d_rel_own, axis=1).reshape(1, seq_len, span).astype(BF16)
-        d_rel_all = lax.all_to_all(
-            jnp.broadcast_to(d_rel_own, (group_size, seq_len, span)), axis_name, split_axis=0, concat_axis=0, tiled=True)
+        d_rel_same = lax.all_to_all(
+            jnp.broadcast_to(d_rel_own, (chips, seq_len, span)), axis_name, split_axis=0, concat_axis=0, tiled=True,
+            axis_index_groups=same_core)
+        d_rel_other = swap(d_rel_same)
+        d_rel_all = jnp.stack(
+            [jnp.where(core == 0, d_rel_same, d_rel_other), jnp.where(core == 0, d_rel_other, d_rel_same)], axis=1)
         table_own = lax.dynamic_slice(pos_table, (0, me * (width // group_size)), (seq_len, width // group_size))
-        grad_rel = dot_tn(table_own, jnp.swapaxes(d_rel_all, 0, 1).reshape(seq_len, hidden)) * scale
-        grad_up = interleave([grad_up0, grad_up1], part, by_kind)
-        grad_query, grad_key, grad_value = to_heads(grad_low, grad_high, span, head_dim)
-        d_u = jnp.concatenate([d_u_low, d_u_high], axis=0)
-        d_w = jnp.concatenate([d_w_low, d_w_high], axis=0)
+        grad_rel = dot_tn(table_own, d_rel_all.transpose(2, 0, 1, 3).reshape(seq_len, hidden)) * scale
+        grad_up = interleave([grad_up, grad_up], part, group_size, [by_kind, lambda d: by_kind(d) + group_size])
+        grad_query, grad_key, grad_value = to_heads(grad_qkv, span, head_dim)
 
         small = jnp.stack([grad_norm_attn.reshape(group_size, span), jnp.sum(d_u, axis=1), jnp.sum(d_w, axis=1),
                            grad_norm_mlp.reshape(group_size, span)], axis=1)

time: 1880 us -> 2090 us (1.11)
  waiting for transfers between devices: 550 us -> 780 us
  matrix products: 825 us -> 609 us
  Pallas kernels: 305 us -> 488 us
    dot_general x11 -> x1, matrix products: 211 us -> 0.81 us  [dot_tn(): lax.dot_general(a, b, (((0,), (0,)), ((), ())), preferred_element_type=F32)]
    pallas_call x4 -> x8, Pallas kernels: 106 us -> 291 us  [the longest x6 276 us: wgrad(): pl.pallas_call(functools.partial(wgrad_kernel, count=len(share), scale=sc...]
    reduce_scatter x7 -> x5, waiting for transfers between devices: 380 us -> 564 us  [spread(): lax.psum_scatter(summed, axis_name, scatter_dimension=0, axis_index_group...]
    ppermute x9 -> x12, waiting for transfers between devices: 19.2 us -> 65 us  [swap(): return lax.ppermute(value, axis_name, pairs)]
    dot_general x7 -> x6, matrix products: 328 us -> 320 us  [dot_nt(): lax.dot_general(a, b, (((1,), (1,)), ((), ())), preferred_element_type=F32)]
    pallas_call x2 -> x1, Pallas kernels: 118 us -> 116 us  [attn_bwd(): pl.pallas_call(functools.partial(attn_bwd_kernel, heads=heads, head_dim=h...]
  transfers between devices with their start and end apart: 22 -> 23, of which waited for: 8 -> 10; matrix products, arithmetic and copies ran while one was open for 50% -> 29% of each run, Pallas kernels for 15% -> 19%
where the time goes in v4:
time: 2090 us
  waiting for transfers between devices  780 us (37%)
  matrix products  609 us (29%)
  Pallas kernels  488 us (23%)
  other arithmetic  79.7 us (4%)
  local copies, waits for them, and re-layouts  69.8 us (3%)
  blocking collectives  35.2 us (2%)
    reduce_scatter x5, waiting for transfers between devices, spread(): lax.psum_scatter(summed, axis_name, scatter_dimension=0, axis_index_group...  564 us
    dot_general x6, matrix products, dot_nt(): lax.dot_general(a, b, (((1,), (1,)), ((), ())), preferred_element_type=F32)  320 us
    dot_general x7, matrix products, dot_nn(): lax.dot_general(a, b, (((1,), (0,)), ((), ())), preferred_element_type=F32)  288 us
    pallas_call x6, Pallas kernels, wgrad(): pl.pallas_call(functools.partial(wgrad_kernel, count=len(share), scale=sc...  276 us
    pallas_call x1, Pallas kernels, attn_bwd(): pl.pallas_call(functools.partial(attn_bwd_kernel, heads=heads, head_dim=h...  116 us
    all_gather x1, waiting for transfers between devices, gather(): return lax.all_gather(local_shard, axis_name, axis=0, tiled=True)  112 us
    pallas_call x1, Pallas kernels, attn_fwd(): pl.pallas_call(functools.partial(attn_fwd_kernel, heads=heads, head_dim=h...  66.6 us
    ppermute x12, waiting for transfers between devices, swap(): return lax.ppermute(value, axis_name, pairs)  65 us
  transfers between devices with their start and end apart: 23, of which 10 were waited for; matrix products, arithmetic and copies ran while one was open for 29% of the time, Pallas kernels for 19%

profile of v4, /device:TPU:0, one launch (start us, length us, event | category | flops | bytes accessed | tf_op | source)
XLA Modules:
  0.0 2086.3 jit_solution(13251686910356074606)
XLA Ops:
  61.9 11.4 all-gather.2
  82.6 27.3 %all-gather.14.cloned.1.call-done = bf16[2560,2048]{1,0:T(8,128)(2,1)} async-done(((bf16[320,2048]{1,0:T(8,128)(2,1)}), bf16[2560,2048]{1,0:T(8,128)(2,1)}) %all-gather.14.cloned.1.call-update) | async-done | bytes 10485776 | tf_op jit(solution)/shard_map/all_gather | solution.py:441
  119.6 112.4 %all-gather.8.cloned.1.call-done = bf16[2048,6144]{1,0:T(8,128)(2,1)} async-done(((bf16[256,6144]{1,0:T(8,128)(2,1)}), bf16[2048,6144]{1,0:T(8,128)(2,1)}) %all-gather.8.cloned.1.call-update) | async-done | bytes 25165840 | tf_op jit(solution)/shard_map/all_gather | solution.py:386
  232.0 60.1 %convolution_convert_fusion = bf16[2048,6144]{1,0:T(8,128)(2,1)} fusion(bf16[2048,2048]{1,0:T(8,128)(2,1)} %fusion.39.refs_0_.refs_1_.refs_2_.refs_3_, bf16[2048,6144]{1,0:T(8,128)(2,1)} %all-gather.8.cloned.1.call-done), kind=kOutput, calls=%fused_computation.36 | convolution fusion | flops 51552190464 | bytes 58720256 | tf_op jit(solution)/shard_map/dot_general | solution.py:38
  292.1 66.6 %attn_fwd.1 = bf16[4,512,2048]{2,1,0:T(8,128)(2,1)} custom-call(bf16[4,512,6144]{2,1,0:T(8,128)(2,1)} %bitcast.174, bf16[8,320,2048]{2,1,0:T(8,128)(2,1)} %bitcast.140, f32[8,1,256]{2,1,0:T(1,128)} %get-tuple-element.91.u_ref, f32[8,1,256]{2,1,0:T(1,128)} %get-tuple-element.90.w_ref), custom_call_target="tpu_custom_call" | custom-call | flops 17179869184 | bytes 33554432 | tf_op jit(solution)/shard_map/attn_fwd/pallas_call | solution.py:217
  358.7 25.0 %fusion.28 = (f32[2048]{0:T(1024)S(1)}, bf16[2048,2048]{1,0:T(8,128)(2,1)}) fusion(bf16[2048,2048]{1,0:T(8,128)(2,1)} %bitcast.123, bf16[2048,2048]{1,0:T(8,128)(2,1)} %bitcast.131, bf16[4,512,2048]{2,1,0:T(8,128)(2,1)} %param.13), kind=kOutput, calls=%fused_computation.52 | convolution fusion | flops 17205032960 | bytes 33562624 | tf_op jit(solution)/shard_map/dot_general | solution.py:38
  394.1 53.8 %fusion.13 = (bf16[2048,4096]{1,0:T(8,128)(2,1)}, bf16[2048,4096]{1,0:T(8,128)(2,1)}) fusion(bf16[2048,2048]{1,0:T(8,128)(2,1)} %fusion.27.refs_0_.refs_1_.refs_2_.refs_3_, bf16[2,2048,4096]{2,1,0:T(8,128)(2,1)} %all-gather.10.cloned.1.call-done), kind=kOutput, calls=%fused_computation.25 | convolution fusion | flops 34452013056 | bytes 58720256 | tf_op jit(solution)/shard_map/dot_general | solution.py:38
  447.8 10.7 constant_dynamic-slice_fusion.9
  458.7 51.3 %fusion.19 = (bf16[2048,4096]{1,0:T(8,128)(2,1)}, bf16[2048,4096]{1,0:T(8,128)(2,1)}) fusion(bf16[2048,2048]{1,0:T(8,128)(2,1)} %fusion.27.refs_0_.refs_1_.refs_2_.refs_3_, bf16[2,2048,4096]{2,1,0:T(8,128)(2,1)} %all-gather.10.cloned.1.call-done), kind=kOutput, calls=%fused_computation.31 | convolution fusion | flops 34452013056 | bytes 58720256 | tf_op jit(solution)/shard_map/dot_general | solution.py:38
  510.0 48.3 %wgrad.6 = f32[2048,2048]{1,0:T(8,128)} custom-call(s32[1]{0:T(128)} %bitcast.12.kind_ref, bf16[2048,4096]{1,0:T(8,128)(2,1)} %get-tuple-element.59.refs_0_, bf16[2048,2048]{1,0:T(8,128)(2,1)} %collective-permute-done.1.refs_1_, bf16[2048,2048]{1,0:T(8,128)(2,1)} %bitcast.134, bf16[2048,2048]{1,0:T(8,128)(2,1)} %collective-permute-done.2.refs_3_), custom_call_target="tpu_custom_call" | custom-call | flops 34359738368 | bytes 50331648 | tf_op jit(solution)/shard_map/wgrad/pallas_call | solution.py:358
  567.1 64.9 %fusion.4.refs_5_ = bf16[2048,4096]{1,0:T(8,128)(2,1)} fusion(bf16[2048,4096]{1,0:T(8,128)(2,1)} %get-tuple-element.98, bf16[2048,2048]{1,0:T(8,128)(2,1)} %bitcast.135, bf16[2,4096,2048]{2,1,0:T(8,128)(2,1)} %all-gather.12.cloned.1.call-done), kind=kOutput, calls=%fused_computation.16 | convolution fusion | flops 34552676352 | bytes 58720256 | tf_op jit(solution)/shard_map/dot_general | solution.py:42
  632.2 48.0 %wgrad.7 = f32[2048,2048]{1,0:T(8,128)} custom-call(s32[1]{0:T(128)} %bitcast.12.kind_ref, bf16[2048,4096]{1,0:T(8,128)(2,1)} %get-tuple-element.49.refs_0_, bf16[2048,2048]{1,0:T(8,128)(2,1)} %collective-permute-done.4.refs_1_, bf16[2048,2048]{1,0:T(8,128)(2,1)} %bitcast.136, bf16[2048,2048]{1,0:T(8,128)(2,1)} %collective-permute-done.2.refs_3_), custom_call_target="tpu_custom_call" | custom-call | flops 34359738368 | bytes 50331648 | tf_op jit(solution)/shard_map/wgrad/pallas_call | solution.py:358
  680.2 64.7 %fusion.7.refs_5_ = bf16[2048,4096]{1,0:T(8,128)(2,1)} fusion(bf16[2048,4096]{1,0:T(8,128)(2,1)} %get-tuple-element.100, bf16[2048,2048]{1,0:T(8,128)(2,1)} %bitcast.137, bf16[2,4096,2048]{2,1,0:T(8,128)(2,1)} %all-gather.12.cloned.1.call-done), kind=kOutput, calls=%fused_computation.19 | convolution fusion | flops 34552676352 | bytes 58720256 | tf_op jit(solution)/shard_map/dot_general | solution.py:42
  754.5 21.9 %collective-permute-done.3.refs_4_ = bf16[2048,1024]{1,0:T(8,128)(2,1)} collective-permute-done((bf16[2048,1024]{1,0:T(8,128)(2,1)}, bf16[2048,1024]{1,0:T(8,128)(2,1)}, u32[]{:S(2)}, u32[]{:S(2)}) %collective-permute-start.3) | collective-permute-done | bytes 4194336 | tf_op jit(solution)/shard_map/ppermute | solution.py:408
  776.4 44.7 %wgrad.8.refs_7_ = f32[1024,8192]{1,0:T(8,128)} custom-call(s32[1]{0:T(128)} %bitcast.12.kind_ref, bf16[2048,2048]{1,0:T(8,128)(2,1)} %fusion.27.refs_0_.refs_1_.refs_2_.refs_3_, bf16[2048,2048]{1,0:T(8,128)(2,1)} %fusion.27.refs_0_.refs_1_.refs_2_.refs_3_, bf16[2048,2048]{1,0:T(8,128)(2,1)} %fusion.27.refs_0_.refs_1_.refs_2_.refs_3_, ...), custom_call_target="tpu_custom_call" | custom-call | flops 34359738368 | bytes 50331648 | tf_op jit(solution)/shard_map/wgrad/pallas_call | solution.py:358
  821.1 44.8 %wgrad.9 = f32[1024,8192]{1,0:T(8,128)} custom-call(s32[1]{0:T(128)} %bitcast.12.kind_ref, bf16[2048,2048]{1,0:T(8,128)(2,1)} %fusion.27.refs_0_.refs_1_.refs_2_.refs_3_, bf16[2048,2048]{1,0:T(8,128)(2,1)} %fusion.27.refs_0_.refs_1_.refs_2_.refs_3_, bf16[2048,2048]{1,0:T(8,128)(2,1)} %fusion.27.refs_0_.refs_1_.refs_2_.refs_3_, ...), custom_call_target="tpu_custom_call", output_to_operand_aliasing={{}: (8, {})} | custom-call | flops 34359738368 | bytes 50331648 | tf_op jit(solution)/shard_map/wgrad/pallas_call | solution.py:358
  865.9 43.2 %fusion.42 = f32[2048,2048]{1,0:T(8,128)} fusion(bf16[2048,4096]{1,0:T(8,128)(2,1)} %fusion.4.refs_5_, bf16[2,2048,4096]{2,1,0:T(8,128)(2,1)} %all-gather.10.cloned.1.call-done), kind=kOutput, calls=%fused_computation.77 | convolution fusion | flops 34359738368 | bytes 50331648 | tf_op jit(solution)/shard_map/dot_general | solution.py:42
  909.1 53.0 %fusion.32 = (f32[2048]{0:T(1024)}, f32[2048]{0:T(1024)S(1)}, bf16[2048,2048]{1,0:T(8,128)(2,1)}) fusion(bf16[2048,2048]{1,0:T(8,128)(2,1)} %get-tuple-element.96, f32[2048]{0:T(1024)S(1)} %copy-done.14, f32[2048]{0:T(1024)S(1)} %bitcast.158, f32[2048,2048]{1,0:T(8,128)} %fusion.42, bf16[2048,4096]{1,0:T(8,128)(2,1)} %fusion.7.refs_5_, ...), kind=kOutput, calls=%fused_computation.56 | convolution fusion | flops 34401681408 | bytes 67141632 | tf_op jit(solution)/shard_map/dot_general | solution.py:42
  962.2 12.1 fusion.35.refs_5_
  974.3 21.2 %convolution_convert_fusion.3 = bf16[2048,2048]{1,0:T(8,128)(2,1)} fusion(bf16[2048,2048]{1,0:T(8,128)(2,1)} %fusion.35.refs_5_, bf16[2048,2048]{1,0:T(8,128)(2,1)S(1)} %bitcast.132), kind=kOutput, calls=%fused_computation.82 | convolution fusion | flops 17184063488 | bytes 25165824 | tf_op jit(solution)/shard_map/dot_general | solution.py:42
  995.8 115.7 %attn_bwd.1 = (bf16[4,512,6144]{2,1,0:T(8,128)(2,1)}, f32[8,512,256]{2,1,0:T(8,128)}, f32[8,8,256]{2,1,0:T(8,128)}, f32[8,8,256]{2,1,0:T(8,128)}) custom-call(bf16[4,512,6144]{2,1,0:T(8,128)(2,1)} %bitcast.175, bf16[8,320,2048]{2,1,0:T(8,128)(2,1)} %bitcast.141, f32[8,1,256]{2,1,0:T(1,128)} %get-tuple-element.91.u_ref, ...), custom_call_target="tpu_custom_call" | custom-call | flops 42949672960 | bytes 58720256 | tf_op jit(solution)/shard_map/attn_bwd/pallas_call | solution.py:237
  1125.6 26.7 %wgrad.10 = f32[4,320,2048]{2,1,0:T(8,128)} custom-call(s32[1]{0:T(128)} %bitcast.12.kind_ref, bf16[2048,2048]{1,0:T(8,128)(2,1)} %bitcast.125, bf16[2048,2048]{1,0:T(8,128)(2,1)} %bitcast.126, bf16[2048,2048]{1,0:T(8,128)(2,1)} %bitcast.127, bf16[2048,2048]{1,0:T(8,128)(2,1)} %bitcast.128, bf16[2048,1024]{1,0:T(8,128)(2,1)} %collective-permute-done.7.refs_4_, ...), custom_call_target="tpu_custom_call" | custom-call | flops 17179869184 | bytes 25165824 | tf_op jit(solution)/shard_map/wgrad/pallas_call | solution.py:358
  1160.8 38.6 %collective-permute-done.refs_4_ = bf16[2048,1024]{1,0:T(8,128)(2,1)S(1)} collective-permute-done((bf16[2048,1024]{1,0:T(8,128)(2,1)S(1)}, bf16[2048,1024]{1,0:T(8,128)(2,1)S(1)}, u32[]{:S(2)}, u32[]{:S(2)}) %collective-permute-start) | collective-permute-done | bytes 4194336 | tf_op jit(solution)/shard_map/ppermute | solution.py:408
  1201.4 63.2 %wgrad.11 = f32[1024,6144]{1,0:T(8,128)} custom-call(s32[1]{0:T(128)} %bitcast.12.kind_ref, bf16[2048,2048]{1,0:T(8,128)(2,1)} %fusion.39.refs_0_.refs_1_.refs_2_.refs_3_, bf16[2048,2048]{1,0:T(8,128)(2,1)} %fusion.39.refs_0_.refs_1_.refs_2_.refs_3_, bf16[2048,2048]{1,0:T(8,128)(2,1)} %fusion.39.refs_0_.refs_1_.refs_2_.refs_3_, ...), custom_call_target="tpu_custom_call" | custom-call | flops 51539607552 | bytes 75497472 | tf_op jit(solution)/shard_map/wgrad/pallas_call | solution.py:358
  1264.7 50.0 %fusion.45 = f32[2048,2048]{1,0:T(8,128)} fusion(bf16[2,4096,2048]{2,1,0:T(8,128)(2,1)} %all-gather.12.cloned.1.call-done, bf16[2048,4096]{1,0:T(8,128)(2,1)} %get-tuple-element.100), kind=kOutput, calls=%fused_computation.80 | convolution fusion | flops 34443624448 | bytes 50331648 | tf_op jit(solution)/shard_map/dot_general | solution.py:38
  1315.9 45.8 %fusion.31 = bf16[2048,2048]{1,0:T(8,128)(2,1)} fusion(f32[2048,2048]{1,0:T(8,128)} %fusion.45, bf16[2048,2048]{1,0:T(8,128)(2,1)} %get-tuple-element.96, bf16[2048,4096]{1,0:T(8,128)(2,1)} %get-tuple-element.59.refs_0_, bf16[2,4096,2048]{2,1,0:T(8,128)(2,1)} %all-gather.12.cloned.1.call-done), kind=kOutput, calls=%fused_computation.55 | convolution fusion | flops 34376515584 | bytes 67108864 | tf_op jit(solution)/shard_map/dot_general | solution.py:38
  1361.8 73.1 %fusion.33 = (f32[2048]{0:T(1024)S(1)}, f32[2048]{0:T(1024)S(1)}, bf16[2048,2048]{1,0:T(8,128)(2,1)}) fusion(bf16[4,512,2048]{2,1,0:T(8,128)(2,1)} %param.13, f32[2048]{0:T(1024)S(1)} %copy-done.12, f32[2048]{0:T(1024)S(1)} %bitcast.155, bf16[2048,6144]{1,0:T(8,128)(2,1)} %bitcast.170, bf16[2048,6144]{1,0:T(8,128)(2,1)} %all-gather.8.cloned.1.call-done), kind=kOutput, calls=%fused_computation.57 | convolution fusion | flops 51577356288 | bytes 67141632 | tf_op jit(solution)/shard_map/dot_general | solution.py:42
  1446.8 118.7 %reduce-scatter.14.cloned.1.call-done = f32[512,2048]{1,0:T(8,128)} async-done(((f32[2048,2048]{1,0:T(8,128)}), f32[512,2048]{1,0:T(8,128)}) %reduce-scatter.14.cloned.1.call-update) | async-done | bytes 4194320 | tf_op jit(solution)/shard_map/reduce_scatter | solution.py:411
  1573.6 23.8 %all-reduce = f32[8,4,256]{2,1,0:T(4,128)S(1)} all-reduce(f32[8,4,256]{2,1,0:T(4,128)S(1)} %maximum_multiply_fusion), channel_id=4, replica_groups=mesh['fsdp'=8] {'fsdp'}, use_global_device_ids=true, to_apply=%region_8.0.clone | all-reduce | flops 8192 | bytes 65536
  1598.1 14.8 fusion.37
  1617.4 235.5 %reduce-scatter.10.cloned.1.call-done.refs_0_.refs_1_ = f32[256,8192]{1,0:T(8,128)} async-done(((f32[1024,8192]{1,0:T(8,128)}), f32[256,8192]{1,0:T(8,128)}) %reduce-scatter.10.cloned.1.call-update) | async-done | bytes 8388624 | tf_op jit(solution)/shard_map/reduce_scatter | solution.py:411
  1862.2 210.0 %reduce-scatter.6.cloned.1.call-done.in_ref = f32[256,6144]{1,0:T(8,128)} async-done(((f32[1024,6144]{1,0:T(8,128)}), f32[256,6144]{1,0:T(8,128)}) %reduce-scatter.6.cloned.1.call-update) | async-done | bytes 6291472 | tf_op jit(solution)/shard_map/reduce_scatter | solution.py:411
  (192 shorter events, 170.5 us)
Async XLA Ops:
  27.6 19.6 all-to-all-start
  31.9 78.1 %all-gather.14.cloned.1.call-start = ((), (), s32[]{:S(2)}) async-start(), calls=%async_computation.15 | async-start | bytes 11796480 | tf_op jit(solution)/shard_map/all_gather | solution.py:441
  53.0 179.0 %all-gather.8.cloned.1.call-start = ((), (), s32[]{:S(2)}) async-start(), calls=%async_computation.7 | async-start | bytes 28311552 | tf_op jit(solution)/shard_map/all_gather | solution.py:386
  53.8 340.3 %all-gather.10.cloned.1.call-start = ((), (), s32[]{:S(2)}) async-start(), calls=%async_computation.8 | async-start | bytes 37748736 | tf_op jit(solution)/shard_map/all_gather | solution.py:414
  54.5 512.6 %all-gather.12.cloned.1.call-start = ((), (), s32[]{:S(2)}) async-start(), calls=%async_computation.9 | async-start | bytes 37748736 | tf_op jit(solution)/shard_map/all_gather | solution.py:414
  55.1 1379.8 %reduce-scatter.8.cloned.1.call-start = ((), (), s32[]{:S(2)}) async-start(), calls=%async_computation.11 | async-start | bytes 13107200 | tf_op jit(solution)/shard_map/reduce_scatter | solution.py:411
  82.6 427.4 %collective-permute-start.2 = (bf16[2048,2048]{1,0:T(8,128)(2,1)}, bf16[2048,2048]{1,0:T(8,128)(2,1)}, u32[]{:S(2)}, u32[]{:S(2)}) collective-permute-start(bf16[2048,2048]{1,0:T(8,128)(2,1)} %bitcast.133), channel_id=1, source_target_pairs={{0,1},{1,0},{2,3},{3,2},{4,5},{5,4},{6,7},{7,6}} | collective-permute-start | bytes 25165832 | tf_op jit(solution)/shard_map/ppermute | solution.py:408
  458.5 51.6 %collective-permute-start.1 = (bf16[2048,2048]{1,0:T(8,128)(2,1)}, bf16[2048,2048]{1,0:T(8,128)(2,1)}, u32[]{:S(2)}, u32[]{:S(2)}) collective-permute-start(bf16[2048,2048]{1,0:T(8,128)(2,1)} %constant_dynamic-slice_fusion.9), channel_id=1, source_target_pairs={{0,1},{1,0},{2,3},{3,2},{4,5},{5,4},{6,7},{7,6}} | collective-permute-start | bytes 25165832 | tf_op jit(solution)/shard_map/ppermute | solution.py:408
  566.8 65.4 %collective-permute-start.4 = (bf16[2048,2048]{1,0:T(8,128)(2,1)}, bf16[2048,2048]{1,0:T(8,128)(2,1)}, u32[]{:S(2)}, u32[]{:S(2)}) collective-permute-start(bf16[2048,2048]{1,0:T(8,128)(2,1)} %constant_dynamic-slice_fusion.4), channel_id=1, source_target_pairs={{0,1},{1,0},{2,3},{3,2},{4,5},{5,4},{6,7},{7,6}} | collective-permute-start | bytes 25165832 | tf_op jit(solution)/shard_map/ppermute | solution.py:408
  631.9 144.5 %collective-permute-start.6 = (bf16[2048,4096]{1,0:T(8,128)(2,1)}, bf16[2048,4096]{1,0:T(8,128)(2,1)}, u32[]{:S(2)}, u32[]{:S(2)}) collective-permute-start(bf16[2048,4096]{1,0:T(8,128)(2,1)} %fusion.4.refs_5_), channel_id=1, source_target_pairs={{0,1},{1,0},{2,3},{3,2},{4,5},{5,4},{6,7},{7,6}} | collective-permute-start | bytes 50331656 | tf_op jit(solution)/shard_map/ppermute | solution.py:408
  744.9 76.2 %collective-permute-start.5 = (bf16[2048,4096]{1,0:T(8,128)(2,1)}, bf16[2048,4096]{1,0:T(8,128)(2,1)}, u32[]{:S(2)}, u32[]{:S(2)}) collective-permute-start(bf16[2048,4096]{1,0:T(8,128)(2,1)} %fusion.7.refs_5_), channel_id=1, source_target_pairs={{0,1},{1,0},{2,3},{3,2},{4,5},{5,4},{6,7},{7,6}} | collective-permute-start | bytes 50331656 | tf_op jit(solution)/shard_map/ppermute | solution.py:408
  750.0 26.4 %collective-permute-start.3 = (bf16[2048,1024]{1,0:T(8,128)(2,1)}, bf16[2048,1024]{1,0:T(8,128)(2,1)}, u32[]{:S(2)}, u32[]{:S(2)}) collective-permute-start(bf16[2048,1024]{1,0:T(8,128)(2,1)} %pad_maximum_fusion.2), channel_id=1, source_target_pairs={{0,1},{1,0},{2,3},{3,2},{4,5},{5,4},{6,7},{7,6}} | collective-permute-start | bytes 12582920 | tf_op jit(solution)/shard_map/ppermute | solution.py:408
  909.1 53.1 %copy-start.24 = (f32[2048]{0:T(1024)S(1)}, f32[2048]{0:T(1024)}, u32[]{:S(2)}) copy-start(f32[2048]{0:T(1024)} %copy-done.23) | copy-start | bytes 24580
  909.1 53.1 %copy-start = (bf16[2048,2048]{1,0:T(8,128)(2,1)S(1)}, bf16[2048,2048]{1,0:T(8,128)(2,1)}, u32[]{:S(2)}) copy-start(bf16[2048,2048]{1,0:T(8,128)(2,1)} %get-tuple-element.96) | copy-start | bytes 25165828
  995.5 130.1 %collective-permute-start.8 = (bf16[2048,2048]{1,0:T(8,128)(2,1)}, bf16[2048,2048]{1,0:T(8,128)(2,1)}, u32[]{:S(2)}, u32[]{:S(2)}) collective-permute-start(bf16[2048,2048]{1,0:T(8,128)(2,1)} %fusion.35.refs_5_), channel_id=1, source_target_pairs={{0,1},{1,0},{2,3},{3,2},{4,5},{5,4},{6,7},{7,6}} | collective-permute-start | bytes 25165832 | tf_op jit(solution)/shard_map/ppermute | solution.py:408
  995.8 119.0 %copy-start.6 = (bf16[2048,256]{1,0:T(8,128)(2,1)S(1)}, bf16[2048,256]{1,0:T(8,128)(2,1)}, u32[]{:S(2)}) copy-start(bf16[2048,256]{1,0:T(8,128)(2,1)} %get-tuple-element.71) | copy-start | bytes 3145732
  995.8 119.0 %copy-start.7 = (bf16[2048,256]{1,0:T(8,128)(2,1)S(1)}, bf16[2048,256]{1,0:T(8,128)(2,1)}, u32[]{:S(2)}) copy-start(bf16[2048,256]{1,0:T(8,128)(2,1)} %get-tuple-element.72) | copy-start | bytes 3145732
  995.8 119.0 %copy-start.8 = (bf16[2048,256]{1,0:T(8,128)(2,1)S(1)}, bf16[2048,256]{1,0:T(8,128)(2,1)}, u32[]{:S(2)}) copy-start(bf16[2048,256]{1,0:T(8,128)(2,1)} %get-tuple-element.73) | copy-start | bytes 3145732
  1114.5 4.5 collective-permute-start.9
  1118.1 7.5 collective-permute-start.7
  1153.9 292.9 %reduce-scatter.12.cloned.1.call-start = ((), (), s32[]{:S(2)}) async-start(), calls=%async_computation.13 | async-start | bytes 20971520 | tf_op jit(solution)/shard_map/reduce_scatter | solution.py:411
  1154.5 411.0 %reduce-scatter.14.cloned.1.call-start = ((), (), s32[]{:S(2)}) async-start(), calls=%async_computation.14 | async-start | bytes 20971520 | tf_op jit(solution)/shard_map/reduce_scatter | solution.py:411
  1155.2 697.7 %reduce-scatter.10.cloned.1.call-start = ((), (), s32[]{:S(2)}) async-start(), calls=%async_computation.12 | async-start | bytes 41943040 | tf_op jit(solution)/shard_map/reduce_scatter | solution.py:411
  1156.0 916.2 %reduce-scatter.6.cloned.1.call-start = ((), (), s32[]{:S(2)}) async-start(), calls=%async_computation.10 | async-start | bytes 31457280 | tf_op jit(solution)/shard_map/reduce_scatter | solution.py:411
  1156.0 43.4 %collective-permute-start.10 = (bf16[2048,6144]{1,0:T(8,128)(2,1)}, bf16[2048,6144]{1,0:T(8,128)(2,1)}, u32[]{:S(2)}, u32[]{:S(2)}) collective-permute-start(bf16[2048,6144]{1,0:T(8,128)(2,1)} %bitcast.168), channel_id=1, source_target_pairs={{0,1},{1,0},{2,3},{3,2},{4,5},{5,4},{6,7},{7,6}} | collective-permute-start | bytes 75497480 | tf_op jit(solution)/shard_map/ppermute | solution.py:408
  1160.7 38.7 %collective-permute-start = (bf16[2048,1024]{1,0:T(8,128)(2,1)S(1)}, bf16[2048,1024]{1,0:T(8,128)(2,1)S(1)}, u32[]{:S(2)}, u32[]{:S(2)}) collective-permute-start(bf16[2048,1024]{1,0:T(8,128)(2,1)S(1)} %pad_maximum_fusion.1), channel_id=1, source_target_pairs={{0,1},{1,0},{2,3},{3,2},{4,5},{5,4},{6,7},{7,6}} | collective-permute-start | bytes 12582920 | tf_op jit(solution)/shard_map/ppermute | solution.py:408
  1434.8 138.7 %copy-start.25 = (f32[8,1,256]{2,1,0:T(1,128)S(1)}, f32[8,1,256]{2,1,0:T(1,128)}, u32[]{:S(2)}) copy-start(f32[8,1,256]{2,1,0:T(1,128)} %stack.39) | copy-start | bytes 24580
  1434.8 138.7 %copy-start.26 = (f32[8,1,256]{2,1,0:T(1,128)S(1)}, f32[8,1,256]{2,1,0:T(1,128)}, u32[]{:S(2)}) copy-start(f32[8,1,256]{2,1,0:T(1,128)} %stack.38) | copy-start | bytes 24580
  1434.8 138.7 %copy-start.27 = (f32[2048]{0:T(1024)S(1)}, f32[2048]{0:T(1024)}, u32[]{:S(2)}) copy-start(f32[2048]{0:T(1024)} %get-tuple-element.69) | copy-start | bytes 24580
  1434.8 163.2 %copy-start.20 = (f32[1,4,4,128]{3,1,2,0:T(4,128)S(1)}, f32[1,4,4,128]{3,1,2,0:T(4,128)}, u32[]{:S(2)}) copy-start(f32[1,4,4,128]{3,1,2,0:T(4,128)} %copy-done.19) | copy-start | bytes 24580
  1443.2 154.8 %all-to-all-start.1 = ((bf16[4,512,256]{1,2,0:T(8,128)(2,1)}), bf16[4,512,256]{1,2,0:T(8,128)(2,1)S(1)}, u32[]{:S(2)}, u32[]{:S(2)}) async-start(bf16[4,512,256]{1,2,0:T(8,128)(2,1)} %broadcast_in_dim.11), calls=%async_computation.3 | async-start | bytes 2097152 | tf_op jit(solution)/shard_map/all_to_all | solution.py:518
  1598.0 16.5 collective-permute-start.11
  (24 other events, 567.6 us)
Sparse Core Ops, SparseCore 0:
  53.1 56.7 all-gather.13
  112.4 119.6 all-gather.7
  233.9 155.0 all-gather.9
  390.7 155.0 all-gather.11
  1154.0 97.9 reduce-scatter.7
  1254.8 148.1 reduce-scatter.11
  1406.1 159.3 reduce-scatter.13
  1568.5 284.3 reduce-scatter.9
  1856.0 216.1 reduce-scatter.5

commit v5 on v4

--- a/solution.py
+++ b/solution.py
@@ -13,7 +13,6 @@
 MASK_VALUE = -1e30
 BLK = 128
 SUB = 64
-SEQ = 512
 F32 = jnp.float32
 BF16 = jnp.bfloat16
 
@@ -32,6 +31,14 @@
 
 def gelu_tanh(pre_f32):
     return jax.nn.gelu(pre_f32, approximate=True)
+
+
+def gelu_slope(x):
+    c, k = (2.0 / jnp.pi) ** 0.5, 0.044715
+    square = x * x
+    scaled = c * x
+    t = jnp.tanh(scaled * (1.0 + k * square))
+    return 0.5 * ((1.0 + t) + (scaled * (1.0 - t * t)) * (1.0 + (3.0 * k) * square))
 
 
 def dot_nn(a, b):
@@ -104,15 +111,10 @@
         ref[rows, rest:rest + BLK] = jnp.zeros((SUB, BLK), ref.dtype)
 
 
-def unpack_rel(r_ref):
-    width = r_ref.shape[1] * r_ref.shape[2] // SEQ
-    return jnp.concatenate([r_ref[0, :, at:at + width] for at in range(0, r_ref.shape[2], width)], axis=0)
-
-
 def attn_fwd_kernel(qkv_ref, r_ref, u_ref, w_ref, c_ref, s_all, t_all, p_all, *, heads, head_dim):
     seq_len = qkv_ref.shape[1]
     q_ref, k_ref, v_ref = (qkv_ref.at[:, :, part * heads * head_dim:(part + 1) * heads * head_dim] for part in range(3))
-    rel_pair = unpack_rel(r_ref)
+    rel_pair = r_ref[0]
     all_cols = [slice(n * head_dim, (n + 1) * head_dim) for n in range(heads)]
     for n, cols in enumerate(all_cols):
         q_f32 = q_ref[0, :, cols].astype(F32)
@@ -133,7 +135,7 @@
     parts = [slice(part * heads * head_dim, (part + 1) * heads * head_dim) for part in range(3)]
     q_ref, k_ref, v_ref = (qkv_ref.at[:, :, part] for part in parts)
     dq_ref, dk_ref, dv_ref = (dqkv_ref.at[:, :, part] for part in parts)
-    rel_pair = unpack_rel(r_ref)
+    rel_pair = r_ref[0]
     blocks = seq_len // BLK
     flip = (lax.broadcasted_iota(jnp.int32, (BLK, BLK), 0) + lax.broadcasted_iota(jnp.int32, (BLK, BLK), 1)
             == BLK - 1).astype(F32).astype(BF16)
@@ -190,14 +192,12 @@
         dr_ref[0, near:, cols] += dot_tn(dt_all[n, low, :near], qw_all[n, low])
 
 
-def attn_args(qkv, rel, bias_u, head_dim, first):
+def attn_args(qkv, bias_u, head_dim, first):
     _, seq_len, width = qkv.shape
     groups, _, span = bias_u.shape
-    lines = seq_len * span // rel.shape[2]
-    at = rel.shape[1] // lines - 1
     specs = [
         pl.BlockSpec((1, seq_len, width // groups), lambda g, b: (b, 0, g + first)),
-        pl.BlockSpec((1, lines, rel.shape[2]), lambda g, b: (g + first, at, 0)),
+        pl.BlockSpec((1, seq_len, span), lambda g, b: (g + first, 0, 0)),
         pl.BlockSpec((1, 1, span), lambda g, b: (g + first, 0, 0)),
         pl.BlockSpec((1, 1, span), lambda g, b: (g + first, 0, 0)),
     ]
@@ -212,7 +212,7 @@
 def attn_fwd(qkv, rel, bias_u, bias_w, head_dim):
     batch, seq_len, width = qkv.shape
     groups = bias_u.shape[0]
-    specs, square, heads, span = attn_args(qkv, rel, bias_u, head_dim, 0)
+    specs, square, heads, span = attn_args(qkv, bias_u, head_dim, 0)
     work = batch * groups * heads * seq_len * seq_len * head_dim
     return pl.pallas_call(
         functools.partial(attn_fwd_kernel, heads=heads, head_dim=head_dim),
@@ -230,7 +230,7 @@
 
 def attn_bwd(qkv, rel, bias_u, bias_w, d_ctx, head_dim, first, count):
     batch, seq_len, _ = qkv.shape
-    specs, square, heads, span = attn_args(qkv, rel, bias_u, head_dim, first)
+    specs, square, heads, span = attn_args(qkv, bias_u, head_dim, first)
     work = batch * count * heads * seq_len * seq_len * head_dim
     small = jax.ShapeDtypeStruct((count, 8, span), F32)
     vec8 = pl.BlockSpec((1, 8, span), lambda g, b: (g, 0, 0))
@@ -317,15 +317,15 @@
 
 def wgrad_kernel(kind_ref, *refs, count, scale, blank):
     del kind_ref
-    a_refs, (a2_ref, b1_ref, b2_ref) = refs[:count], refs[count:count + 3]
-    out_ref, t1, t2 = refs[count + 3 + blank:]
+    a1_refs, a2_refs, (b1_ref, b2_ref) = refs[:count], refs[count:2 * count], refs[2 * count:2 * count + 2]
+    out_ref, t1, t2 = refs[2 * count + 2 + blank:]
 
     @pl.when(pl.program_id(1) == 0)
     def _():
-        part = a_refs[0].shape[1]
-        for c, ref in enumerate(a_refs):
-            t1[c * part:(c + 1) * part] = ref[...].T
-            t2[c * part:(c + 1) * part] = a2_ref[:, c * part:(c + 1) * part].T
+        part = a1_refs[0].shape[1]
+        for c in range(count):
+            t1[c * part:(c + 1) * part] = a1_refs[c][...].T
+            t2[c * part:(c + 1) * part] = a2_refs[c][...].T
 
     total = (dot_nn(t1[...], b1_ref[...]) + dot_nn(t2[...], b2_ref[...])) * scale
     out_ref[...] = total.reshape(out_ref.shape)
@@ -341,8 +341,8 @@
     else:
         share = [pl.BlockSpec((tokens, tile), lambda i, j, k: (0, tiles * k[0] + i))]
     block = pl.BlockSpec((tokens, width), lambda i, j, k: (0, j))
-    specs = share + [pl.BlockSpec((tokens, tile), lambda i, j, k: (0, i)), block, block]
-    args = [acts] * len(share) + [acts2, cots, cots2]
+    specs = share * 2 + [block, block]
+    args = [acts] * len(share) + [acts2] * len(share) + [cots, cots2]
     at, aliases = 0, {}
     if into is not None:
         specs.append(pl.BlockSpec(memory_space=pl.ANY))
@@ -395,17 +395,35 @@
         me = lax.axis_index(axis_name)
         core = lax.rem(me, 2)
 
-        def shares(acts, kind):
-            part = acts.shape[1] // group_size
-            return jnp.concatenate(
-                [lax.dynamic_slice(acts, (0, (2 * c + kind) * part), (tokens, part)) for c in range(chips)], axis=1)
-
-        def block_of(acts, kind):
-            half = acts.shape[1] // 2
-            return lax.dynamic_slice(acts, (0, kind * half), (tokens, half))
-
         def swap(value):
             return lax.ppermute(value, axis_name, pairs)
+
+        def ring_place(chip):
+            return chip ^ (chip >> 1)
+
+        ring = []
+        for d in range(group_size):
+            to = (ring_place(d // 2) + (1 if d % 2 == 0 else chips - 1)) % chips
+            ring.append((d, 2 * ring_place(to) + d % 2))
+        here, turn = ring_place(lax.div(me, 2)), 1 - 2 * core
+
+        def behind(steps):
+            return ring_place(lax.rem(here - turn * steps + 2 * chips, chips))
+
+        def pass_on(value):
+            return lax.ppermute(value, axis_name, ring)
+
+        def term(summed, steps):
+            return lax.dynamic_index_in_dim(summed, behind(steps), 0, keepdims=False)
+
+        def both_kinds(same, other):
+            first, second = jnp.where(core == 0, same, other), jnp.where(core == 0, other, same)
+            return jnp.stack([first, second], axis=1).reshape(group_size, *same.shape[1:])
+
+        def share_rel(own):
+            same = lax.all_to_all(jnp.broadcast_to(own[None], (chips, *own.shape)), axis_name, split_axis=0, concat_axis=0,
+                                  tiled=True, axis_index_groups=same_core)
+            return both_kinds(same, swap(same))
 
         def spread(summed):
             return lax.psum_scatter(summed, axis_name, scatter_dimension=0, axis_index_groups=same_core, tiled=True)
@@ -436,10 +454,15 @@
         rel_rows = after(w_rel, up_own).reshape(-1, hidden)
         rel_cols = lax.all_to_all(rel_rows, axis_name, split_axis=1, concat_axis=0, tiled=True)
         rel_own = dot_nn(pos_table, rel_cols).astype(BF16)
-        lines = seq_len * span // width
-        folded = jnp.concatenate([rel_own[at:at + lines] for at in range(0, seq_len, lines)], axis=1)
-        out_rel = lax.all_gather(jnp.concatenate([w_attn_out, folded], axis=0), axis_name, axis=0)
-        out_full = out_rel[:, :-lines].reshape(hidden, width)
+        rel_all = share_rel(rel_own)
+
+        got = w_attn_out
+        out_same = jnp.zeros((chips, *got.shape), BF16)
+        out_same = lax.dynamic_update_slice(out_same, got[None], (behind(0), 0, 0))
+        for step in range(chips - 1):
+            got = pass_on(got)
+            out_same = lax.dynamic_update_slice(out_same, got[None], (behind(step + 1), 0, 0))
+        out_full = both_kinds(out_same, swap(out_same)).reshape(hidden, width)
 
         up_full = gather_halves(up_own)
         down_full = gather_halves(after(w_down, up_own).reshape(2, part, width), [same_core[0] + same_core[1]])
@@ -447,7 +470,7 @@
         h_attn = rms_norm(x_f32, gain_attn)
         shape3 = (batch_local, seq_len, -1)
         qkv = dot_nn(h_attn, qkv_full).astype(BF16).reshape(shape3)
-        context = attn_fwd(qkv, out_rel, u_full, w_full, head_dim).reshape(tokens, hidden)
+        context = attn_fwd(qkv, rel_all, u_full, w_full, head_dim).reshape(tokens, hidden)
         x1_f32 = (x_f32 + dot_nn(context, out_full)).astype(BF16).astype(F32)
         h_mlp = rms_norm(x1_f32, gain_mlp)
 
@@ -457,21 +480,21 @@
 
         def unfeed(cots, weight, pre):
             d_act = dot_nt(cots, weight).astype(BF16)
-            return jax.vjp(gelu_tanh, pre.astype(F32))[1](d_act.astype(F32))[0].astype(BF16)
+            return (d_act.astype(F32) * gelu_slope(pre.astype(F32))).astype(BF16)
 
         kind = core[None]
         dy_theirs = swap(after(dy, h_attn))
-        attn_theirs = swap(shares(after(h_attn, qkv), 1 - core))
-        context_theirs = swap(shares(after(context, x1_f32), 1 - core))
+        attn_theirs = swap(h_attn)
+        context_theirs = swap(context)
 
         pre0, act0 = feed(h_mlp, up_full[0])
-        act0_theirs = swap(block_of(act0, 1 - core))
+        act0_theirs = swap(act0)
         pre1, act1 = feed(after(h_mlp, act0), up_full[1])
         sum_down0 = wgrad(kind, after(act0, act1), act0_theirs, dy, dy_theirs, chips, scale, False)
-        act1_theirs = swap(block_of(after(act1, sum_down0), 1 - core))
+        act1_theirs = swap(act1)
         d_pre0 = unfeed(after(dy, sum_down0), down_full[0], pre0)
         d_pre0_theirs = swap(d_pre0)
-        hidden_theirs = swap(shares(h_mlp, 1 - core))
+        hidden_theirs = swap(h_mlp)
         sum_down1 = wgrad(kind, after(act1, d_pre0), act1_theirs, dy, dy_theirs, chips, scale, False)
         d_pre1 = unfeed(after(dy, sum_down1), down_full[1], pre1)
         d_pre1_theirs = swap(d_pre1)
@@ -490,39 +513,33 @@
         d_x1_theirs = swap(d_x1)
         d_context = dot_nt(d_x1, out_full).astype(BF16).reshape(shape3)
         d_qkv, d_rel, d_u, d_w = attn_bwd(
-            qkv, out_rel, u_full, w_full, d_context, head_dim, 0, group_size)
+            qkv, rel_all, u_full, w_full, d_context, head_dim, 0, group_size)
         d_qkv = d_qkv.reshape(tokens, -1)
         d_qkv_theirs = swap(d_qkv)
         d_rel = d_rel.reshape(chips, 2, seq_len, span)
         got_rel = swap(lax.dynamic_index_in_dim(d_rel, 1 - core, 1, keepdims=False))
-        rows = hidden // group_size
-        sum_o = wgrad(kind, context, context_theirs, after(d_x1, d_qkv), d_x1_theirs, chips, scale,
-                      place=(rows + lines, None))
-        d_rel = lax.dynamic_index_in_dim(d_rel, core, 1, keepdims=False) + got_rel
-        d_rel = jnp.concatenate([d_rel[:, at:at + lines] for at in range(0, seq_len, lines)], axis=2)
-        sum_o = lax.dynamic_update_slice(sum_o, d_rel, (0, rows, 0)).reshape(-1, width)
-        grad_o_rel = spread(sum_o)
-        sum_qkv = wgrad(kind, h_attn, attn_theirs, after(d_qkv, sum_o), d_qkv_theirs, chips, scale)
+        sum_o = wgrad(kind, context, context_theirs, after(d_x1, d_qkv), d_x1_theirs, chips, scale)
+        sum_o = sum_o.reshape(chips, -1, width)
+        sum_rel = lax.dynamic_index_in_dim(d_rel, core, 1, keepdims=False) + got_rel
+        part_o, part_rel = term(sum_o, 1), term(sum_rel, 1)
+        got_o, got_rel = pass_on(part_o), pass_on(part_rel)
+        sum_qkv = wgrad(kind, h_attn, attn_theirs, after(d_qkv, part_o, part_rel), d_qkv_theirs, chips, scale)
         grad_qkv = spread(sum_qkv)
-        y_out = (x1_f32 + dot_nn(after(act0, sum_qkv), down_full[0]) + dot_nn(act1, down_full[1])).astype(BF16)
-
-        d_h_attn = dot_nt(after(d_qkv, y_out), qkv_full).astype(BF16)
+        part_o, part_rel = term(after(sum_o, sum_qkv), 2) + got_o, term(after(sum_rel, sum_qkv), 2) + got_rel
+        got_o, got_rel = pass_on(part_o), pass_on(part_rel)
+        y_out = (x1_f32 + dot_nn(after(act0, part_o, part_rel), down_full[0]) + dot_nn(act1, down_full[1])).astype(BF16)
+        part_o, part_rel = term(after(sum_o, y_out), 3) + got_o, term(after(sum_rel, y_out), 3) + got_rel
+        got_o, got_rel = pass_on(part_o), pass_on(part_rel)
+        d_h_attn = dot_nt(after(d_qkv, part_o, part_rel), qkv_full).astype(BF16)
         d_x_norm, grad_norm_attn = jax.vjp(rms_norm, x_f32, gain_attn)[1](d_h_attn)
+        grad_attn_out = term(after(sum_o, d_h_attn), 0) + got_o
+        d_rel_own = (term(after(sum_rel, d_h_attn), 0) + got_rel).reshape(seq_len // BLK, BLK, span)
+        d_rel_own = jnp.flip(d_rel_own, axis=1).reshape(seq_len, span).astype(BF16)
+        d_rel_all = share_rel(d_rel_own)
         grad_x = (d_x1.astype(F32) + d_x_norm).astype(BF16)
 
-        grad_o_rel = after(grad_o_rel, d_h_attn)
-        grad_attn_out = grad_o_rel[:-lines]
-        d_rel_own = jnp.concatenate(
-            [grad_o_rel[-lines:, at:at + span] for at in range(0, width, span)], axis=0).reshape(seq_len // BLK, BLK, span)
-        d_rel_own = jnp.flip(d_rel_own, axis=1).reshape(1, seq_len, span).astype(BF16)
-        d_rel_same = lax.all_to_all(
-            jnp.broadcast_to(d_rel_own, (chips, seq_len, span)), axis_name, split_axis=0, concat_axis=0, tiled=True,
-            axis_index_groups=same_core)
-        d_rel_other = swap(d_rel_same)
-        d_rel_all = jnp.stack(
-            [jnp.where(core == 0, d_rel_same, d_rel_other), jnp.where(core == 0, d_rel_other, d_rel_same)], axis=1)
         table_own = lax.dynamic_slice(pos_table, (0, me * (width // group_size)), (seq_len, width // group_size))
-        grad_rel = dot_tn(table_own, d_rel_all.transpose(2, 0, 1, 3).reshape(seq_len, hidden)) * scale
+        grad_rel = dot_tn(table_own, d_rel_all.transpose(1, 0, 2).reshape(seq_len, hidden)) * scale
         grad_up = interleave([grad_up, grad_up], part, group_size, [by_kind, lambda d: by_kind(d) + group_size])
         grad_query, grad_key, grad_value = to_heads(grad_qkv, span, head_dim)
 

time: 2090 us -> 1640 us (0.78)
  waiting for transfers between devices: 780 us -> 267 us
  blocking collectives: 35.2 us -> 88.8 us
  local copies, waits for them, and re-layouts: 69.8 us -> 38.2 us
  starting transfers between devices: 10.7 us -> 33.4 us
    reduce_scatter x5 -> x4, waiting for transfers between devices: 564 us -> 0.01 us  [spread(): lax.psum_scatter(summed, axis_name, scatter_dimension=0, axis_index_group...]
    ppermute x0 -> x9, waiting for transfers between devices: none -> 158 us  [pass_on(): return lax.ppermute(value, axis_name, ring)]
    all_gather x1, waiting for transfers between devices: 112 us -> 0.01 us  [gather(): return lax.all_gather(local_shard, axis_name, axis=0, tiled=True)]
    ppermute x12 -> x14, waiting for transfers between devices: 65 us -> 109 us  [swap(): return lax.ppermute(value, axis_name, pairs)]
    unnamed x1, blocking collectives: 23.8 us -> 66.2 us
    dynamic_slice x5 -> x0, local copies, waits for them, and re-layouts: 29.2 us -> none  [the longest x2 19 us: block_of(): return lax.dynamic_slice(acts, (0, kind * half), (tokens, half))]
    all_gather x1 -> x0, waiting for transfers between devices: 27.3 us -> none  [local_step(): lax.all_gather(jnp.concatenate([w_attn_out, folded], axis=0), axis_name,...]
  transfers between devices with their start and end apart: 23 -> 33, of which waited for: 10 -> 7; matrix products, arithmetic and copies ran while one was open for 29% -> 44% of each run, Pallas kernels for 19% -> 29%
where the time goes in v5:
time: 1640 us; the launch traced here: 1630 us
  matrix products  603 us (37%)
  Pallas kernels  491 us (30%)
  waiting for transfers between devices  267 us (16%)
  other arithmetic  91.5 us (6%)
  blocking collectives  88.8 us (5%)
  local copies, waits for them, and re-layouts  38.2 us (2%)
  starting transfers between devices  33.4 us (2%)
    dot_general x6, matrix products, dot_nt(): lax.dot_general(a, b, (((1,), (1,)), ((), ())), preferred_element_type=F32)  316 us
    dot_general x7, matrix products, dot_nn(): lax.dot_general(a, b, (((1,), (0,)), ((), ())), preferred_element_type=F32)  286 us
    pallas_call x6, Pallas kernels, wgrad(): pl.pallas_call(functools.partial(wgrad_kernel, count=len(share), scale=sc...  278 us
    ppermute x9, waiting for transfers between devices, pass_on(): return lax.ppermute(value, axis_name, ring)  158 us
    pallas_call x1, Pallas kernels, attn_bwd(): pl.pallas_call(functools.partial(attn_bwd_kernel, heads=heads, head_dim=h...  117 us
    ppermute x14, waiting for transfers between devices, swap(): return lax.ppermute(value, axis_name, pairs)  109 us
    pallas_call x1, Pallas kernels, attn_fwd(): pl.pallas_call(functools.partial(attn_fwd_kernel, heads=heads, head_dim=h...  66.3 us
    unnamed x1, blocking collectives  66.2 us
  transfers between devices with their start and end apart: 33, of which 7 were waited for; matrix products, arithmetic and copies ran while one was open for 44% of the time, Pallas kernels for 29%

profile of v5, /device:TPU:0, one launch (start us, length us, event | category | flops | bytes accessed | tf_op | source)
XLA Modules:
  0.0 1628.2 jit_solution(5538485336473423899)
XLA Ops:
  29.8 34.5 %collective-permute-done.1 = bf16[256,2048]{1,0:T(8,128)(2,1)S(1)} collective-permute-done((bf16[256,2048]{1,0:T(8,128)(2,1)S(1)}, bf16[256,2048]{1,0:T(8,128)(2,1)S(1)}, u32[]{:S(2)}, u32[]{:S(2)}) %collective-permute-start.1) | collective-permute-done | bytes 1048608 | tf_op jit(solution)/shard_map/ppermute | solution.py:414
  70.7 25.8 %collective-permute-done.2 = bf16[256,2048]{1,0:T(8,128)(2,1)} collective-permute-done((bf16[256,2048]{1,0:T(8,128)(2,1)S(1)}, bf16[256,2048]{1,0:T(8,128)(2,1)}, u32[]{:S(2)}, u32[]{:S(2)}) %collective-permute-start.2) | collective-permute-done | bytes 1048608 | tf_op jit(solution)/shard_map/ppermute | solution.py:414
  106.0 41.1 %collective-permute-done.3 = bf16[256,2048]{1,0:T(8,128)(2,1)} collective-permute-done((bf16[256,2048]{1,0:T(8,128)(2,1)}, bf16[256,2048]{1,0:T(8,128)(2,1)}, u32[]{:S(2)}, u32[]{:S(2)}) %collective-permute-start.3) | collective-permute-done | bytes 1048608 | tf_op jit(solution)/shard_map/ppermute | solution.py:414
  171.7 22.6 %all-gather.1 = bf16[8,4,256]{2,1,0:T(4,128)(2,1)S(1)} all-gather(bf16[1,4,256]{2,1,0:T(4,128)(2,1)S(1)} %maximum_bitcast_fusion), channel_id=2, replica_groups=mesh['fsdp'=8] {'fsdp'}, dimensions={0}, use_global_device_ids=true | all-gather | bytes 18432 | tf_op jit(solution)/shard_map/all_gather | solution.py:440
  195.0 9.9 fusion.53.refs_0_.refs_1_.refs_2_.refs_3_
  218.8 59.9 %convolution_convert_fusion = bf16[2048,6144]{1,0:T(8,128)(2,1)} fusion(bf16[2048,2048]{1,0:T(8,128)(2,1)} %fusion.53.refs_0_.refs_1_.refs_2_.refs_3_, bf16[2048,6144]{1,0:T(8,128)(2,1)} %all-gather.6.cloned.1.call-done), kind=kOutput, calls=%fused_computation.53 | convolution fusion | flops 51552190464 | bytes 58720256 | tf_op jit(solution)/shard_map/dot_general | solution.py:45
  278.7 66.3 %attn_fwd.1 = bf16[4,512,2048]{2,1,0:T(8,128)(2,1)} custom-call(bf16[4,512,6144]{2,1,0:T(8,128)(2,1)} %bitcast.208, bf16[8,512,256]{2,1,0:T(8,128)(2,1)} %bitcast.179, f32[8,1,256]{2,1,0:T(1,128)} %get-tuple-element.87.u_ref, f32[8,1,256]{2,1,0:T(1,128)} %get-tuple-element.86.w_ref), custom_call_target="tpu_custom_call" | custom-call | flops 17179869184 | bytes 33554432 | tf_op jit(solution)/shard_map/attn_fwd/pallas_call | solution.py:217
  345.0 25.5 %fusion.48 = (f32[2048]{0:T(1024)S(1)}, bf16[2048,2048]{1,0:T(8,128)(2,1)}) fusion(bf16[2048,2048]{1,0:T(8,128)(2,1)} %bitcast.154, bf16[2048,2048]{1,0:T(8,128)(2,1)} %bitcast.165, bf16[4,512,2048]{2,1,0:T(8,128)(2,1)} %param.13), kind=kOutput, calls=%fused_computation.70 | convolution fusion | flops 17205032960 | bytes 33562624 | tf_op jit(solution)/shard_map/dot_general | solution.py:45
  380.4 51.2 %fusion.29 = (bf16[2048,4096]{1,0:T(8,128)(2,1)}, bf16[2048,4096]{1,0:T(8,128)(2,1)}) fusion(bf16[2048,2048]{1,0:T(8,128)(2,1)} %fusion.40.refs_0_.refs_1_.refs_2_.refs_3_, bf16[2,2048,4096]{2,1,0:T(8,128)(2,1)} %all-gather.8.cloned.1.call-done), kind=kOutput, calls=%fused_computation.39 | convolution fusion | flops 34452013056 | bytes 58720256 | tf_op jit(solution)/shard_map/dot_general | solution.py:45
  432.3 51.3 %fusion.35 = (bf16[2048,4096]{1,0:T(8,128)(2,1)}, bf16[2048,4096]{1,0:T(8,128)(2,1)}) fusion(bf16[2048,2048]{1,0:T(8,128)(2,1)} %fusion.40.refs_0_.refs_1_.refs_2_.refs_3_, bf16[2,2048,4096]{2,1,0:T(8,128)(2,1)} %all-gather.8.cloned.1.call-done), kind=kOutput, calls=%fused_computation.45 | convolution fusion | flops 34452013056 | bytes 58720256 | tf_op jit(solution)/shard_map/dot_general | solution.py:45
  483.6 48.1 %wgrad.6 = f32[2048,2048]{1,0:T(8,128)} custom-call(s32[1]{0:T(128)} %bitcast.21.kind_ref, bf16[2048,4096]{1,0:T(8,128)(2,1)} %get-tuple-element.60.refs_0_, bf16[2048,4096]{1,0:T(8,128)(2,1)} %collective-permute-done.6.refs_1_, bf16[2048,2048]{1,0:T(8,128)(2,1)} %bitcast.169, bf16[2048,2048]{1,0:T(8,128)(2,1)} %collective-permute-done.7.refs_3_), custom_call_target="tpu_custom_call" | custom-call | flops 34359738368 | bytes 50331648 | tf_op jit(solution)/shard_map/wgrad/pallas_call | solution.py:358
  532.7 61.3 %fusion.19.refs_8_ = bf16[2048,4096]{1,0:T(8,128)(2,1)} fusion(bf16[2048,4096]{1,0:T(8,128)(2,1)} %get-tuple-element.94, bf16[2048,2048]{1,0:T(8,128)(2,1)} %bitcast.170, bf16[2,4096,2048]{2,1,0:T(8,128)(2,1)} %all-gather.10.cloned.1.call-done), kind=kOutput, calls=%fused_computation.29 | convolution fusion | flops 34519121920 | bytes 58720256 | tf_op jit(solution)/shard_map/dot_general | solution.py:49
  594.0 49.8 %wgrad.7 = f32[2048,2048]{1,0:T(8,128)} custom-call(s32[1]{0:T(128)} %bitcast.21.kind_ref, bf16[2048,4096]{1,0:T(8,128)(2,1)} %get-tuple-element.49.refs_0_, bf16[2048,4096]{1,0:T(8,128)(2,1)} %collective-permute-done.9.refs_1_, bf16[2048,2048]{1,0:T(8,128)(2,1)} %bitcast.171, bf16[2048,2048]{1,0:T(8,128)(2,1)} %collective-permute-done.7.refs_3_), custom_call_target="tpu_custom_call" | custom-call | flops 34359738368 | bytes 50331648 | tf_op jit(solution)/shard_map/wgrad/pallas_call | solution.py:358
  643.9 61.0 %fusion.13.refs_8_ = bf16[2048,4096]{1,0:T(8,128)(2,1)} fusion(bf16[2048,4096]{1,0:T(8,128)(2,1)} %get-tuple-element.96, bf16[2048,2048]{1,0:T(8,128)(2,1)} %bitcast.172, bf16[2,4096,2048]{2,1,0:T(8,128)(2,1)} %all-gather.10.cloned.1.call-done), kind=kOutput, calls=%fused_computation.23 | convolution fusion | flops 34519121920 | bytes 58720256 | tf_op jit(solution)/shard_map/dot_general | solution.py:49
  705.4 37.0 %collective-permute-done.8.refs_4_.refs_5_.refs_6_.refs_7_ = bf16[2048,2048]{1,0:T(8,128)(2,1)} collective-permute-done((bf16[2048,2048]{1,0:T(8,128)(2,1)}, bf16[2048,2048]{1,0:T(8,128)(2,1)}, u32[]{:S(2)}, u32[]{:S(2)}) %collective-permute-start.8) | collective-permute-done | bytes 8388640 | tf_op jit(solution)/shard_map/ppermute | solution.py:399
  742.4 45.3 %wgrad.8.refs_10_ = f32[1024,8192]{1,0:T(8,128)} custom-call(s32[1]{0:T(128)} %bitcast.21.kind_ref, bf16[2048,2048]{1,0:T(8,128)(2,1)} %fusion.40.refs_0_.refs_1_.refs_2_.refs_3_, bf16[2048,2048]{1,0:T(8,128)(2,1)} %fusion.40.refs_0_.refs_1_.refs_2_.refs_3_, bf16[2048,2048]{1,0:T(8,128)(2,1)} %fusion.40.refs_0_.refs_1_.refs_2_.refs_3_, ...), custom_call_target="tpu_custom_call" | custom-call | flops 34359738368 | bytes 50331648 | tf_op jit(solution)/shard_map/wgrad/pallas_call | solution.py:358
  787.6 45.2 %wgrad.9 = f32[1024,8192]{1,0:T(8,128)} custom-call(s32[1]{0:T(128)} %bitcast.21.kind_ref, bf16[2048,2048]{1,0:T(8,128)(2,1)} %fusion.40.refs_0_.refs_1_.refs_2_.refs_3_, bf16[2048,2048]{1,0:T(8,128)(2,1)} %fusion.40.refs_0_.refs_1_.refs_2_.refs_3_, bf16[2048,2048]{1,0:T(8,128)(2,1)} %fusion.40.refs_0_.refs_1_.refs_2_.refs_3_, ...), custom_call_target="tpu_custom_call", output_to_operand_aliasing={{}: (11, {})} | custom-call | flops 34359738368 | bytes 50331648 | tf_op jit(solution)/shard_map/wgrad/pallas_call | solution.py:358
  833.0 43.2 %fusion.56 = f32[2048,2048]{1,0:T(8,128)} fusion(bf16[2048,4096]{1,0:T(8,128)(2,1)} %fusion.19.refs_8_, bf16[2,2048,4096]{2,1,0:T(8,128)(2,1)} %all-gather.8.cloned.1.call-done), kind=kOutput, calls=%fused_computation.89 | convolution fusion | flops 34359738368 | bytes 50331648 | tf_op jit(solution)/shard_map/dot_general | solution.py:49
  876.2 53.8 %fusion.42 = (f32[2048]{0:T(1024)}, f32[2048]{0:T(1024)S(1)}, bf16[2048,2048]{1,0:T(8,128)(2,1)}) fusion(bf16[2048,2048]{1,0:T(8,128)(2,1)} %get-tuple-element.92, f32[2048]{0:T(1024)S(1)} %copy-done.12, f32[2048]{0:T(1024)S(1)} %bitcast.192, f32[2048,2048]{1,0:T(8,128)} %fusion.56, bf16[2048,4096]{1,0:T(8,128)(2,1)} %fusion.13.refs_8_, ...), kind=kOutput, calls=%fused_computation.64 | convolution fusion | flops 34401681408 | bytes 67141632 | tf_op jit(solution)/shard_map/dot_general | solution.py:49
  930.0 9.2 fusion.45.refs_8_
  939.3 23.9 %convolution_convert_fusion.3 = bf16[2048,2048]{1,0:T(8,128)(2,1)} fusion(bf16[2048,2048]{1,0:T(8,128)(2,1)S(1)} %fusion.45.refs_8_, bf16[2048,2048]{1,0:T(8,128)(2,1)} %bitcast.166), kind=kOutput, calls=%fused_computation.95 | convolution fusion | flops 17184063488 | bytes 25165824 | tf_op jit(solution)/shard_map/dot_general | solution.py:49
  963.2 117.1 %attn_bwd.1 = (bf16[4,512,6144]{2,1,0:T(8,128)(2,1)}, f32[8,512,256]{2,1,0:T(8,128)}, f32[8,8,256]{2,1,0:T(8,128)}, f32[8,8,256]{2,1,0:T(8,128)}) custom-call(bf16[4,512,6144]{2,1,0:T(8,128)(2,1)} %bitcast.209, bf16[8,512,256]{2,1,0:T(8,128)(2,1)} %bitcast.180, f32[8,1,256]{2,1,0:T(1,128)} %get-tuple-element.87.u_ref, f32[8,1,256]{2,1,0:T(1,128)} %get-tuple-element.86.w_ref, ...), custom_call_target="tpu_custom_call" | custom-call | flops 42949672960 | bytes 58720256 | tf_op jit(solution)/shard_map/attn_bwd/pallas_call | solution.py:237
  1084.6 72.1 %collective-permute-done.14 = f32[4,512,256]{2,1,0:T(8,128)S(1)} collective-permute-done((f32[4,512,256]{2,1,0:T(8,128)}, f32[4,512,256]{2,1,0:T(8,128)S(1)}, u32[]{:S(2)}, u32[]{:S(2)}) %collective-permute-start.14) | collective-permute-done | bytes 2097184 | tf_op jit(solution)/shard_map/ppermute | solution.py:399
  1159.9 26.8 %wgrad.10 = f32[1024,2048]{1,0:T(8,128)} custom-call(s32[1]{0:T(128)} %bitcast.21.kind_ref, bf16[2048,2048]{1,0:T(8,128)(2,1)} %bitcast.156, bf16[2048,2048]{1,0:T(8,128)(2,1)} %bitcast.157, bf16[2048,2048]{1,0:T(8,128)(2,1)} %bitcast.158, bf16[2048,2048]{1,0:T(8,128)(2,1)} %bitcast.159, ...), custom_call_target="tpu_custom_call" | custom-call | flops 17179869184 | bytes 25165824 | tf_op jit(solution)/shard_map/wgrad/pallas_call | solution.py:358
  1189.9 63.1 %wgrad.11 = f32[1024,6144]{1,0:T(8,128)} custom-call(s32[1]{0:T(128)} %bitcast.21.kind_ref, bf16[2048,2048]{1,0:T(8,128)(2,1)} %fusion.53.refs_0_.refs_1_.refs_2_.refs_3_, bf16[2048,2048]{1,0:T(8,128)(2,1)} %fusion.53.refs_0_.refs_1_.refs_2_.refs_3_, bf16[2048,2048]{1,0:T(8,128)(2,1)} %fusion.53.refs_0_.refs_1_.refs_2_.refs_3_, ...), custom_call_target="tpu_custom_call" | custom-call | flops 51539607552 | bytes 75497472 | tf_op jit(solution)/shard_map/wgrad/pallas_call | solution.py:358
  1256.5 50.7 %fusion.59 = f32[2048,2048]{1,0:T(8,128)} fusion(bf16[2,4096,2048]{2,1,0:T(8,128)(2,1)} %all-gather.10.cloned.1.call-done, bf16[2048,4096]{1,0:T(8,128)(2,1)} %get-tuple-element.96), kind=kOutput, calls=%fused_computation.92 | convolution fusion | flops 34443624448 | bytes 50331648 | tf_op jit(solution)/shard_map/dot_general | solution.py:45
  1308.7 26.4 %collective-permute-done.16 = f32[256,2048]{1,0:T(8,128)} collective-permute-done((f32[256,2048]{1,0:T(8,128)}, f32[256,2048]{1,0:T(8,128)}, u32[]{:S(2)}, u32[]{:S(2)}) %collective-permute-start.16) | collective-permute-done | bytes 2097184 | tf_op jit(solution)/shard_map/ppermute | solution.py:414
  1341.6 45.4 %fusion.51 = bf16[2048,2048]{1,0:T(8,128)(2,1)} fusion(f32[2048,2048]{1,0:T(8,128)} %fusion.59, bf16[2048,2048]{1,0:T(8,128)(2,1)} %get-tuple-element.92, bf16[2048,4096]{1,0:T(8,128)(2,1)} %get-tuple-element.60.refs_0_, bf16[2,4096,2048]{2,1,0:T(8,128)(2,1)} %all-gather.10.cloned.1.call-done), kind=kOutput, calls=%fused_computation.73 | convolution fusion | flops 34376515584 | bytes 67108864 | tf_op jit(solution)/shard_map/dot_general | solution.py:45
  1389.4 30.0 %collective-permute-done.18 = f32[256,2048]{1,0:T(8,128)} collective-permute-done((f32[256,2048]{1,0:T(8,128)}, f32[256,2048]{1,0:T(8,128)}, u32[]{:S(2)}, u32[]{:S(2)}) %collective-permute-start.18) | collective-permute-done | bytes 2097184 | tf_op jit(solution)/shard_map/ppermute | solution.py:414
  1423.7 73.2 %fusion.43 = (f32[2048]{0:T(1024)S(1)}, f32[2048]{0:T(1024)S(1)}, bf16[2048,2048]{1,0:T(8,128)(2,1)}) fusion(bf16[4,512,2048]{2,1,0:T(8,128)(2,1)} %param.13, f32[2048]{0:T(1024)S(1)} %copy-done.10, f32[2048]{0:T(1024)S(1)} %bitcast.189, bf16[2048,6144]{1,0:T(8,128)(2,1)} %bitcast.204, bf16[2048,6144]{1,0:T(8,128)(2,1)} %all-gather.6.cloned.1.call-done), kind=kOutput, calls=%fused_computation.65 | convolution fusion | flops 51577356288 | bytes 67141632 | tf_op jit(solution)/shard_map/dot_general | solution.py:49
  1513.7 66.2 %all-reduce = f32[8,4,256]{2,1,0:T(4,128)S(1)} all-reduce(f32[8,4,256]{2,1,0:T(4,128)S(1)} %maximum_multiply_fusion), channel_id=3, replica_groups=mesh['fsdp'=8] {'fsdp'}, use_global_device_ids=true, to_apply=%region_8.9.clone | all-reduce | flops 8192 | bytes 65536
  1580.6 13.3 fusion.47
  (187 shorter events, 162.9 us)
Async XLA Ops:
  7.2 211.6 %all-gather.6.cloned.1.call-start = ((), (), s32[]{:S(2)}) async-start(), calls=%async_computation.7 | async-start | bytes 28311552 | tf_op jit(solution)/shard_map/all_gather | solution.py:386
  19.4 360.9 %all-gather.8.cloned.1.call-start = ((), (), s32[]{:S(2)}) async-start(), calls=%async_computation.8 | async-start | bytes 37748736 | tf_op jit(solution)/shard_map/all_gather | solution.py:432
  26.2 506.5 %all-gather.10.cloned.1.call-start = ((), (), s32[]{:S(2)}) async-start(), calls=%async_computation.9 | async-start | bytes 37748736 | tf_op jit(solution)/shard_map/all_gather | solution.py:432
  26.3 38.1 %collective-permute-start.1 = (bf16[256,2048]{1,0:T(8,128)(2,1)S(1)}, bf16[256,2048]{1,0:T(8,128)(2,1)S(1)}, u32[]{:S(2)}, u32[]{:S(2)}) collective-permute-start(bf16[256,2048]{1,0:T(8,128)(2,1)S(1)} %copy-done.7), channel_id=1, source_target_pairs={{0,2},{1,5},{2,6},{3,1},{4,0},{5,7},{6,4},{7,3}} | collective-permute-start | bytes 3145736 | tf_op jit(solution)/shard_map/ppermute | solution.py:414
  64.3 32.1 %collective-permute-start.2 = (bf16[256,2048]{1,0:T(8,128)(2,1)S(1)}, bf16[256,2048]{1,0:T(8,128)(2,1)}, u32[]{:S(2)}, u32[]{:S(2)}) collective-permute-start(bf16[256,2048]{1,0:T(8,128)(2,1)S(1)} %collective-permute-done.1), channel_id=1, source_target_pairs={{0,2},{1,5},{2,6},{3,1},{4,0},{5,7},{6,4},{7,3}} | collective-permute-start | bytes 3145736 | tf_op jit(solution)/shard_map/ppermute | solution.py:414
  68.4 89.2 %all-to-all-start = ((bf16[256,8,256]{0,2,1:T(8,128)(2,1)}), bf16[256,8,256]{0,2,1:T(8,128)(2,1)S(1)}, u32[]{:S(2)}, u32[]{:S(2)}) async-start(bf16[256,8,256]{0,2,1:T(8,128)(2,1)} %bitcast.4), calls=%async_computation | async-start | bytes 2097152 | tf_op jit(solution)/shard_map/all_to_all | solution.py:455
  96.5 50.7 %collective-permute-start.3 = (bf16[256,2048]{1,0:T(8,128)(2,1)}, bf16[256,2048]{1,0:T(8,128)(2,1)}, u32[]{:S(2)}, u32[]{:S(2)}) collective-permute-start(bf16[256,2048]{1,0:T(8,128)(2,1)} %collective-permute-done.2), channel_id=1, source_target_pairs={{0,2},{1,5},{2,6},{3,1},{4,0},{5,7},{6,4},{7,3}} | collective-permute-start | bytes 3145736 | tf_op jit(solution)/shard_map/ppermute | solution.py:414
  149.4 57.4 %collective-permute-start.4 = (bf16[4,256,2048]{2,1,0:T(8,128)(2,1)}, bf16[4,256,2048]{2,1,0:T(8,128)(2,1)}, u32[]{:S(2)}, u32[]{:S(2)}) collective-permute-start(bf16[4,256,2048]{2,1,0:T(8,128)(2,1)} %bitcast_dynamic-update-slice_fusion), channel_id=1, source_target_pairs={{0,1},{1,0},{2,3},{3,2},{4,5},{5,4},{6,7},{7,6}} | collective-permute-start | bytes 12582920 | tf_op jit(solution)/shard_map/ppermute | solution.py:399
  162.1 32.8 %all-to-all-start.1 = ((bf16[4,512,256]{2,1,0:T(8,128)(2,1)}), bf16[4,512,256]{2,1,0:T(8,128)(2,1)S(1)}, u32[]{:S(2)}, u32[]{:S(2)}) async-start(bf16[4,512,256]{2,1,0:T(8,128)(2,1)} %broadcast_in_dim.20), calls=%async_computation.1 | async-start | bytes 2097152 | tf_op jit(solution)/shard_map/all_to_all | solution.py:424
  165.9 1337.3 %reduce-scatter.9.cloned.1.call-start = ((), (), s32[]{:S(2)}) async-start(), calls=%async_computation.12 | async-start | bytes 20971520 | tf_op jit(solution)/shard_map/reduce_scatter | solution.py:429
  431.6 52.0 %collective-permute-start.6 = (bf16[2048,4096]{1,0:T(8,128)(2,1)}, bf16[2048,4096]{1,0:T(8,128)(2,1)}, u32[]{:S(2)}, u32[]{:S(2)}) collective-permute-start(bf16[2048,4096]{1,0:T(8,128)(2,1)} %get-tuple-element.60.refs_0_), channel_id=1, source_target_pairs={{0,1},{1,0},{2,3},{3,2},{4,5},{5,4},{6,7},{7,6}} | collective-permute-start | bytes 50331656 | tf_op jit(solution)/shard_map/ppermute | solution.py:399
  432.3 51.3 %collective-permute-start.7 = (bf16[2048,2048]{1,0:T(8,128)(2,1)}, bf16[2048,2048]{1,0:T(8,128)(2,1)}, u32[]{:S(2)}, u32[]{:S(2)}) collective-permute-start(bf16[2048,2048]{1,0:T(8,128)(2,1)} %bitcast.168), channel_id=1, source_target_pairs={{0,1},{1,0},{2,3},{3,2},{4,5},{5,4},{6,7},{7,6}} | collective-permute-start | bytes 25165832 | tf_op jit(solution)/shard_map/ppermute | solution.py:399
  531.8 971.5 %reduce-scatter.11.cloned.1.call-start = ((), (), s32[]{:S(2)}) async-start(), calls=%async_computation.13 | async-start | bytes 20971520 | tf_op jit(solution)/shard_map/reduce_scatter | solution.py:429
  531.8 62.2 %collective-permute-start.9 = (bf16[2048,4096]{1,0:T(8,128)(2,1)}, bf16[2048,4096]{1,0:T(8,128)(2,1)}, u32[]{:S(2)}, u32[]{:S(2)}) collective-permute-start(bf16[2048,4096]{1,0:T(8,128)(2,1)} %get-tuple-element.49.refs_0_), channel_id=1, source_target_pairs={{0,1},{1,0},{2,3},{3,2},{4,5},{5,4},{6,7},{7,6}} | collective-permute-start | bytes 50331656 | tf_op jit(solution)/shard_map/ppermute | solution.py:399
  643.8 961.0 %reduce-scatter.7.cloned.1.call-start = ((), (), s32[]{:S(2)}) async-start(), calls=%async_computation.11 | async-start | bytes 41943040 | tf_op jit(solution)/shard_map/reduce_scatter | solution.py:429
  643.9 98.5 %collective-permute-start.11 = (bf16[2048,4096]{1,0:T(8,128)(2,1)}, bf16[2048,4096]{1,0:T(8,128)(2,1)}, u32[]{:S(2)}, u32[]{:S(2)}) collective-permute-start(bf16[2048,4096]{1,0:T(8,128)(2,1)} %fusion.19.refs_8_), channel_id=1, source_target_pairs={{0,1},{1,0},{2,3},{3,2},{4,5},{5,4},{6,7},{7,6}} | collective-permute-start | bytes 50331656 | tf_op jit(solution)/shard_map/ppermute | solution.py:399
  704.9 82.8 %collective-permute-start.10 = (bf16[2048,4096]{1,0:T(8,128)(2,1)}, bf16[2048,4096]{1,0:T(8,128)(2,1)}, u32[]{:S(2)}, u32[]{:S(2)}) collective-permute-start(bf16[2048,4096]{1,0:T(8,128)(2,1)} %fusion.13.refs_8_), channel_id=1, source_target_pairs={{0,1},{1,0},{2,3},{3,2},{4,5},{5,4},{6,7},{7,6}} | collective-permute-start | bytes 50331656 | tf_op jit(solution)/shard_map/ppermute | solution.py:399
  705.3 37.1 %collective-permute-start.8 = (bf16[2048,2048]{1,0:T(8,128)(2,1)}, bf16[2048,2048]{1,0:T(8,128)(2,1)}, u32[]{:S(2)}, u32[]{:S(2)}) collective-permute-start(bf16[2048,2048]{1,0:T(8,128)(2,1)} %fusion.40.refs_0_.refs_1_.refs_2_.refs_3_), channel_id=1, source_target_pairs={{0,1},{1,0},{2,3},{3,2},{4,5},{5,4},{6,7},{7,6}} | collective-permute-start | bytes 25165832 | tf_op jit(solution)/shard_map/ppermute | solution.py:399
  832.9 780.7 %reduce-scatter.5.cloned.1.call-start = ((), (), s32[]{:S(2)}) async-start(), calls=%async_computation.10 | async-start | bytes 31457280 | tf_op jit(solution)/shard_map/reduce_scatter | solution.py:429
  1080.3 109.6 %collective-permute-start.15 = (bf16[2048,6144]{1,0:T(8,128)(2,1)}, bf16[2048,6144]{1,0:T(8,128)(2,1)}, u32[]{:S(2)}, u32[]{:S(2)}) collective-permute-start(bf16[2048,6144]{1,0:T(8,128)(2,1)} %bitcast.202), channel_id=1, source_target_pairs={{0,1},{1,0},{2,3},{3,2},{4,5},{5,4},{6,7},{7,6}} | collective-permute-start | bytes 75497480 | tf_op jit(solution)/shard_map/ppermute | solution.py:399
  1080.4 79.6 %collective-permute-start.5 = (bf16[2048,2048]{1,0:T(8,128)(2,1)}, bf16[2048,2048]{1,0:T(8,128)(2,1)}, u32[]{:S(2)}, u32[]{:S(2)}) collective-permute-start(bf16[2048,2048]{1,0:T(8,128)(2,1)} %bitcast.155), channel_id=1, source_target_pairs={{0,1},{1,0},{2,3},{3,2},{4,5},{5,4},{6,7},{7,6}} | collective-permute-start | bytes 25165832 | tf_op jit(solution)/shard_map/ppermute | solution.py:399
  1080.8 79.1 %collective-permute-start.12 = (bf16[2048,2048]{1,0:T(8,128)(2,1)}, bf16[2048,2048]{1,0:T(8,128)(2,1)}, u32[]{:S(2)}, u32[]{:S(2)}) collective-permute-start(bf16[2048,2048]{1,0:T(8,128)(2,1)} %copy-done), channel_id=1, source_target_pairs={{0,1},{1,0},{2,3},{3,2},{4,5},{5,4},{6,7},{7,6}} | collective-permute-start | bytes 25165832 | tf_op jit(solution)/shard_map/ppermute | solution.py:399
  1080.9 109.0 %collective-permute-start.13 = (bf16[2048,2048]{1,0:T(8,128)(2,1)}, bf16[2048,2048]{1,0:T(8,128)(2,1)}, u32[]{:S(2)}, u32[]{:S(2)}) collective-permute-start(bf16[2048,2048]{1,0:T(8,128)(2,1)} %fusion.53.refs_0_.refs_1_.refs_2_.refs_3_), channel_id=1, source_target_pairs={{0,1},{1,0},{2,3},{3,2},{4,5},{5,4},{6,7},{7,6}} | collective-permute-start | bytes 25165832 | tf_op jit(solution)/shard_map/ppermute | solution.py:399
  1084.6 72.1 %collective-permute-start.14 = (f32[4,512,256]{2,1,0:T(8,128)}, f32[4,512,256]{2,1,0:T(8,128)S(1)}, u32[]{:S(2)}, u32[]{:S(2)}) collective-permute-start(f32[4,512,256]{2,1,0:T(8,128)} %dynamic-slice_bitcast_fusion), channel_id=1, source_target_pairs={{0,1},{1,0},{2,3},{3,2},{4,5},{5,4},{6,7},{7,6}} | collective-permute-start | bytes 6291464 | tf_op jit(solution)/shard_map/ppermute | solution.py:399
  1253.1 55.4 %collective-permute-start.17 = (f32[512,256]{1,0:T(8,128)S(1)}, f32[512,256]{1,0:T(8,128)S(1)}, u32[]{:S(2)}, u32[]{:S(2)}) collective-permute-start(f32[512,256]{1,0:T(8,128)S(1)} %dynamic-slice_bitcast_fusion.2), channel_id=1, source_target_pairs={{0,2},{1,5},{2,6},{3,1},{4,0},{5,7},{6,4},{7,3}} | collective-permute-start | bytes 1572872 | tf_op jit(solution)/shard_map/ppermute | solution.py:414
  1254.6 80.5 %collective-permute-start.16 = (f32[256,2048]{1,0:T(8,128)}, f32[256,2048]{1,0:T(8,128)}, u32[]{:S(2)}, u32[]{:S(2)}) collective-permute-start(f32[256,2048]{1,0:T(8,128)} %dynamic-slice_bitcast_fusion.1), channel_id=1, source_target_pairs={{0,2},{1,5},{2,6},{3,1},{4,0},{5,7},{6,4},{7,3}} | collective-permute-start | bytes 6291464 | tf_op jit(solution)/shard_map/ppermute | solution.py:414
  1308.6 78.4 %collective-permute-start.19 = (f32[512,256]{1,0:T(8,128)S(1)}, f32[512,256]{1,0:T(8,128)S(1)}, u32[]{:S(2)}, u32[]{:S(2)}) collective-permute-start(f32[512,256]{1,0:T(8,128)S(1)} %bitcast_add_fusion.7), channel_id=1, source_target_pairs={{0,2},{1,5},{2,6},{3,1},{4,0},{5,7},{6,4},{7,3}} | collective-permute-start | bytes 1572872 | tf_op jit(solution)/shard_map/ppermute | solution.py:414
  1339.0 80.4 %collective-permute-start.18 = (f32[256,2048]{1,0:T(8,128)}, f32[256,2048]{1,0:T(8,128)}, u32[]{:S(2)}, u32[]{:S(2)}) collective-permute-start(f32[256,2048]{1,0:T(8,128)} %bitcast_add_fusion.3), channel_id=1, source_target_pairs={{0,2},{1,5},{2,6},{3,1},{4,0},{5,7},{6,4},{7,3}} | collective-permute-start | bytes 6291464 | tf_op jit(solution)/shard_map/ppermute | solution.py:414
  1387.1 109.8 %collective-permute-start.20 = (f32[512,256]{1,0:T(8,128)S(1)}, f32[512,256]{1,0:T(8,128)S(1)}, u32[]{:S(2)}, u32[]{:S(2)}) collective-permute-start(f32[512,256]{1,0:T(8,128)S(1)} %bitcast_add_fusion.6), channel_id=1, source_target_pairs={{0,2},{1,5},{2,6},{3,1},{4,0},{5,7},{6,4},{7,3}} | collective-permute-start | bytes 1572872 | tf_op jit(solution)/shard_map/ppermute | solution.py:414
  1498.4 82.1 %all-to-all-start.2 = ((bf16[4,512,256]{2,1,0:T(8,128)(2,1)}), bf16[4,512,256]{2,1,0:T(8,128)(2,1)S(1)}, u32[]{:S(2)}, u32[]{:S(2)}) async-start(bf16[4,512,256]{2,1,0:T(8,128)(2,1)} %broadcast_in_dim.55), calls=%async_computation.3 | async-start | bytes 2097152 | tf_op jit(solution)/shard_map/all_to_all | solution.py:424
  1511.6 89.3 %collective-permute-start.22 = (f32[256,2048]{1,0:T(8,128)}, f32[256,2048]{1,0:T(8,128)}, u32[]{:S(2)}, u32[]{:S(2)}) collective-permute-start(f32[256,2048]{1,0:T(8,128)} %bitcast_add_fusion.2), channel_id=1, source_target_pairs={{0,2},{1,5},{2,6},{3,1},{4,0},{5,7},{6,4},{7,3}} | collective-permute-start | bytes 6291464 | tf_op jit(solution)/shard_map/ppermute | solution.py:414
  1580.5 13.4 collective-permute-start.21
  (31 other events, 1252.0 us)
Sparse Core Ops, SparseCore 0:
  19.6 172.1 all-gather.5
  193.6 156.5 all-gather.7
  352.0 155.0 all-gather.9
  531.9 149.8 reduce-scatter.8
  684.6 148.1 reduce-scatter.10
  835.7 282.9 reduce-scatter.6
  1253.2 297.2 reduce-scatter.4
